TPU v7x, 32 devices: a whole 2x2x4 slice. The times are simulated.
32 devices in a mesh: dp: 16 (over z, y, core), tensor: 2 (over x).
Axes of the slice: x: 2, y: 2, z: 4, core: 2. Of those that a mesh axis runs over, the one named last changes fastest.
Arguments:
- inputs: bfloat16 [32768, 512], P(('dp', 'tensor')), may hold values from -6 to 6
- norm_scale: float32 [2, 512], replicated, may hold values from 0.1 to 1.9
- norm_shift: float32 [2, 512], replicated, may hold values from -3 to 3
- head_weight: bfloat16 [3, 512, 512], P(None, None, 'tensor'), may hold values from -0.25 to 0.25
- query_bias: float32 [512], P('tensor'), may hold values from -3 to 3
- value_bias: float32 [512], P('tensor'), may hold values from -0.3 to 0.3
- out_weight: bfloat16 [512, 512], P('tensor'), may hold values from -4 to 4
- out_bias: float32 [512], replicated, may hold values from -2 to 2
- up_weight: bfloat16 [512, 2048], P(None, 'tensor'), may hold values from -0.25 to 0.25
- up_bias: float32 [2048], P('tensor'), may hold values from -3 to 3
- down_weight: bfloat16 [2048, 512], P('tensor'), may hold values from -0.125 to 0.125
- down_bias: float32 [512], replicated, may hold values from -2 to 2
- cotangent: bfloat16 [32768, 512], P(('dp', 'tensor')), may hold values from -6 to 6
Outputs:
- layer_out: bfloat16 [32768, 512], P(('dp', 'tensor'))
- input_grad: bfloat16 [32768, 512], P(('dp', 'tensor'))
- norm_scale_grad: float32 [2, 512], replicated
- norm_shift_grad: float32 [2, 512], replicated
- head_weight_grad: float32 [3, 512, 512], P(None, None, 'tensor')
- query_bias_grad: float32 [512], P('tensor')
- value_bias_grad: float32 [512], P('tensor')
- out_weight_grad: float32 [512, 512], P('tensor')
- out_bias_grad: float32 [512], replicated
- up_weight_grad: float32 [512, 2048], P(None, 'tensor')
- up_bias_grad: float32 [2048], P('tensor')
- down_weight_grad: float32 [2048, 512], P('tensor')
- down_bias_grad: float32 [512], replicated
All inputs are finite; a program needn't handle non-finite values.
Results may differ from a plain program's by a relative error of at most 0.012.
Values may be sent and summed in bfloat16 or wider, within the bound.
A program may use at most 192 MiB of HBM per device.

v0:
```python
from functools import partial

import jax
import jax.numpy as jnp
from jax import lax
from jax.sharding import PartitionSpec as P

HD = 64
LEN = 1024
BLK = 256


EPSILON = 1e-05


def layer_norm(values, gain, shift):
    center = jnp.mean(values, -1, keepdims=True)
    centered = values - center
    spread = jnp.mean(centered * centered, -1, keepdims=True)
    return centered * lax.rsqrt(spread + EPSILON) * gain + shift


def allowed_mask():
    place = lax.iota(jnp.int32, LEN) // BLK
    return place[None, :] <= place[:, None]


def attend_forward(pieces):
    queries, key_rows, values = pieces
    scores = jnp.einsum(
        "qhd,khd->hqk", queries, key_rows, preferred_element_type=jnp.float32
    ) * HD ** (-0.5)
    masked = jnp.where(allowed_mask()[None], scores, -1e30)
    largest = jnp.max(masked, -1, keepdims=True)
    powers = jnp.exp(masked - largest)
    row_total = jnp.sum(powers, -1, keepdims=True)
    attn_probs = (powers / row_total).astype(jnp.bfloat16)
    mixed_out = jnp.einsum(
        "hqk,khd->qhd", attn_probs, values, preferred_element_type=jnp.float32
    ).astype(jnp.bfloat16)
    return (mixed_out, largest[..., 0] + jnp.log(row_total[..., 0]))


def attend_backward(pieces):
    queries, key_rows, values, logsum, grad_mixed = pieces
    scale = HD ** (-0.5)
    scores = (
        jnp.einsum("qhd,khd->hqk", queries, key_rows, preferred_element_type=jnp.float32) * scale
    )
    masked = jnp.where(allowed_mask()[None], scores, -1e30)
    attn_probs = jnp.exp(masked - logsum[..., None])
    low_probs = attn_probs.astype(jnp.bfloat16)
    grad_probs = jnp.einsum("qhd,khd->hqk", grad_mixed, values, preferred_element_type=jnp.float32)
    grad_values = jnp.einsum(
        "hqk,qhd->khd", low_probs, grad_mixed, preferred_element_type=jnp.float32
    )
    inner = jnp.sum(attn_probs * grad_probs, -1, keepdims=True)
    grad_scores = (attn_probs * (grad_probs - inner)).astype(jnp.bfloat16)
    grad_queries = (
        jnp.einsum("hqk,khd->qhd", grad_scores, key_rows, preferred_element_type=jnp.float32)
        * scale
    )
    grad_keys = (
        jnp.einsum("hqk,qhd->khd", grad_scores, queries, preferred_element_type=jnp.float32) * scale
    )
    return (
        grad_queries.astype(jnp.bfloat16),
        grad_keys.astype(jnp.bfloat16),
        grad_values.astype(jnp.bfloat16),
    )


def to_heads(table):
    row_count = table.shape[0]
    return table.reshape(row_count // LEN, LEN, table.shape[1] // HD, HD)


def from_heads(table):
    return table.reshape(table.shape[0] * table.shape[1], table.shape[2] * table.shape[3])


def attention_part(normed_full, head_weight, query_bias, value_bias):
    queries = (
        jnp.dot(normed_full, head_weight[0], preferred_element_type=jnp.float32) + query_bias
    ).astype(jnp.bfloat16)
    key_rows = jnp.dot(normed_full, head_weight[1], preferred_element_type=jnp.float32).astype(
        jnp.bfloat16
    )
    values = (
        jnp.dot(normed_full, head_weight[2], preferred_element_type=jnp.float32) + value_bias
    ).astype(jnp.bfloat16)
    mixed_out, logsum = lax.map(
        attend_forward, (to_heads(queries), to_heads(key_rows), to_heads(values))
    )
    return (queries, key_rows, values, from_heads(mixed_out), logsum)


def feed_part(second_full, up_weight, up_bias):
    pre_act = jnp.dot(second_full, up_weight, preferred_element_type=jnp.float32) + up_bias
    activated = jax.nn.gelu(pre_act, approximate=True).astype(jnp.bfloat16)
    return (pre_act, activated)


def local(
    inputs,
    norm_scale,
    norm_shift,
    head_weight,
    query_bias,
    value_bias,
    out_weight,
    out_bias,
    up_weight,
    up_bias,
    down_weight,
    down_bias,
    cotangent,
):
    input_f = inputs.astype(jnp.float32)
    normed = layer_norm(input_f, norm_scale[0], norm_shift[0]).astype(jnp.bfloat16)
    normed_full = lax.all_gather(normed, "tensor", axis=0, tiled=True)
    queries, key_rows, values, mixed_out, logsum = attention_part(
        normed_full, head_weight, query_bias, value_bias
    )
    head_terms = jnp.dot(mixed_out, out_weight, preferred_element_type=jnp.float32)
    head_total = lax.psum_scatter(head_terms, "tensor", scatter_dimension=0, tiled=True)
    residual = input_f + (head_total + out_bias)
    normed_two = layer_norm(residual, norm_scale[1], norm_shift[1]).astype(jnp.bfloat16)
    second_full = lax.all_gather(normed_two, "tensor", axis=0, tiled=True)
    pre_act, activated = feed_part(second_full, up_weight, up_bias)
    unit_terms = jnp.dot(activated, down_weight, preferred_element_type=jnp.float32)
    unit_total = lax.psum_scatter(
        unit_terms.astype(jnp.bfloat16), "tensor", scatter_dimension=0, tiled=True
    ).astype(jnp.float32)
    layer_out = (residual + (unit_total + down_bias)).astype(jnp.bfloat16)
    normed_again = layer_norm(input_f, norm_scale[0], norm_shift[0]).astype(jnp.bfloat16)
    normed_full = lax.all_gather(normed_again, "tensor", axis=0, tiled=True)
    queries, key_rows, values, mixed_out, logsum = attention_part(
        normed_full, head_weight, query_bias, value_bias
    )
    again_terms = jnp.dot(mixed_out, out_weight, preferred_element_type=jnp.float32)
    again_total = lax.psum_scatter(again_terms, "tensor", scatter_dimension=0, tiled=True)
    residual = input_f + (again_total + out_bias)
    second_again = layer_norm(residual, norm_scale[1], norm_shift[1]).astype(jnp.bfloat16)
    second_full = lax.all_gather(second_again, "tensor", axis=0, tiled=True)
    pre_act, activated = feed_part(second_full, up_weight, up_bias)
    grad_full = lax.all_gather(cotangent, "tensor", axis=0, tiled=True)
    down_weight_grad = jnp.einsum(
        "tf,td->fd", activated, grad_full, preferred_element_type=jnp.float32
    )
    down_bias_grad = jnp.sum(grad_full, 0, dtype=jnp.float32)
    grad_act = jnp.einsum("td,fd->tf", grad_full, down_weight, preferred_element_type=jnp.float32)
    gelu_pull = jax.vjp(partial(jax.nn.gelu, approximate=True), pre_act)[1]
    grad_pre = gelu_pull(grad_act)[0].astype(jnp.bfloat16)
    up_bias_grad = jnp.sum(grad_pre, 0, dtype=jnp.float32)
    up_weight_grad = jnp.einsum(
        "td,tf->df", second_full, grad_pre, preferred_element_type=jnp.float32
    )
    second_terms = jnp.einsum("tf,df->td", grad_pre, up_weight, preferred_element_type=jnp.float32)
    grad_second = lax.psum_scatter(second_terms, "tensor", scatter_dimension=0, tiled=True)
    second_pull = jax.vjp(layer_norm, residual, norm_scale[1], norm_shift[1])[1]
    grad_resid, scale_two, shift_two = second_pull(grad_second)
    grad_resid = grad_resid + cotangent.astype(jnp.float32)
    branch_low = grad_resid.astype(jnp.bfloat16)
    branch_rows = lax.all_gather(branch_low, "tensor", axis=0, tiled=True)
    out_bias_grad = jnp.sum(branch_rows, 0, dtype=jnp.float32)
    out_weight_grad = jnp.einsum(
        "tc,td->cd", mixed_out, branch_rows, preferred_element_type=jnp.float32
    )
    grad_mixed = jnp.einsum(
        "td,cd->tc", branch_rows, out_weight, preferred_element_type=jnp.float32
    ).astype(jnp.bfloat16)
    grad_q, grad_k, grad_v = lax.map(
        attend_backward,
        (to_heads(queries), to_heads(key_rows), to_heads(values), logsum, to_heads(grad_mixed)),
    )
    grad_stack = jnp.stack([from_heads(grad_q), from_heads(grad_k), from_heads(grad_v)])
    head_weight_grad = jnp.einsum(
        "td,jtc->jdc", normed_full, grad_stack, preferred_element_type=jnp.float32
    )
    query_bias_grad = jnp.sum(grad_stack[0], 0, dtype=jnp.float32)
    value_bias_grad = jnp.sum(grad_stack[2], 0, dtype=jnp.float32)
    first_terms = jnp.einsum(
        "jtc,jdc->td", grad_stack, head_weight, preferred_element_type=jnp.float32
    )
    grad_first = lax.psum_scatter(first_terms, "tensor", scatter_dimension=0, tiled=True)
    first_pull = jax.vjp(layer_norm, input_f, norm_scale[0], norm_shift[0])[1]
    grad_input, scale_one, shift_one = first_pull(grad_first)
    input_grad = (grad_resid + grad_input).astype(jnp.bfloat16)
    scale_sum, shift_sum = lax.psum(
        (jnp.stack([scale_one, scale_two]), jnp.stack([shift_one, shift_two])), ("dp", "tensor")
    )
    grads = (
        head_weight_grad,
        query_bias_grad,
        value_bias_grad,
        out_weight_grad,
        out_bias_grad,
        up_weight_grad,
        up_bias_grad,
        down_weight_grad,
        down_bias_grad,
    )
    summed = lax.psum(
        (grads[0], grads[1], grads[2], grads[3], grads[4], grads[5], grads[6], grads[7], grads[8]),
        "dp",
    )
    return (
        layer_out,
        input_grad,
        scale_sum,
        shift_sum,
        summed[0],
        summed[1],
        summed[2],
        summed[3],
        summed[4],
        summed[5],
        summed[6],
        summed[7],
        summed[8],
    )


def solution(mesh):
    in_specs = (
        P(("dp", "tensor"), None),
        P(),
        P(),
        P(None, None, "tensor"),
        P("tensor"),
        P("tensor"),
        P("tensor", None),
        P(),
        P(None, "tensor"),
        P("tensor"),
        P("tensor", None),
        P(),
        P(("dp", "tensor"), None),
    )
    out_specs = (
        P(("dp", "tensor"), None),
        P(("dp", "tensor"), None),
        P(),
        P(),
        P(None, None, "tensor"),
        P("tensor"),
        P("tensor"),
        P("tensor", None),
        P(),
        P(None, "tensor"),
        P("tensor"),
        P("tensor", None),
        P(),
    )
    return jax.shard_map(local, mesh=mesh, in_specs=in_specs, out_specs=out_specs, check_vma=False)
```

profile of v0, /device:TPU:0, one launch (start us, length us, event | category | flops | bytes accessed | tf_op | source)
XLA Modules:
  0.0 857.2 jit_solution(11974064768287296589)
XLA Ops:
  13.9 35.9 %all-gather.6.cloned.1.call-done = bf16[2048,512]{1,0:T(8,128)(2,1)} async-done(((bf16[1024,512]{1,0:T(8,128)(2,1)}), bf16[2048,512]{1,0:T(8,128)(2,1)}) %all-gather.6.cloned.1.call-update) | async-done | bytes 2097168 | tf_op jit(solution)/shard_map/all_gather | solution.py:121
  76.7 41.4 %while.42 = (s32[]{:T(128)}, bf16[2,1024,4,64]{1,3,2,0:T(8,128)(2,1)}, bf16[2,1024,4,64]{1,3,2,0:T(8,128)(2,1)}, bf16[2,1024,4,64]{1,3,2,0:T(8,128)(2,1)S(1)}, bf16[2,1024,4,64]{1,3,2,0:T(8,128)(2,1)S(1)}, /*index=5*/s32[]{:T(128)}) while((s32[]{:T(128)}, bf16[2,1024,4,64]{1,3,2,0:T(8,128)(2,1)}, bf16[2,1024,4,64]{1,3,2,0:T(8,128)(2,1)}, ...), condition=%wide.region_5.6_spmd, body=%wide.region_2.5_spmd.sunk | while | flops 1100227584 | bytes 37791820 | solution.py:92
  78.3 10.7 %fusion.234 = (f32[4,1024]{1,0:T(4,128)S(1)}, f32[4,1024,1024]{1,2,0:T(8,128)}) fusion(pred[1024,1024]{0,1:T(8,128)(4,1)} %broadcast_compare_fusion.6, bf16[2,1024,4,64]{1,3,2,0:T(8,128)(2,1)S(1)} %get-tuple-element.601, s32[]{:T(128)S(6)} %copy.114, bf16[2,1024,4,64]{1,3,2,0:T(8,128)(2,1)S(1)} %get-tuple-element.600), kind=kOutput, calls=%fused_computation.212.clone.1 | convolution fusion | flops 553649152 | bytes 18891776 | tf_op jit(solution)/shard_map/while/body/eval_jaxpr/sub | solution.py:35
  89.1 8.3 fusion.235
  99.0 10.7 %fusion.234 = (f32[4,1024]{1,0:T(4,128)S(1)}, f32[4,1024,1024]{1,2,0:T(8,128)}) fusion(pred[1024,1024]{0,1:T(8,128)(4,1)} %broadcast_compare_fusion.6, bf16[2,1024,4,64]{1,3,2,0:T(8,128)(2,1)S(1)} %get-tuple-element.601, s32[]{:T(128)S(6)} %copy.114, bf16[2,1024,4,64]{1,3,2,0:T(8,128)(2,1)S(1)} %get-tuple-element.600), kind=kOutput, calls=%fused_computation.212.clone.1 | convolution fusion | flops 553649152 | bytes 18891776 | tf_op jit(solution)/shard_map/while/body/eval_jaxpr/sub | solution.py:35
  109.8 8.3 fusion.235
  124.8 26.8 %while.43 = (s32[]{:T(128)}, bf16[2,1024,4,64]{1,3,2,0:T(8,128)(2,1)}, f32[2,4,1024]{2,1,0:T(4,128)S(1)}, bf16[2,1024,4,64]{1,3,2,0:T(8,128)(2,1)}, bf16[2,1024,...) while((s32[]{:T(128)}, bf16[2,1024,4,64]{1,3,2,0:T(8,128)(2,1)}, ...), condition=%wide.region_13.14_spmd, body=%wide.region_10.13_spmd.sunk | while | flops 1125388288 | bytes 69347504 | solution.py:92
  158.7 19.2 %reduce-scatter.6.cloned.1.call-done = f32[1024,512]{1,0:T(8,128)} async-done(((f32[2048,512]{1,0:T(8,128)}), f32[1024,512]{1,0:T(8,128)}) %reduce-scatter.6.cloned.1.call-update) | async-done | bytes 2097168 | tf_op jit(solution)/shard_map/reduce_scatter | solution.py:126
  178.0 56.7 %reduce-scatter.10.cloned.1.call-done = f32[1024,512]{1,0:T(8,128)} async-done(((f32[2048,512]{1,0:T(8,128)}), f32[1024,512]{1,0:T(8,128)}) %reduce-scatter.10.cloned.1.call-update) | async-done | bytes 2097168 | tf_op jit(solution)/shard_map/reduce_scatter | solution.py:142
  241.7 32.2 %all-gather.12.cloned.1.call-done = bf16[2048,512]{1,0:T(8,128)(2,1)} async-done(((bf16[1024,512]{1,0:T(8,128)(2,1)}), bf16[2048,512]{1,0:T(8,128)(2,1)}) %all-gather.12.cloned.1.call-update) | async-done | bytes 2097168 | tf_op jit(solution)/shard_map/all_gather | solution.py:145
  273.9 7.2 fusion.178
  281.1 27.3 %all-gather.10.cloned.1.call-done = bf16[2048,512]{1,0:T(8,128)(2,1)} async-done(((bf16[1024,512]{1,0:T(8,128)(2,1)}), bf16[2048,512]{1,0:T(8,128)(2,1)}) %all-gather.10.cloned.1.call-update) | async-done | bytes 2097168 | tf_op jit(solution)/shard_map/all_gather | solution.py:147
  308.4 11.0 %convert_reduce_fusion = (f32[1024]{0:T(1024)}, bf16[2048,1024]{1,0:T(8,128)(2,1)S(1)}) fusion(f32[2048,1024]{1,0:T(8,128)} %fusion.178, f32[1024]{0:T(1024)S(1)} %copy-done.60, bf16[2048,512]{1,0:T(8,128)(2,1)} %all-gather.10.cloned.1.call-done, bf16[1024,512]{1,0:T(8,128)(2,1)} %param.29), kind=kOutput, calls=%fused_computation.130 | convolution fusion | flops 2195717120 | bytes 15736832 | tf_op jit(solution)/shard_map/td,fd->tf/dot_general | solution.py:152
  325.9 54.5 %reduce-scatter.12.cloned.1.call-done = f32[1024,512]{1,0:T(8,128)} async-done(((f32[2048,512]{1,0:T(8,128)}), f32[1024,512]{1,0:T(8,128)}) %reduce-scatter.12.cloned.1.call-update) | async-done | bytes 2097168 | tf_op jit(solution)/shard_map/reduce_scatter | solution.py:160
  387.1 33.2 %all-gather.14.cloned.1.call-done = bf16[2048,512]{1,0:T(8,128)(2,1)} async-done(((bf16[1024,512]{1,0:T(8,128)(2,1)}), bf16[2048,512]{1,0:T(8,128)(2,1)}) %all-gather.14.cloned.1.call-update) | async-done | bytes 2097168 | tf_op jit(solution)/shard_map/all_gather | solution.py:165
  430.9 97.1 %while.44 = (s32[]{:T(128)}, bf16[2,1024,4,64]{1,3,2,0:T(8,128)(2,1)}, bf16[2,1024,4,64]{1,3,2,0:T(8,128)(2,1)}, bf16[2,1024,4,64]{1,3,2,0:T(8,128)(2,1)}, bf16[...) while((s32[]{:T(128)}, ...), condition=%wide.region_22.23_spmd, body=%wide.region_20.22_spmd.sunk | while | flops 2724466688 | bytes 183858528 | solution.py:173
  433.1 9.1 %fusion.248 = f32[4,1024,1024]{1,2,0:T(8,128)} fusion(bf16[2,1024,4,64]{1,3,2,0:T(8,128)(2,1)} %get-tuple-element.631, s32[]{:T(128)S(6)} %copy.122, bf16[2,1024,4,64]{1,3,2,0:T(8,128)(2,1)S(1)} %get-tuple-element.630), kind=kOutput, calls=%fused_computation.83.clone.1 | convolution fusion | flops 536870912 | bytes 17826816 | tf_op jit(solution)/shard_map/while/body/eval_jaxpr/qhd,khd->hqk/dot_general | solution.py:53
  442.3 12.7 %multiply_reduce_fusion.6 = (f32[4,1024]{1,0:T(4,128)}, f32[4,1024,1024]{1,2,0:T(8,128)S(1)}) fusion(f32[4,1024,1024]{1,2,0:T(8,128)} %fusion.248, f32[4,1024]{1,0:T(4,128)} %dynamic-slice_bitcast_fusion.2, bf16[2,1024,4,64]{1,3,2,0:T(8,128)(2,1)} %get-tuple-element.627, s32[]{:T(128)S(6)} %copy.122, ...), kind=kOutput, calls=%fused_computation.67.clone.1 | convolution fusion | flops 557838336 | bytes 35685376 | tf_op jit(solution)/shard_map/while/body/eval_jaxpr/qhd,khd->hqk/dot_general | solution.py:48
  454.9 10.4 %multiply_convert_fusion.4 = bf16[4,1024,1024]{1,2,0:T(8,128)(2,1)} fusion(f32[4,1024,1024]{1,2,0:T(8,128)S(1)} %get-tuple-element.562, f32[4,1024,1024]{1,2,0:T(8,128)} %fusion.248, f32[4,1024]{1,0:T(4,128)} %get-tuple-element.563), kind=kLoop, calls=%fused_computation.66.clone.1 | loop fusion | flops 12582912 | bytes 41959424 | tf_op jit(solution)/shard_map/while/body/eval_jaxpr/convert_element_type | solution.py:58
  469.9 7.0 fusion.250
  481.6 9.1 %fusion.248 = f32[4,1024,1024]{1,2,0:T(8,128)} fusion(bf16[2,1024,4,64]{1,3,2,0:T(8,128)(2,1)} %get-tuple-element.631, s32[]{:T(128)S(6)} %copy.122, bf16[2,1024,4,64]{1,3,2,0:T(8,128)(2,1)S(1)} %get-tuple-element.630), kind=kOutput, calls=%fused_computation.83.clone.1 | convolution fusion | flops 536870912 | bytes 17826816 | tf_op jit(solution)/shard_map/while/body/eval_jaxpr/qhd,khd->hqk/dot_general | solution.py:53
  490.8 12.7 %multiply_reduce_fusion.6 = (f32[4,1024]{1,0:T(4,128)}, f32[4,1024,1024]{1,2,0:T(8,128)S(1)}) fusion(f32[4,1024,1024]{1,2,0:T(8,128)} %fusion.248, f32[4,1024]{1,0:T(4,128)} %dynamic-slice_bitcast_fusion.2, bf16[2,1024,4,64]{1,3,2,0:T(8,128)(2,1)} %get-tuple-element.627, s32[]{:T(128)S(6)} %copy.122, ...), kind=kOutput, calls=%fused_computation.67.clone.1 | convolution fusion | flops 557838336 | bytes 35685376 | tf_op jit(solution)/shard_map/while/body/eval_jaxpr/qhd,khd->hqk/dot_general | solution.py:48
  503.4 10.4 %multiply_convert_fusion.4 = bf16[4,1024,1024]{1,2,0:T(8,128)(2,1)} fusion(f32[4,1024,1024]{1,2,0:T(8,128)S(1)} %get-tuple-element.562, f32[4,1024,1024]{1,2,0:T(8,128)} %fusion.248, f32[4,1024]{1,0:T(4,128)} %get-tuple-element.563), kind=kLoop, calls=%fused_computation.66.clone.1 | loop fusion | flops 12582912 | bytes 41959424 | tf_op jit(solution)/shard_map/while/body/eval_jaxpr/convert_element_type | solution.py:58
  518.4 7.0 fusion.250
  558.8 53.9 %reduce-scatter.14.cloned.1.call-done = f32[1024,512]{1,0:T(8,128)} async-done(((f32[2048,512]{1,0:T(8,128)}), f32[1024,512]{1,0:T(8,128)}) %reduce-scatter.14.cloned.1.call-update) | async-done | bytes 2097168 | tf_op jit(solution)/shard_map/reduce_scatter | solution.py:186
  619.4 6.7 fusion.181
  626.1 8.9 %fusion.119 = f32[1024,512]{1,0:T(8,128)} fusion(bf16[2048,512]{1,0:T(8,128)(2,1)S(1)} %copy-done.29, f32[2048,1024]{1,0:T(8,128)} %fusion.178, f32[1024]{0:T(1024)S(1)} %copy-done.61), kind=kOutput, calls=%fused_computation.134 | convolution fusion | flops 2168455168 | bytes 12587008 | tf_op jit(solution)/shard_map/tf,td->fd/dot_general | solution.py:148
  640.2 12.1 %all-gather.8.cloned.1.call-done = bf16[2048,512]{1,0:T(8,128)(2,1)} async-done(((bf16[1024,512]{1,0:T(8,128)(2,1)}), bf16[2048,512]{1,0:T(8,128)(2,1)}) %all-gather.8.cloned.1.call-update) | async-done | bytes 2097168 | tf_op jit(solution)/shard_map/all_gather | solution.py:129
  652.3 7.5 fusion.124
  664.5 63.7 %all-reduce.1 = (f32[256]{0:T(256)}, f32[256]{0:T(256)}, f32[512]{0:T(512)}, f32[1024]{0:T(1024)}, f32[512]{0:T(512)}) all-reduce(f32[256]{0:T(256)S(1)} %reduce_sum.243, f32[256]{0:T(256)S(1)} %reduce_sum.248, f32[512]{0:T(512)S(1)} %convert_reduce_fusion.2, f32[1024]{0:T(1024)S(1)} %copy-done.57, ...), channel_id=1, replica_groups=mesh['dp'=16,'tensor'=2] {'dp'}, use_global_device_ids=true, to_apply=%region_34.35 | all-reduce | flops 2560 | bytes 20480 | tf_op jit(solution)/shard_map/psum | solution.py:204
  728.2 68.8 %all-reduce.5.cloned.1.call-done = (f32[3,512,256]{1,2,0:T(8,128)}, f32[256,512]{1,0:T(8,128)}, f32[512,1024]{1,0:T(8,128)}, f32[1024,512]{1,0:T(8,128)}) async-done(((f32[3,512,256]{1,2,0:T(8,128)}, f32[256,512]{1,0:T(8,128)}, f32[512,1024]{1,0:T(8,128)}, f32[1024,512]{1,0:T(8,128)}), (f32[3,512,256]{1,2,0:T(8,128)}, f32[256,512]{1,0:T(8,128)}, f32[512,1024]{1,0:T(8,128)}, ...) | async-done | bytes 6291472 | tf_op jit(solution)/shard_map/psum | solution.py:204
  800.0 40.8 %all-reduce = (f32[2,512]{1,0:T(2,128)}, f32[2,512]{1,0:T(2,128)}) all-reduce(f32[2,512]{1,0:T(2,128)S(1)} %get-tuple-element.427, f32[2,512]{1,0:T(2,128)S(1)} %get-tuple-element.428), channel_id=1, replica_groups=mesh['dp'=16,'tensor'=2] {'dp','tensor'}, use_global_device_ids=true, to_apply=%region_28.29 | all-reduce | flops 2048 | bytes 16384 | tf_op jit(solution)/shard_map/psum | solution.py:190
  (270 shorter events, 185.8 us)
Async XLA Ops:
  7.2 266.7 %copy-start = (bf16[512,1024]{1,0:T(8,128)(2,1)S(1)}, bf16[512,1024]{1,0:T(8,128)(2,1)}, u32[]{:S(2)}) copy-start(bf16[512,1024]{1,0:T(8,128)(2,1)} %param.27) | copy-start | bytes 3145732
  7.2 42.5 %all-gather.6.cloned.1.call-start = ((), (), s32[]{:S(2)}) async-start(), calls=%async_computation.5 | async-start | bytes 3145728 | tf_op jit(solution)/shard_map/all_gather | solution.py:121
  13.8 164.2 %reduce-scatter.6.cloned.1.call-start = ((), (), s32[]{:S(2)}) async-start(), calls=%async_computation.6 | async-start | bytes 6291456 | tf_op jit(solution)/shard_map/reduce_scatter | solution.py:126
  123.5 111.2 %reduce-scatter.10.cloned.1.call-start = ((), (), s32[]{:S(2)}) async-start(), calls=%async_computation.10 | async-start | bytes 6291456 | tf_op jit(solution)/shard_map/reduce_scatter | solution.py:142
  158.7 76.0 %copy-start.48 = (f32[512]{0:T(512)S(1)}, f32[512]{0:T(512)}, u32[]{:S(2)}) copy-start(f32[512]{0:T(512)} %param.26) | copy-start | bytes 6148
  158.7 115.2 %all-gather.12.cloned.1.call-start = ((), (), s32[]{:S(2)}) async-start(), calls=%async_computation.11 | async-start | bytes 3145728 | tf_op jit(solution)/shard_map/all_gather | solution.py:145
  240.6 67.8 %all-gather.10.cloned.1.call-start = ((), (), s32[]{:S(2)}) async-start(), calls=%async_computation.9 | async-start | bytes 3145728 | tf_op jit(solution)/shard_map/all_gather | solution.py:147
  241.2 67.2 %copy-start.60 = (f32[1024]{0:T(1024)S(1)}, f32[1024]{0:T(1024)}, u32[]{:S(2)}) copy-start(f32[1024]{0:T(1024)} %param.28) | copy-start | bytes 12292
  241.2 139.2 %reduce-scatter.12.cloned.1.call-start = ((), (), s32[]{:S(2)}) async-start(), calls=%async_computation.12 | async-start | bytes 6291456 | tf_op jit(solution)/shard_map/reduce_scatter | solution.py:160
  325.9 94.4 %all-gather.14.cloned.1.call-start = ((), (), s32[]{:S(2)}) async-start(), calls=%async_computation.13 | async-start | bytes 3145728 | tf_op jit(solution)/shard_map/all_gather | solution.py:165
  387.0 225.6 %reduce-scatter.14.cloned.1.call-start = ((), (), s32[]{:S(2)}) async-start(), calls=%async_computation.14 | async-start | bytes 6291456 | tf_op jit(solution)/shard_map/reduce_scatter | solution.py:186
  469.9 7.0 copy-start.5
  558.1 54.6 %copy-start.3 = (bf16[1024,512]{1,0:T(8,128)(2,1)S(1)}, bf16[1024,512]{1,0:T(8,128)(2,1)}, u32[]{:S(2)}) copy-start(bf16[1024,512]{1,0:T(8,128)(2,1)} %param.19) | copy-start | bytes 3145732
  558.1 54.6 %copy-start.37 = (f32[1024]{0:T(1024)S(1)}, f32[1024]{0:T(1024)}, u32[]{:S(2)}) copy-start(f32[1024]{0:T(1024)} %copy-done.36) | copy-start | bytes 12292
  558.1 54.6 %copy-start.43 = (f32[1,512]{1,0:T(1,128)S(1)}, f32[1,512]{1,0:T(1,128)}, u32[]{:S(2)}) copy-start(f32[1,512]{1,0:T(1,128)} %copy-done.42) | copy-start | bytes 6148
  558.1 54.6 %copy-start.49 = (f32[512]{0:T(512)S(1)}, f32[512]{0:T(512)}, u32[]{:S(2)}) copy-start(f32[512]{0:T(512)} %param.26) | copy-start | bytes 6148
  558.2 94.1 %all-gather.8.cloned.1.call-start = ((), (), s32[]{:S(2)}) async-start(), calls=%async_computation.7 | async-start | bytes 3145728 | tf_op jit(solution)/shard_map/all_gather | solution.py:129
  558.8 57.7 %copy-start.47 = (f32[1024]{0:T(1024)S(1)}, f32[1024]{0:T(1024)}, u32[]{:S(2)}) copy-start(f32[1024]{0:T(1024)} %copy-done.46) | copy-start | bytes 12292
  558.8 57.7 %copy-start.39 = (f32[1024]{0:T(1024)S(1)}, f32[1024]{0:T(1024)}, u32[]{:S(2)}) copy-start(f32[1024]{0:T(1024)} %copy-done.38) | copy-start | bytes 12292
  558.8 57.7 %copy-start.41 = (f32[1,512]{1,0:T(1,128)S(1)}, f32[1,512]{1,0:T(1,128)}, u32[]{:S(2)}) copy-start(f32[1,512]{1,0:T(1,128)} %get-tuple-element.420) | copy-start | bytes 6148
  558.8 57.7 %copy-start.51 = (f32[1,512]{1,0:T(1,128)S(1)}, f32[1,512]{1,0:T(1,128)}, u32[]{:S(2)}) copy-start(f32[1,512]{1,0:T(1,128)} %get-tuple-element.422) | copy-start | bytes 6148
  619.0 7.0 copy-start.61
  619.1 177.9 %all-reduce.5.cloned.1.call-start = ((), (), s32[]{:S(2)}) async-start(), calls=%async_computation.15 | async-start | bytes 12582912 | tf_op jit(solution)/shard_map/psum | solution.py:204
  626.1 9.0 %copy-start.18 = (bf16[2048,512]{1,0:T(8,128)(2,1)S(1)}, bf16[2048,512]{1,0:T(8,128)(2,1)}, u32[]{:S(2)}) copy-start(bf16[2048,512]{1,0:T(8,128)(2,1)} %all-gather.14.cloned.1.call-done) | copy-start | bytes 6291460
  626.1 9.0 %copy-start.21 = (bf16[32,8,2,1024]{3,1,2,0:T(8,128)(2,1)S(1)}, bf16[32,8,2,1024]{3,1,2,0:T(8,128)(2,1)}, u32[]{:S(2)}) copy-start(bf16[32,8,2,1024]{3,1,2,0:T(8,128)(2,1)} %copy-done.20) | copy-start | bytes 3145732
  626.1 10.5 %copy-start.30 = (bf16[2048,512]{1,0:T(8,128)(2,1)S(1)}, bf16[2048,512]{1,0:T(8,128)(2,1)}, u32[]{:S(2)}) copy-start(bf16[2048,512]{1,0:T(8,128)(2,1)} %all-gather.6.cloned.1.call-done) | copy-start | bytes 6291460
  640.1 200.7 %reduce-scatter.8.cloned.1.call-start = ((), (), s32[]{:S(2)}) async-start(), calls=%async_computation.8 | async-start | bytes 3145728 | tf_op jit(solution)/shard_map/reduce_scatter | solution.py:132
  664.5 135.6 %copy-start.53 = (f32[512]{0:T(512)S(1)}, f32[512]{0:T(512)}, u32[]{:S(2)}) copy-start(f32[512]{0:T(512)} %get-tuple-element.346) | copy-start | bytes 6148
  664.5 135.6 %copy-start.54 = (f32[512]{0:T(512)S(1)}, f32[512]{0:T(512)}, u32[]{:S(2)}) copy-start(f32[512]{0:T(512)} %get-tuple-element.352) | copy-start | bytes 6148
  664.5 176.3 %copy-start.17 = (bf16[1024,512]{1,0:T(8,128)(2,1)S(1)}, bf16[1024,512]{1,0:T(8,128)(2,1)}, u32[]{:S(2)}) copy-start(bf16[1024,512]{1,0:T(8,128)(2,1)} %param.31) | copy-start | bytes 3145732
  664.5 176.3 %copy-start.45 = (f32[1024]{0:T(1024)S(1)}, f32[1024]{0:T(1024)}, u32[]{:S(2)}) copy-start(f32[1024]{0:T(1024)} %copy-done.44) | copy-start | bytes 12292
  664.5 176.3 %copy-start.58 = (f32[512]{0:T(512)S(1)}, f32[512]{0:T(512)}, u32[]{:S(2)}) copy-start(f32[512]{0:T(512)} %param.30) | copy-start | bytes 6148
  (54 other events, 161.3 us)
Sparse Core Ops, SparseCore 0:
  13.9 35.8 all-gather.5
  123.6 54.3 reduce-scatter.5
  180.3 54.3 reduce-scatter.9
  240.8 33.0 all-gather.11
  275.3 33.0 all-gather.9
  326.0 54.3 reduce-scatter.11
  387.2 33.0 all-gather.13
  558.3 54.3 reduce-scatter.13
  619.2 33.0 all-gather.7
  656.7 140.2 all-reduce.4
  799.8 32.5 reduce-scatter.7
where the time goes:
time: 868 us; the launch traced here: 857 us
  waiting for transfers between devices  395 us (46%)
  matrix products  195 us (22%)
  blocking collectives  104 us (12%)
  local copies, waits for them, and re-layouts  79 us (9%)
  other arithmetic  67.1 us (8%)
  between operations  14.9 us (2%)
    psum x1, waiting for transfers between devices, local(): lax.psum((grads[0], grads[1], grads[2], grads[3], grads[4], grads[5], gra...  68.8 us
    psum x1, blocking collectives, local(): lax.psum((grads[0], grads[1], grads[2], grads[3], grads[4], grads[5], gra...  63.7 us
    reduce_scatter x1, waiting for transfers between devices, local(): lax.psum_scatter(again_terms, 'tensor', scatter_dimension=0, tiled=True)  56.7 us
    reduce_scatter x1, waiting for transfers between devices, local(): lax.psum_scatter(second_terms, 'tensor', scatter_dimension=0, tiled=True)  54.5 us
    reduce_scatter x1, waiting for transfers between devices, local(): lax.psum_scatter(first_terms, 'tensor', scatter_dimension=0, tiled=True)  53.9 us
    psum x1, blocking collectives, local(): lax.psum((jnp.stack([scale_one, scale_two]), jnp.stack([shift_one, shift_...  40.8 us
    all_gather x1, waiting for transfers between devices, local(): normed_full = lax.all_gather(normed, 'tensor', axis=0, tiled=True)  35.9 us
    all_gather x1, waiting for transfers between devices, local(): branch_rows = lax.all_gather(branch_low, 'tensor', axis=0, tiled=True)  33.2 us
  transfers between devices with their start and end apart: 11, of which 10 were waited for; matrix products, arithmetic and copies ran while one was open for 9% of the time, Pallas kernels for 0%

commit v1 on v0

v1 whole, which is shorter than its diff:
```python
from functools import partial

import jax
import jax.numpy as jnp
from jax import lax
from jax.sharding import PartitionSpec as P

HD = 64
BLK = 256
EPSILON = 1e-05
F32 = jnp.float32
BF16 = jnp.bfloat16


def layer_norm(values, gain, shift):
    center = jnp.mean(values, -1, keepdims=True)
    centered = values - center
    spread = jnp.mean(centered * centered, -1, keepdims=True)
    return centered * lax.rsqrt(spread + EPSILON) * gain + shift


def split_heads(t):
    return t.reshape(t.shape[0], t.shape[1] // HD, HD).transpose(1, 0, 2)


def merge_heads(t):
    return t.transpose(1, 0, 2).reshape(t.shape[1], t.shape[0] * t.shape[2])


def local(inputs, norm_scale, norm_shift, head_weight, query_bias, value_bias, out_weight, out_bias,
          up_weight, up_bias, down_weight, down_bias, cotangent):
    dot = partial(jnp.einsum, preferred_element_type=F32)
    gather = lambda w, d: lax.all_gather(w, "tensor", axis=d, tiled=True)
    hw = gather(head_weight, 2)
    qb, vb = gather(query_bias, 0), gather(value_bias, 0)
    ow = gather(out_weight, 0)
    uw, ub, dw = gather(up_weight, 1), gather(up_bias, 0), gather(down_weight, 0)
    x = inputs.astype(F32)
    n1 = layer_norm(x, norm_scale[0], norm_shift[0]).astype(BF16)
    q = (dot("td,dc->tc", n1, hw[0]) + qb).astype(BF16)
    k = dot("td,dc->tc", n1, hw[1]).astype(BF16)
    v = (dot("td,dc->tc", n1, hw[2]) + vb).astype(BF16)
    qh, kh, vh = split_heads(q), split_heads(k), split_heads(v)
    rows = x.shape[0]
    probs, outs = [], []
    for b in range(rows // BLK):
        hi = (b + 1) * BLK
        s = dot("hqd,hkd->hqk", qh[:, b * BLK:hi], kh[:, :hi]) * HD ** -0.5
        e = jnp.exp(s - jnp.max(s, -1, keepdims=True))
        p = (e / jnp.sum(e, -1, keepdims=True)).astype(BF16)
        probs.append(p)
        outs.append(dot("hqk,hkd->hqd", p, vh[:, :hi]).astype(BF16))
    mixed = merge_heads(jnp.concatenate(outs, 1))
    residual = x + (dot("tc,cd->td", mixed, ow) + out_bias)
    n2 = layer_norm(residual, norm_scale[1], norm_shift[1]).astype(BF16)
    pre = dot("td,df->tf", n2, uw) + ub
    act, gelu_pull = jax.vjp(partial(jax.nn.gelu, approximate=True), pre)
    act = act.astype(BF16)
    layer_out = (residual + (dot("tf,fd->td", act, dw) + down_bias)).astype(BF16)
    d_dw = dot("tf,td->fd", act, cotangent)
    gf = cotangent.astype(F32)
    d_db = jnp.sum(gf, 0)
    gpre = gelu_pull(dot("td,fd->tf", cotangent, dw))[0].astype(BF16)
    d_ub = jnp.sum(gpre.astype(F32), 0)
    d_uw = dot("td,tf->df", n2, gpre)
    g2 = dot("tf,df->td", gpre, uw)
    gres, sc2, sh2 = jax.vjp(layer_norm, residual, norm_scale[1], norm_shift[1])[1](g2)
    gres = gres + gf
    br = gres.astype(BF16)
    d_ob = jnp.sum(br.astype(F32), 0)
    d_ow = dot("tc,td->cd", mixed, br)
    gm = split_heads(dot("td,cd->tc", br, ow).astype(BF16))
    gq, gk, gv = [], 0.0, 0.0
    for b in range(rows // BLK):
        hi = (b + 1) * BLK
        pad = lambda t: jnp.pad(t, ((0, 0), (0, rows - hi), (0, 0)))
        p, g = probs[b], gm[:, b * BLK:hi]
        gp = dot("hqd,hkd->hqk", g, vh[:, :hi])
        pf = p.astype(F32)
        gs = (pf * (gp - jnp.sum(pf * gp, -1, keepdims=True))).astype(BF16)
        gq.append(dot("hqk,hkd->hqd", gs, kh[:, :hi]))
        gk = gk + pad(dot("hqk,hqd->hkd", gs, qh[:, b * BLK:hi]))
        gv = gv + pad(dot("hqk,hqd->hkd", p, g))
    gq = merge_heads((jnp.concatenate(gq, 1) * HD ** -0.5).astype(BF16))
    gk = merge_heads((gk * HD ** -0.5).astype(BF16))
    gv = merge_heads(gv.astype(BF16))
    d_hw = jnp.stack([dot("td,tc->dc", n1, g) for g in (gq, gk, gv)])
    d_qb, d_vb = jnp.sum(gq.astype(F32), 0), jnp.sum(gv.astype(F32), 0)
    g1 = dot("tc,dc->td", gq, hw[0]) + dot("tc,dc->td", gk, hw[1]) + dot("tc,dc->td", gv, hw[2])
    gin, sc1, sh1 = jax.vjp(layer_norm, x, norm_scale[0], norm_shift[0])[1](g1)
    input_grad = (gres + gin).astype(BF16)
    scat = lambda g, d: lax.psum_scatter(g, "tensor", scatter_dimension=d, tiled=True)
    big = (scat(d_hw, 2), scat(d_ow, 0), scat(d_uw, 1), scat(d_dw, 0))
    big = lax.psum(big, "dp")
    small = lax.psum((jnp.stack([sc1, sc2]), jnp.stack([sh1, sh2]), d_qb, d_vb, d_ob, d_ub, d_db), ("dp", "tensor"))
    mine = lambda g: lax.dynamic_slice_in_dim(
        g, lax.axis_index("tensor") * (g.shape[0] // lax.axis_size("tensor")), g.shape[0] // lax.axis_size("tensor"))
    return (layer_out, input_grad, small[0], small[1], big[0], mine(small[2]), mine(small[3]), big[1], small[4],
            big[2], mine(small[5]), big[3], small[6])


def solution(mesh):
    in_specs = (P(("dp", "tensor"), None), P(), P(), P(None, None, "tensor"), P("tensor"), P("tensor"), P("tensor", None),
                P(), P(None, "tensor"), P("tensor"), P("tensor", None), P(), P(("dp", "tensor"), None))
    out_specs = (P(("dp", "tensor"), None), P(("dp", "tensor"), None), P(), P(), P(None, None, "tensor"), P("tensor"),
                 P("tensor"), P("tensor", None), P(), P(None, "tensor"), P("tensor"), P("tensor", None), P())
    return jax.shard_map(local, mesh=mesh, in_specs=in_specs, out_specs=out_specs, check_vma=False)
```

time: 868 us -> 522 us (0.60)
  waiting for transfers between devices: 395 us -> 263 us
  matrix products: 195 us -> 98.7 us
  local copies, waits for them, and re-layouts: 79 us -> 35.3 us
  other arithmetic: 67.1 us -> 29.8 us
  blocking collectives: 104 us -> 69.9 us
    all_gather x5 -> x3, waiting for transfers between devices: 141 us -> 25.3 us  [local(): gather = lambda w, d: lax.all_gather(w, 'tensor', axis=d, tiled=True)]
    dot_general x31 -> x40, matrix products: 174 us -> 91.8 us  [the longest x1 10.3 us: local(): gpre = gelu_pull(dot('td,fd->tf', cotangent, dw))[0].astype(BF16)]
    psum x2 -> x1, blocking collectives: 104 us -> 41.5 us  [local(): lax.psum((jnp.stack([sc1, sc2]), jnp.stack([sh1, sh2]), d_qb, d_vb, d_ob,...]
    reduce_scatter x5 -> x4, waiting for transfers between devices: 184 us -> 152 us  [local(): lax.psum_scatter(g, 'tensor', scatter_dimension=d, tiled=True)]
    another operation x12 -> x0, local copies, waits for them, and re-layouts: 28.4 us -> none  [the longest x7 22.9 us: local(): jnp.stack([from_heads(grad_q), from_heads(grad_k), from_heads(grad_v)])]
    all_gather x0 -> x4, blocking collectives: none -> 28.4 us  [local(): gather = lambda w, d: lax.all_gather(w, 'tensor', axis=d, tiled=True)]
    while x46 -> x0, local copies, waits for them, and re-layouts: 20.2 us -> none  [the longest x5 15.3 us: attention_part(): lax.map(attend_forward, (to_heads(queries), to_heads(key_rows), to_heads(...]
    convert_element_type x6 -> x8, other arithmetic: 29.7 us -> 11.7 us  [the longest x4 9.1 us: local(): gs = (pf * (gp - jnp.sum(pf * gp, -1, keepdims=True))).astype(BF16)]
  transfers between devices with their start and end apart: 11 -> 8, of which waited for: 10 -> 6; matrix products, arithmetic and copies ran while one was open for 9% -> 17% of each run, Pallas kernels for 0% -> 0%
where the time goes in v1:
time: 522 us; the launch traced here: 513 us
  waiting for transfers between devices  263 us (50%)
  matrix products  98.7 us (19%)
  blocking collectives  69.9 us (13%)
  local copies, waits for them, and re-layouts  35.3 us (7%)
  other arithmetic  29.8 us (6%)
  between operations  15.4 us (3%)
    reduce_scatter x4, waiting for transfers between devices, local(): lax.psum_scatter(g, 'tensor', scatter_dimension=d, tiled=True)  152 us
    psum x1, waiting for transfers between devices, local(): big = lax.psum(big, 'dp')  83.6 us
    psum x1, blocking collectives, local(): lax.psum((jnp.stack([sc1, sc2]), jnp.stack([sh1, sh2]), d_qb, d_vb, d_ob,...  41.5 us
    unnamed x138, local copies, waits for them, and re-layouts  30.2 us
    all_gather x4, blocking collectives, local(): gather = lambda w, d: lax.all_gather(w, 'tensor', axis=d, tiled=True)  28.4 us
    all_gather x3, waiting for transfers between devices, local(): gather = lambda w, d: lax.all_gather(w, 'tensor', axis=d, tiled=True)  25.3 us
  transfers between devices with their start and end apart: 8, of which 6 were waited for; matrix products, arithmetic and copies ran while one was open for 17% of the time, Pallas kernels for 0%

profile of v1, /device:TPU:0, one launch (start us, length us, event | category | flops | bytes accessed | tf_op | source)
XLA Modules:
  0.0 513.0 jit_solution(9560738680294393389)
XLA Ops:
  10.7 5.2 %all-gather = f32[2,1,256]{2,1,0:T(1,128)S(1)} all-gather(f32[1,1,256]{2,1,0:T(1,128)S(1)} %bitcast.172), channel_id=1, replica_groups=mesh['dp'=16,'tensor'=2] {'tensor'}, dimensions={0}, use_global_device_ids=true | all-gather | bytes 3072 | tf_op jit(solution)/shard_map/all_gather | solution.py:33
  15.8 4.2 all-gather.1
  20.1 13.9 %all_gather.24 = bf16[512,512]{1,0:T(8,128)(2,1)} all-gather(bf16[256,512]{1,0:T(8,128)(2,1)S(1)} %copy-done.51), channel_id=1, replica_groups=mesh['dp'=16,'tensor'=2] {'tensor'}, dimensions={0}, use_global_device_ids=true | all-gather | bytes 786432 | tf_op jit(solution)/shard_map/all_gather | solution.py:33
  33.9 5.1 all_gather.26
  40.3 3.6 all-gather.6.cloned.1.call-done
  45.8 2.3 add_convert_fusion.5
  48.1 2.7 fusion.62
  50.8 3.7 fusion.53
  56.8 4.8 fusion.133
  61.6 4.7 fusion.139
  66.8 2.3 fusion.138
  69.6 2.3 add_convert_fusion.4
  83.6 9.2 %multiply_convert_fusion = (bf16[1024,2048]{1,0:T(8,128)(2,1)}, f32[1024,2048]{1,0:T(8,128)}) fusion(f32[2048]{0:T(1024)S(1)} %all_gather.26, bf16[512,2048]{1,0:T(8,128)(2,1)} %all-gather.8.cloned.1.call-done, f32[1024,512]{0,1:T(8,128)S(1)} %get-tuple-element.77, f32[512]{0:T(512)S(1)} %bitcast.163, f32[512]{0:T(512)S(1)} %bitcast.154, ...), kind=kOutput, calls=%fused_computation.18 | convolution fusion | flops 2171076608 | bytes 16797696 | tf_op jit(solution)/shard_map/td,df->tf/dot_general | solution.py:56
  92.8 21.7 %all-gather.10.cloned.1.call-done = bf16[2048,512]{1,0:T(8,128)(2,1)} async-done(((bf16[1024,512]{1,0:T(8,128)(2,1)}), bf16[2048,512]{1,0:T(8,128)(2,1)}) %all-gather.10.cloned.1.call-update) | async-done | bytes 2097168 | tf_op jit(solution)/shard_map/all_gather | solution.py:33
  114.5 10.3 %convert_reduce_fusion = (f32[2048]{0:T(1024)S(1)}, bf16[1024,2048]{1,0:T(8,128)(2,1)S(1)}) fusion(f32[1024,2048]{1,0:T(8,128)} %get-tuple-element.79, f32[2048]{0:T(1024)S(1)} %all_gather.26, bf16[1024,512]{1,0:T(8,128)(2,1)} %param.25, bf16[2048,512]{1,0:T(8,128)(2,1)} %all-gather.10.cloned.1.call-done), kind=kOutput, calls=%fused_computation.17 | convolution fusion | flops 2195716096 | bytes 15745024 | tf_op jit(solution)/shard_map/td,fd->tf/dot_general | solution.py:63
  124.8 3.7 fusion.146
  128.5 3.1 copy.43
  131.6 2.4 multiply_reduce_fusion.3
  143.2 4.6 fusion.4
  161.0 6.8 %fusion.5 = bf16[8,256,1024]{2,1,0:T(8,128)(2,1)S(1)} fusion(f32[8,256,1024]{2,1,0:T(8,128)} %get-tuple-element.81, f32[8,256]{1,0:T(8,128)S(1)} %get-tuple-element.80, f32[8,256,1024]{2,1,0:T(8,128)} %get-tuple-element.69, f32[8,256]{1,0:T(8,128)S(1)} %get-tuple-element.68), kind=kLoop, calls=%fused_computation.9 | loop fusion | flops 12582912 | bytes 20987904 | tf_op jit(solution)/shard_map/convert_element_type | solution.py:80
  167.8 2.2 fusion.147
  187.7 6.7 %fusion.119 = f32[512,2048]{1,0:T(8,128)} fusion(bf16[1024,2048]{1,0:T(8,128)(2,1)} %copy-done.60, f32[1024,512]{0,1:T(8,128)S(1)} %get-tuple-element.77, f32[512]{0:T(512)S(1)} %bitcast.164, f32[512]{0:T(512)S(1)} %bitcast.157, f32[1024]{0:T(1024)S(1)} %fusion.110, f32[1024]{0:T(1024)S(1)} %broadcast_multiply_fusion), kind=kOutput, calls=%fused_computation.166 | convolution fusion | flops 2150105088 | bytes 10498048 | tf_op jit(solution)/shard_map/td,tf->df/dot_general | solution.py:65
  194.5 6.8 %fusion.149 = f32[2048,512]{1,0:T(8,128)} fusion(bf16[1024,2048]{1,0:T(8,128)(2,1)} %get-tuple-element.78, bf16[1024,512]{1,0:T(8,128)(2,1)} %param.25), kind=kOutput, calls=%fused_computation.180 | convolution fusion | flops 2147483648 | bytes 9437184 | tf_op jit(solution)/shard_map/tf,td->fd/dot_general | solution.py:60
  201.8 38.9 %reduce-scatter.5.cloned.1.call-done = f32[3,512,256]{2,1,0:T(8,128)} async-done(((f32[3,512,512]{2,1,0:T(8,128)}), f32[3,512,256]{2,1,0:T(8,128)}) %reduce-scatter.5.cloned.1.call-update) | async-done | bytes 1572880 | tf_op jit(solution)/shard_map/reduce_scatter | solution.py:92
  240.8 56.6 %reduce-scatter.9.cloned.1.call-done = f32[512,1024]{1,0:T(8,128)} async-done(((f32[512,2048]{1,0:T(8,128)}), f32[512,1024]{1,0:T(8,128)}) %reduce-scatter.9.cloned.1.call-update) | async-done | bytes 2097168 | tf_op jit(solution)/shard_map/reduce_scatter | solution.py:92
  297.3 56.7 %reduce-scatter.11.cloned.1.call-done = f32[1024,512]{1,0:T(8,128)} async-done(((f32[2048,512]{1,0:T(8,128)}), f32[1024,512]{1,0:T(8,128)}) %reduce-scatter.11.cloned.1.call-update) | async-done | bytes 2097168 | tf_op jit(solution)/shard_map/reduce_scatter | solution.py:92
  354.1 2.2 fusion.56
  362.5 41.5 %all-reduce.6 = (f32[2,512]{1,0:T(2,128)}, f32[2,512]{1,0:T(2,128)}, f32[512]{0:T(512)S(1)}, f32[512]{0:T(512)S(1)}, f32[512]{0:T(512)}, /*index=5*/f32[2048]{0:T(1024)S(1)}, f32[512]{0:T(512)}) all-reduce(f32[2,512]{1,0:T(2,128)S(1)} %get-tuple-element.95, ...), channel_id=1, replica_groups=mesh['dp'=16,'tensor'=2] {'dp','tensor'}, use_global_device_ids=true, to_apply=%region_22.0 | all-reduce | flops 6144 | bytes 49152 | tf_op jit(solution)/shard_map/psum | solution.py:95
  405.3 2.3 copy.53
  407.6 5.2 %add_convert_fusion.2 = bf16[1024,512]{0,1:T(8,128)(2,1)S(1)} fusion(f32[1024,512]{0,1:T(8,128)S(1)} %get-tuple-element.77, bf16[1024,2048]{1,0:T(8,128)(2,1)} %get-tuple-element.78, bf16[2048,512]{1,0:T(8,128)(2,1)} %all-gather.10.cloned.1.call-done, f32[512]{0:T(512)S(1)} %copy-done.59), kind=kOutput, calls=%fused_computation.75 | convolution fusion | flops 2149056512 | bytes 9439232 | tf_op jit(solution)/shard_map/tf,fd->td/dot_general | solution.py:59
  414.8 83.6 %all-reduce.10.cloned.1.call-done = (f32[3,512,256]{2,1,0:T(8,128)}, f32[256,512]{1,0:T(8,128)}, f32[512,1024]{1,0:T(8,128)}, f32[1024,512]{1,0:T(8,128)}) async-done(((f32[3,512,256]{2,1,0:T(8,128)}, f32[256,512]{1,0:T(8,128)}, f32[512,1024]{1,0:T(8,128)}, f32[1024,512]{1,0:T(8,128)}), (f32[3,512,256]{2,1,0:T(8,128)}, f32[256,512]{1,0:T(8,128)}, f32[512,1024]{1,0:T(8,128)}, ...) | async-done | bytes 6291472 | tf_op jit(solution)/shard_map/psum | solution.py:94
  498.4 2.8 copy.66
  (217 shorter events, 75.4 us)
Async XLA Ops:
  7.2 36.7 %all-gather.6.cloned.1.call-start = ((), (), s32[]{:S(2)}) async-start(), calls=%async_computation.4 | async-start | bytes 2359296 | tf_op jit(solution)/shard_map/all_gather | solution.py:33
  7.9 75.7 %all-gather.8.cloned.1.call-start = ((), (), s32[]{:S(2)}) async-start(), calls=%async_computation.5 | async-start | bytes 3145728 | tf_op jit(solution)/shard_map/all_gather | solution.py:33
  8.7 105.8 %all-gather.10.cloned.1.call-start = ((), (), s32[]{:S(2)}) async-start(), calls=%async_computation.6 | async-start | bytes 3145728 | tf_op jit(solution)/shard_map/all_gather | solution.py:33
  9.4 6.4 %copy-start.56 = (f32[256]{0:T(256)S(1)}, f32[256]{0:T(256)}, u32[]{:S(2)}) copy-start(f32[256]{0:T(256)} %param.18) | copy-start | bytes 3076
  9.4 10.6 %copy-start.51 = (bf16[256,512]{1,0:T(8,128)(2,1)S(1)}, bf16[256,512]{1,0:T(8,128)(2,1)}, u32[]{:S(2)}) copy-start(bf16[256,512]{1,0:T(8,128)(2,1)} %param.19) | copy-start | bytes 786436
  9.5 24.5 %copy-start.52 = (f32[1024]{0:T(1024)S(1)}, f32[1024]{0:T(1024)}, u32[]{:S(2)}) copy-start(f32[1024]{0:T(1024)} %param.22) | copy-start | bytes 12292
  9.5 29.6 %copy-start.44 = (bf16[1024,512]{1,0:T(8,128)(2,1)S(1)}, bf16[1024,512]{1,0:T(8,128)(2,1)}, u32[]{:S(2)}) copy-start(bf16[1024,512]{1,0:T(8,128)(2,1)} %param.25) | copy-start | bytes 3145732
  9.5 192.3 %reduce-scatter.7.cloned.1.call-start = ((), (), s32[]{:S(2)}) async-start(), calls=%async_computation.8 | async-start | bytes 1572864 | tf_op jit(solution)/shard_map/reduce_scatter | solution.py:92
  45.8 10.9 %copy-start.21 = (bf16[1024,512]{0,1:T(8,128)(2,1)}, bf16[1024,512]{0,1:T(8,128)(2,1)S(1)}, u32[]{:S(2)}) copy-start(bf16[1024,512]{0,1:T(8,128)(2,1)S(1)} %convolution_convert_fusion.1) | copy-start | bytes 3145732
  48.1 8.6 %copy-start.37 = (bf16[1024,512]{0,1:T(8,128)(2,1)}, bf16[1024,512]{0,1:T(8,128)(2,1)S(1)}, u32[]{:S(2)}) copy-start(bf16[1024,512]{0,1:T(8,128)(2,1)S(1)} %add_convert_fusion.5) | copy-start | bytes 3145732
  61.6 5.2 %copy-start.9 = (f32[8,256,768]{2,1,0:T(8,128)S(1)}, f32[8,256,768]{2,1,0:T(8,128)}, u32[]{:S(2)}) copy-start(f32[8,256,768]{2,1,0:T(8,128)} %fusion.53) | copy-start | bytes 18874372
  69.2 3.5 copy-start.3
  71.9 7.5 %copy-start.19 = (bf16[1024,512]{0,1:T(8,128)(2,1)}, bf16[1024,512]{0,1:T(8,128)(2,1)S(1)}, u32[]{:S(2)}) copy-start(bf16[1024,512]{0,1:T(8,128)(2,1)S(1)} %add_convert_fusion.4) | copy-start | bytes 3145732
  71.9 5.3 %slice-start.2 = ((s8[8388608]{0:T(1024)(128)(4,1)}), s8[4194304]{0:T(1024)(128)(4,1)S(1)}, s32[]{:S(2)}) async-start(s8[8388608]{0:T(1024)(128)(4,1)} %bitcast.103), calls=%async_computation.14 | async-start | bytes 8388608
  72.7 5.1 slice-start.3
  73.2 3.5 copy-start.26
  114.5 10.3 %copy-start.57 = (bf16[512,2048]{1,0:T(8,128)(2,1)S(1)}, bf16[512,2048]{1,0:T(8,128)(2,1)}, u32[]{:S(2)}) copy-start(bf16[512,2048]{1,0:T(8,128)(2,1)} %all-gather.8.cloned.1.call-done) | copy-start | bytes 6291460
  124.7 3.7 copy-start.60
  137.0 5.1 copy-start.30
  143.2 4.6 copy-start.27
  143.2 5.0 copy-start.38
  147.8 2.8 copy-start.5
  150.5 3.8 slice-start
  150.5 3.8 slice-start.1
  161.0 6.8 %copy-start.23 = (bf16[1024,512]{0,1:T(8,128)(2,1)S(1)}, bf16[1024,512]{0,1:T(8,128)(2,1)}, u32[]{:S(2)}) copy-start(bf16[1024,512]{0,1:T(8,128)(2,1)} %copy-done.21) | copy-start | bytes 3145732
  174.7 66.1 %reduce-scatter.5.cloned.1.call-start = ((), (), s32[]{:S(2)}) async-start(), calls=%async_computation.7 | async-start | bytes 4718592 | tf_op jit(solution)/shard_map/reduce_scatter | solution.py:92
  187.7 109.7 %reduce-scatter.9.cloned.1.call-start = ((), (), s32[]{:S(2)}) async-start(), calls=%async_computation.9 | async-start | bytes 6291456 | tf_op jit(solution)/shard_map/reduce_scatter | solution.py:92
  194.4 159.6 %reduce-scatter.11.cloned.1.call-start = ((), (), s32[]{:S(2)}) async-start(), calls=%async_computation.10 | async-start | bytes 6291456 | tf_op jit(solution)/shard_map/reduce_scatter | solution.py:92
  201.4 297.0 %all-reduce.10.cloned.1.call-start = ((), (), s32[]{:S(2)}) async-start(), calls=%async_computation.11 | async-start | bytes 12582912 | tf_op jit(solution)/shard_map/psum | solution.py:94
  362.5 45.1 %copy-start.59 = (f32[512]{0:T(512)S(1)}, f32[512]{0:T(512)}, u32[]{:S(2)}) copy-start(f32[512]{0:T(512)} %param.24) | copy-start | bytes 6148
  498.4 2.8 copy-start.50
  498.4 3.6 copy-start.41
  (41 other events, 72.0 us)
Sparse Core Ops, SparseCore 0:
  9.5 34.3 all-gather.5
  45.4 34.3 all-gather.7
  81.4 33.0 all-gather.9
  174.8 20.3 reduce-scatter.6
  197.3 43.3 reduce-scatter.4
  242.9 54.3 reduce-scatter.8
  299.6 54.3 reduce-scatter.10
  358.0 140.3 all-reduce.9

commit v2 on v1

v2 whole, which is shorter than its diff:
```python
import functools
import jax, jax.numpy as jnp
from jax import lax
from jax.experimental import pallas as pl
from jax.experimental.pallas import tpu as pltpu

F32, BF16 = jnp.float32, jnp.bfloat16
NN, NT, TN = ((1,), (0,)), ((1,), (1,)), ((0,), (0,))
EPS = 1e-5
LOG2E = 1.4426950408889634
LN2 = 0.6931471805599453
C0, C1 = 0.7978845608, 0.044715
HD, BLK = 64, 256


def dot(a, b, dims=NN):
    return lax.dot_general(a, b, (dims, ((), ())), preferred_element_type=F32)


def normed(v):
    c = jnp.mean(v, -1, keepdims=True)
    d = v - c
    r = lax.rsqrt(jnp.mean(d * d, -1, keepdims=True) + EPS)
    return d * r, r


def ln_back(g, xhat, r, gain):
    gx = g * gain
    return r * (gx - jnp.mean(gx, -1, keepdims=True) - xhat * jnp.mean(gx * xhat, -1, keepdims=True))


class Refs:
    pass


def rows_of(r):
    return pl.ds(pl.multiple_of(r * BLK, BLK), BLK)


def ln1(z):
    def body(r, c):
        xh, _ = normed(z.x[rows_of(r), :].astype(F32))
        n = (xh * z.ns[0:1, :] + z.nsh[0:1, :]).astype(BF16)
        z.n1T[:, rows_of(r)] = n.T
        return c
    lax.fori_loop(0, z.nb, body, 0)


def column(row):
    return jnp.broadcast_to(row, (8, row.shape[-1])).T[:, 0:1]


def qkv(z, s):
    n = z.n1T
    hw = z.hw
    for qb in range(z.nb):
        sl = slice(qb * BLK, (qb + 1) * BLK)
        nt = n[:, sl]
        q = dot(hw[s, 0], nt, TN) + column(z.qb[s])
        z.qT[s, :, sl] = (q * (LOG2E / 8.0)).astype(BF16)
        z.kT[s, :, sl] = dot(hw[s, 1], nt, TN).astype(BF16)
        v = (dot(hw[s, 2], nt, TN) + column(z.vb[s])).astype(BF16)
        for h in range(z.nh):
            z.vT[s, h, 0:HD, sl] = v[h * HD:(h + 1) * HD]
            z.vT[s, h, HD:HD + 16, sl] = jnp.ones((16, BLK), BF16)


def attn_fwd(z, s):
    def body(h, c):
        hr = pl.ds(pl.multiple_of(h * HD, HD), HD)
        kh = z.kT[s, hr, :].T
        for qb in range(z.nb):
            nk = BLK * (qb + 1)
            off = BLK * (qb * (qb + 1) // 2)
            sl = slice(qb * BLK, nk)
            sc = dot(kh[:nk], z.qT[s, hr, sl])
            m = jnp.max(sc, 0, keepdims=True)
            e = jnp.exp2(sc - m).astype(BF16)
            z.E[s * z.nh + h, off:off + nk, :] = e
            o = dot(z.vT[s, h, :, 0:nk], e)
            rl = 1.0 / o[HD:HD + 1]
            z.rl[s * z.nh + h, 0:1, sl] = rl
            z.mixT[s, hr, sl] = (o[0:HD] * rl).astype(BF16)
        return c
    lax.fori_loop(0, z.nh, body, 0)


def out_proj(z):
    for r in range(z.nb):
        sl = slice(r * BLK, (r + 1) * BLK)
        t = dot(z.mixT[0, :, sl], z.ow[0], TN) + dot(z.mixT[1, :, sl], z.ow[1], TN)
        res = z.x[sl, :].astype(F32) + (t + z.ob[...])
        z.res[sl, :] = res
        xh, _ = normed(res)
        z.n2[sl, :] = (xh * z.ns[1:2, :] + z.nsh[1:2, :]).astype(BF16)


def ffn(z, s, first, last):
    def body(r, c):
        rr = rows_of(r)
        n2 = z.n2[rr, :]
        ct = z.cot[rr, :]
        fh = z.ub.shape[-1]
        FC = 512
        for f in range(0, fh, FC):
            fs = slice(f, f + FC)
            u = dot(n2, z.uw[s, :, fs]) + z.ub[s, :, fs]
            da = dot(ct, z.dw[s, fs, :], NT)
            u2 = u * u
            t = jnp.tanh(u * (C0 + (C0 * C1) * u2))
            hp = 0.5 + 0.5 * t
            a = (u * hp).astype(BF16)
            gp = hp + (u * (0.5 - 0.5 * t * t)) * (C0 + (3 * C0 * C1) * u2)
            dp = (da * gp).astype(BF16)
            z.act[s, rr, fs] = a
            z.dpre[s, rr, fs] = dp
        o = dot(z.act[s, rr, :], z.dw[s])
        g = dot(z.dpre[s, rr, :], z.uw[s], NT)
        if first:
            z.oacc[rr, :] = z.res[rr, :] + (o + z.db[...])
            z.g2[rr, :] = g
        elif not last:
            z.oacc[rr, :] = z.oacc[rr, :] + o
            z.g2[rr, :] = z.g2[rr, :] + g
        else:
            z.lo[rr, :] = (z.oacc[rr, :] + o).astype(BF16)
            g2 = z.g2[rr, :] + g
            xh, rs = normed(z.res[rr, :])
            gres = ct.astype(F32) + ln_back(g2, xh, rs, z.ns[1:2, :])
            br = gres.astype(BF16)
            z.res[rr, :] = gres
            z.br[rr, :] = br
            c = (c[0] + jnp.sum(g2 * xh, 0, keepdims=True), c[1] + jnp.sum(g2, 0, keepdims=True),
                 c[2] + jnp.sum(br.astype(F32), 0, keepdims=True), c[3] + jnp.sum(ct.astype(F32), 0, keepdims=True))
        return c
    zero = jnp.zeros((1, z.ns.shape[-1]), F32)
    c = lax.fori_loop(0, z.nb, body, (zero,) * 4 if last else 0)
    if last:
        z.small[1:2, :] = c[0]
        z.small[3:4, :] = c[1]
        z.small[4:5, :] = c[2]
        z.small[5:6, :] = c[3]


def rowsum(t):
    return dot(jnp.ones((8, t.shape[-1]), BF16), t, NT)[0:1]


def d_down(z, s):
    for f in range(0, z.ub.shape[-1], 256):
        z.GD[s, f:f + 256, :] = dot(z.act[s, :, f:f + 256], z.cot[...], TN).astype(BF16)


def d_up(z, s):
    fh = z.ub.shape[-1]
    ones = jnp.ones((8, z.dpre.shape[1]), BF16)
    for f in range(0, fh, 512):
        z.GU[s, :, f:f + 512] = dot(z.n2[...], z.dpre[s, :, f:f + 512], TN).astype(BF16)
        z.small[8 + 2 * s + f // 512:9 + 2 * s + f // 512, :] = dot(ones, z.dpre[s, :, f:f + 512])[0:1]


def d_out(z):
    for s in (0, 1):
        z.GO[s] = dot(z.mixT[s], z.br[...]).astype(BF16)
        for r in range(z.nb):
            sl = slice(r * BLK, (r + 1) * BLK)
            z.gmT[s, :, sl] = dot(z.ow[s], z.br[sl, :], NT).astype(BF16)


def attn_bwd(z, s, hook=None):
    def body(h, c):
        hr = pl.ds(pl.multiple_of(h * HD, HD), HD)
        hi = s * z.nh + h
        vh = z.vT[s, h, 0:HD, :].T
        gs = (z.gmT[s, hr, :].astype(F32) * z.rl[hi]).astype(BF16)
        delta = jnp.sum(gs.astype(F32) * z.mixT[s, hr, :].astype(F32), 0, keepdims=True)
        for qb in range(z.nb):
            nk = BLK * (qb + 1)
            off = BLK * (qb * (qb + 1) // 2)
            sl = slice(qb * BLK, nk)
            gq = gs[:, sl]
            e = z.E[hi, off:off + nk, :]
            dp = dot(vh[:nk], gq)
            ds = (e.astype(F32) * (dp - delta[:, sl])).astype(BF16)
            z.dT[s, pl.ds(pl.multiple_of(h * HD, HD), HD), sl] = (dot(z.kT[s, hr, 0:nk], ds) * 0.125).astype(BF16)
            dv = dot(gq, e, NT)
            dk = dot(z.qT[s, hr, sl], ds, NT)
            if qb:
                z.dva[:, 0:nk - BLK] = z.dva[:, 0:nk - BLK] + dv[:, 0:nk - BLK]
                z.dka[:, 0:nk - BLK] = z.dka[:, 0:nk - BLK] + dk[:, 0:nk - BLK]
            z.dva[:, sl] = dv[:, nk - BLK:nk]
            z.dka[:, sl] = dk[:, nk - BLK:nk]
        z.dT[s, pl.ds(pl.multiple_of(256 + h * HD, HD), HD), :] = (z.dka[...] * LN2).astype(BF16)
        z.dT[s, pl.ds(pl.multiple_of(512 + h * HD, HD), HD), :] = z.dva[...].astype(BF16)
        if hook is not None:
            hook(h)
        return c
    lax.fori_loop(0, z.nh, body, 0)


def d_head(z, s):
    for j in range(3):
        z.GH[s, j] = dot(z.n1T[...], z.dT[s, j * 256:(j + 1) * 256, :], NT).astype(BF16)
    for i, j in enumerate((0, 2)):
        z.small[6 + s:7 + s, i * 256:(i + 1) * 256] = rowsum(z.dT[s, j * 256:(j + 1) * 256, :])


def grad_in(z):
    zero = jnp.zeros((1, z.ns.shape[-1]), F32)
    sc, sh = zero, zero
    for r in range(z.nb):
        sl = slice(r * BLK, (r + 1) * BLK)
        gT = 0.0
        for s in (0, 1):
            for j in range(3):
                gT = gT + dot(z.hw[s, j], z.dT[s, j * 256:(j + 1) * 256, sl])
        g = gT.T
        xh, rs = normed(z.x[sl, :].astype(F32))
        z.ig[sl, :] = (z.res[sl, :] + ln_back(g, xh, rs, z.ns[0:1, :])).astype(BF16)
        sc = sc + jnp.sum(g * xh, 0, keepdims=True)
        sh = sh + jnp.sum(g, 0, keepdims=True)
    z.small[0:1, :] = sc
    z.small[2:3, :] = sh


def scratch(T):
    nb = T // BLK
    V = pltpu.VMEM
    return dict(
        n1T=V((512, T), BF16), qT=V((2, 256, T), BF16), kT=V((2, 256, T), BF16), vT=V((2, 4, 80, T), BF16),
        E=V((8, BLK * nb * (nb + 1) // 2, BLK), BF16), rl=V((8, 1, T), F32), mixT=V((2, 256, T), BF16),
        res=V((T, 512), F32), n2=V((T, 512), BF16), act=V((2, T, 1024), BF16), dpre=V((2, T, 1024), BF16),
        oacc=V((T, 512), F32), g2=V((T, 512), F32), br=V((T, 512), BF16), gmT=V((2, 256, T), BF16),
        dT=V((2, 768, T), BF16), dva=V((64, T), F32), dka=V((64, T), F32))


INS = ["x", "cot", "ns", "nsh", "hw", "qb", "vb", "ow", "ob", "uw", "ub", "dw", "db"]
OUTS = ["lo", "ig", "GH", "GO", "GU", "GD", "small"]


def run_all(z):
    ln1(z)
    for s in (0, 1):
        qkv(z, s)
        attn_fwd(z, s)
    out_proj(z)
    ffn(z, 0, True, False)
    d_down(z, 0)
    d_up(z, 0)
    ffn(z, 1, False, True)
    d_down(z, 1)
    d_up(z, 1)
    d_out(z)
    attn_bwd(z, 0)
    attn_bwd(z, 1)
    d_head(z, 0)
    d_head(z, 1)
    grad_in(z)


def call(args, T, phases=None):
    scr = scratch(T)
    names = list(scr)

    def kernel(*refs):
        z = Refs()
        for n, r in zip(INS + OUTS + names, refs):
            setattr(z, n, r)
        z.nb, z.nh = T // BLK, 4
        (phases or run_all)(z)

    S = jax.ShapeDtypeStruct
    outs = [S((T, 512), BF16), S((T, 512), BF16), S((2, 3, 512, 256), BF16), S((2, 256, 512), BF16),
            S((2, 512, 1024), BF16), S((2, 1024, 512), BF16), S((16, 512), F32)]
    vm = pl.BlockSpec(memory_space=pltpu.VMEM)
    return pl.pallas_call(kernel, out_shape=outs, in_specs=[vm] * len(INS), out_specs=[vm] * len(OUTS),
                          scratch_shapes=list(scr.values()),
                          compiler_params=pltpu.CompilerParams(vmem_limit_bytes=67043328))(*args)


def local(inputs, norm_scale, norm_shift, head_weight, query_bias, value_bias, out_weight, out_bias,
          up_weight, up_bias, down_weight, down_bias, cotangent):
    T = inputs.shape[0]
    gather = lambda w: lax.all_gather(w, "tensor", axis=0)
    row = lambda b: b.reshape(b.shape[:-1] + (1, b.shape[-1]))
    args = (inputs, cotangent, norm_scale, norm_shift, gather(head_weight), row(gather(query_bias)), row(gather(value_bias)),
            gather(out_weight), row(out_bias), gather(up_weight), row(gather(up_bias)), gather(down_weight), row(down_bias))
    lo, ig, GH, GO, GU, GD, sm = call(args, T)
    scat = lambda g: lax.psum_scatter(g.astype(F32), "tensor", scatter_dimension=0)
    big = lax.psum(tuple(scat(g) for g in (GH, GO, GU, GD)), "dp")
    sm = lax.psum(sm, ("dp", "tensor"))
    t = lax.axis_index("tensor")
    qv = sm[6:8].reshape(2, 2, 256)[t]
    ub = sm[8:12].reshape(2, 1024)[t]
    return (lo, ig, sm[0:2], sm[2:4], big[0], qv[0], qv[1], big[1], sm[4], big[2], ub, big[3], sm[5])


def solution(mesh):
    P = jax.sharding.PartitionSpec
    in_specs = (P(("dp", "tensor"), None), P(), P(), P(None, None, "tensor"), P("tensor"), P("tensor"), P("tensor", None),
                P(), P(None, "tensor"), P("tensor"), P("tensor", None), P(), P(("dp", "tensor"), None))
    out_specs = (P(("dp", "tensor"), None), P(("dp", "tensor"), None), P(), P(), P(None, None, "tensor"), P("tensor"),
                 P("tensor"), P("tensor", None), P(), P(None, "tensor"), P("tensor"), P("tensor", None), P())
    return jax.shard_map(local, mesh=mesh, in_specs=in_specs, out_specs=out_specs, check_vma=False)
```

time: 522 us -> 520 us (level); the launches traced: 513 us -> 519 us
  matrix products: 98.7 us -> 0 us
  waiting for transfers between devices: 263 us -> 348 us
  Pallas kernels: 0 us -> 64.5 us
  local copies, waits for them, and re-layouts: 35.3 us -> 13.5 us
  other arithmetic: 29.8 us -> 9.28 us
    dot_general x40 -> x0, matrix products: 91.8 us -> none  [the longest x1 10.3 us: local(): gpre = gelu_pull(dot('td,fd->tf', cotangent, dw))[0].astype(BF16)]
    pallas_call x0 -> x1, Pallas kernels: none -> 64.5 us  [call(): pl.pallas_call(kernel, out_shape=outs, in_specs=[vm] * len(INS), out_spec...]
    all_gather x3, waiting for transfers between devices: 25.3 us -> 76.9 us  [local(): gather = lambda w: lax.all_gather(w, 'tensor', axis=0)]
    unnamed x138 -> x26, local copies, waits for them, and re-layouts: 30.2 us -> 11.1 us
    reduce_scatter x4, waiting for transfers between devices: 152 us -> 169 us  [local(): lax.psum_scatter(g.astype(F32), 'tensor', scatter_dimension=0)]
    psum x1, waiting for transfers between devices: 83.6 us -> 100 us  [local(): big = lax.psum(tuple((scat(g) for g in (GH, GO, GU, GD))), 'dp')]
    reduce_sum x9 -> x0, other arithmetic: 8.87 us -> none  [the longest x2 3.26 us: layer_norm(): return centered * lax.rsqrt(spread + EPSILON) * gain + shift]
    sub x2 -> x0, other arithmetic: 7.05 us -> none  [local(): e = jnp.exp(s - jnp.max(s, -1, keepdims=True))]
  transfers between devices with their start and end apart: 8 -> 8, of which waited for: 6 -> 8; matrix products, arithmetic and copies ran while one was open for 17% -> 2% of each run, Pallas kernels for 0% -> 0%
where the time goes in v2:
time: 520 us; the launch traced here: 519 us
  waiting for transfers between devices  348 us (67%)
  blocking collectives  69.1 us (13%)
  Pallas kernels  64.5 us (12%)
  between operations  14.2 us (3%)
  local copies, waits for them, and re-layouts  13.5 us (3%)
  other arithmetic  9.28 us (2%)
    reduce_scatter x4, waiting for transfers between devices, local(): lax.psum_scatter(g.astype(F32), 'tensor', scatter_dimension=0)  169 us
    psum x1, waiting for transfers between devices, local(): big = lax.psum(tuple((scat(g) for g in (GH, GO, GU, GD))), 'dp')  100 us
    all_gather x3, waiting for transfers between devices, local(): gather = lambda w: lax.all_gather(w, 'tensor', axis=0)  76.9 us
    pallas_call x1, Pallas kernels, call(): pl.pallas_call(kernel, out_shape=outs, in_specs=[vm] * len(INS), out_spec...  64.5 us
    psum x1, blocking collectives, local(): sm = lax.psum(sm, ('dp', 'tensor'))  41 us
    all_gather x4, blocking collectives, local(): gather = lambda w: lax.all_gather(w, 'tensor', axis=0)  28.1 us
    unnamed x26, local copies, waits for them, and re-layouts  11.1 us
  transfers between devices with their start and end apart: 8, of which 8 were waited for; matrix products, arithmetic and copies ran while one was open for 2% of the time, Pallas kernels for 0%

profile of v2, /device:TPU:0, one launch (start us, length us, event | category | flops | bytes accessed | tf_op | source)
XLA Modules:
  0.0 519.3 jit_solution(10849492874055809800)
XLA Ops:
  7.3 0.7 all-gather.13.cloned.1.call-update
  8.0 0.7 all-gather.15.cloned.1.call-update
  8.7 0.7 all-gather.17.cloned.1.call-update
  9.5 5.3 %all-gather.7.refs_5_ = f32[2,1,256]{2,1,0:T(1,128)} all-gather(f32[1,1,256]{2,1,0:T(1,128)S(1)} %bitcast.32), channel_id=3, replica_groups=mesh['dp'=16,'tensor'=2] {'tensor'}, dimensions={0}, use_global_device_ids=true | all-gather | bytes 3072 | tf_op jit(solution)/shard_map/all_gather | solution.py:284
  14.8 4.3 all-gather.8.refs_6_
  19.1 4.5 all-gather.5
  23.6 14.1 %all-gather.3 = bf16[512,512]{1,0:T(8,128)(2,1)} all-gather(bf16[256,512]{1,0:T(8,128)(2,1)S(1)} %copy-done.6), channel_id=5, replica_groups=mesh['dp'=16,'tensor'=2] {'tensor'}, dimensions={0}, use_global_device_ids=true | all-gather | bytes 786432 | tf_op jit(solution)/shard_map/all_gather | solution.py:284
  37.7 7.5 %all-gather.13.cloned.1.call-done = bf16[6,512,256]{2,1,0:T(8,128)(2,1)} async-done(((bf16[3,512,256]{2,1,0:T(8,128)(2,1)}), bf16[6,512,256]{2,1,0:T(8,128)(2,1)}) %all-gather.13.cloned.1.call-update) | async-done | bytes 1572880 | tf_op jit(solution)/shard_map/all_gather | solution.py:284
  45.2 34.7 %all-gather.15.cloned.1.call-done = bf16[1024,1024]{1,0:T(8,128)(2,1)} async-done(((bf16[512,1024]{1,0:T(8,128)(2,1)}), bf16[1024,1024]{1,0:T(8,128)(2,1)}) %all-gather.15.cloned.1.call-update) | async-done | bytes 2097168 | tf_op jit(solution)/shard_map/all_gather | solution.py:284
  79.8 34.7 %all-gather.17.cloned.1.call-done = bf16[2048,512]{1,0:T(8,128)(2,1)} async-done(((bf16[1024,512]{1,0:T(8,128)(2,1)}), bf16[2048,512]{1,0:T(8,128)(2,1)}) %all-gather.17.cloned.1.call-update) | async-done | bytes 2097168 | tf_op jit(solution)/shard_map/all_gather | solution.py:284
  114.5 64.5 %shard_map.228 = (bf16[1024,512]{1,0:T(8,128)(2,1)}, bf16[1024,512]{1,0:T(8,128)(2,1)}, bf16[2,3,512,256]{3,2,1,0:T(8,128)(2,1)}, bf16[2,256,512]{2,1,0:T(8,128)...) custom-call(bf16[1024,512]{1,0:T(8,128)(2,1)} %refs_0_.1, ...), custom_call_target="tpu_custom_call" | custom-call | tf_op jit(solution)/shard_map/pallas_call | solution.py:276
  179.1 2.3 convert_element_type.13
  181.5 2.0 convert_element_type.12
  183.5 1.5 copy-done.1
  185.0 2.4 convert_element_type.14
  187.5 1.5 copy-done
  189.0 2.6 convert_element_type.15
  191.7 10.2 %reduce-scatter.7.cloned.1.call-done = f32[1,256,512]{2,1,0:T(8,128)} async-done(((f32[2,256,512]{2,1,0:T(8,128)}), f32[1,256,512]{2,1,0:T(8,128)}) %reduce-scatter.7.cloned.1.call-update) | async-done | bytes 524304 | tf_op jit(solution)/shard_map/reduce_scatter | solution.py:289
  201.9 45.6 %reduce-scatter.5.cloned.1.call-done = f32[1,3,512,256]{3,2,1,0:T(8,128)} async-done(((f32[2,3,512,256]{3,2,1,0:T(8,128)}), f32[1,3,512,256]{3,2,1,0:T(8,128)}) %reduce-scatter.5.cloned.1.call-update) | async-done | bytes 1572880 | tf_op jit(solution)/shard_map/reduce_scatter | solution.py:289
  247.5 56.6 %reduce-scatter.9.cloned.1.call-done = f32[1,512,1024]{2,1,0:T(8,128)} async-done(((f32[2,512,1024]{2,1,0:T(8,128)}), f32[1,512,1024]{2,1,0:T(8,128)}) %reduce-scatter.9.cloned.1.call-update) | async-done | bytes 2097168 | tf_op jit(solution)/shard_map/reduce_scatter | solution.py:289
  304.0 56.7 %reduce-scatter.11.cloned.1.call-done = f32[1,1024,512]{2,1,0:T(8,128)} async-done(((f32[2,1024,512]{2,1,0:T(8,128)}), f32[1,1024,512]{2,1,0:T(8,128)}) %reduce-scatter.11.cloned.1.call-update) | async-done | bytes 2097168 | tf_op jit(solution)/shard_map/reduce_scatter | solution.py:289
  360.8 0.7 copy-done.7
  361.5 41.0 %psum.35 = f32[16,512]{1,0:T(8,128)S(1)} all-reduce(f32[16,512]{1,0:T(8,128)S(1)} %copy-done.7), channel_id=1, replica_groups=mesh['dp'=16,'tensor'=2] {'dp','tensor'}, use_global_device_ids=true, to_apply=%region_0.0 | all-reduce | flops 8192 | bytes 65536 | tf_op jit(solution)/shard_map/psum | solution.py:291
  402.5 0.6 fusion.1
  403.7 0.6 constant_dynamic-slice_fusion.1
  404.3 0.6 fusion
  404.9 100.2 %all-reduce.3.cloned.1.call-done = (f32[3,512,256]{2,1,0:T(8,128)}, f32[256,512]{1,0:T(8,128)}, f32[512,1024]{1,0:T(8,128)}, f32[1024,512]{1,0:T(8,128)}) async-done(((f32[3,512,256]{2,1,0:T(8,128)}, f32[256,512]{1,0:T(8,128)}, f32[512,1024]{1,0:T(8,128)}, f32[1024,512]{1,0:T(8,128)}), (f32[3,512,256]{2,1,0:T(8,128)}, f32[256,512]{1,0:T(8,128)}, f32[512,1024]{1,0:T(8,128)}, ...) | async-done | bytes 6291472 | tf_op jit(solution)/shard_map/psum | solution.py:290
  505.1 2.8 copy.30
  507.9 0.8 copy.31
  508.7 1.3 copy.32
  510.1 1.0 copy-done.2
  511.1 1.3 copy.33
  (35 shorter events, 1.0 us)
Async XLA Ops:
  7.2 2.3 copy-start.9
  7.2 7.6 %copy-start.10 = (f32[256]{0:T(256)S(1)}, f32[256]{0:T(256)}, u32[]{:S(2)}) copy-start(f32[256]{0:T(256)} %param.18) | copy-start | bytes 3076
  7.2 11.9 %copy-start.8 = (f32[1024]{0:T(1024)S(1)}, f32[1024]{0:T(1024)}, u32[]{:S(2)}) copy-start(f32[1024]{0:T(1024)} %param.22) | copy-start | bytes 12292
  7.2 16.4 %copy-start.6 = (bf16[256,512]{1,0:T(8,128)(2,1)S(1)}, bf16[256,512]{1,0:T(8,128)(2,1)}, u32[]{:S(2)}) copy-start(bf16[256,512]{1,0:T(8,128)(2,1)} %param.19) | copy-start | bytes 786436
  7.2 38.0 %all-gather.13.cloned.1.call-start = ((), (), s32[]{:S(2)}) async-start(), calls=%async_computation.8 | async-start | bytes 2359296 | tf_op jit(solution)/shard_map/all_gather | solution.py:284
  8.0 71.9 %all-gather.15.cloned.1.call-start = ((), (), s32[]{:S(2)}) async-start(), calls=%async_computation.9 | async-start | bytes 3145728 | tf_op jit(solution)/shard_map/all_gather | solution.py:284
  8.7 105.8 %all-gather.17.cloned.1.call-start = ((), (), s32[]{:S(2)}) async-start(), calls=%async_computation.10 | async-start | bytes 3145728 | tf_op jit(solution)/shard_map/all_gather | solution.py:284
  9.4 192.5 %reduce-scatter.7.cloned.1.call-start = ((), (), s32[]{:S(2)}) async-start(), calls=%async_computation.5 | async-start | bytes 1572864 | tf_op jit(solution)/shard_map/reduce_scatter | solution.py:289
  179.1 2.4 copy-start.4
  181.4 66.1 %reduce-scatter.5.cloned.1.call-start = ((), (), s32[]{:S(2)}) async-start(), calls=%async_computation.4 | async-start | bytes 4718592 | tf_op jit(solution)/shard_map/reduce_scatter | solution.py:289
  183.4 1.6 copy-start.1
  183.5 120.6 %reduce-scatter.9.cloned.1.call-start = ((), (), s32[]{:S(2)}) async-start(), calls=%async_computation.6 | async-start | bytes 6291456 | tf_op jit(solution)/shard_map/reduce_scatter | solution.py:289
  187.4 1.6 copy-start
  187.5 173.3 %reduce-scatter.11.cloned.1.call-start = ((), (), s32[]{:S(2)}) async-start(), calls=%async_computation.7 | async-start | bytes 6291456 | tf_op jit(solution)/shard_map/reduce_scatter | solution.py:289
  191.7 313.5 %all-reduce.3.cloned.1.call-start = ((), (), s32[]{:S(2)}) async-start(), calls=%async_computation.11 | async-start | bytes 12582912 | tf_op jit(solution)/shard_map/psum | solution.py:290
  360.8 0.8 copy-start.7
  505.1 2.8 copy-start.5
  505.1 3.6 copy-start.3
  508.7 2.3 copy-start.2
Sparse Core Ops, SparseCore 0:
  9.6 35.5 all-gather.12
  46.7 33.0 all-gather.14
  81.4 33.0 all-gather.16
  181.5 20.3 reduce-scatter.6
  204.0 43.4 reduce-scatter.4
  249.6 54.3 reduce-scatter.8
  306.3 54.3 reduce-scatter.10
  364.7 140.3 all-reduce.2

commit v3 on v2

v3 whole, which is shorter than its diff:
```python
import jax
import jax.numpy as jnp
from jax import lax
from jax.experimental import pallas as pl
from jax.experimental.pallas import tpu as pltpu
from jax.sharding import PartitionSpec as P

F32, BF16 = jnp.float32, jnp.bfloat16
NN, NT, TN = ((1,), (0,)), ((1,), (1,)), ((0,), (0,))
EPS = 1e-5
LOG2E = 1.4426950408889634
LN2 = 0.6931471805599453
C0, C1 = 0.7978845608, 0.044715
HD, BLK, D, HALF, FH, NH = 64, 256, 512, 256, 1024, 4
MESH = pl.DeviceIdType.MESH
VMEM_BYTES = 67043328


def dot(a, b, dims=NN):
    return lax.dot_general(a, b, (dims, ((), ())), preferred_element_type=F32)


def normed(v):
    c = jnp.mean(v, -1, keepdims=True)
    d = v - c
    r = lax.rsqrt(jnp.mean(d * d, -1, keepdims=True) + EPS)
    return d * r, r


def ln_back(g, xhat, r, gain):
    gx = g * gain
    return r * (gx - jnp.mean(gx, -1, keepdims=True) - xhat * jnp.mean(gx * xhat, -1, keepdims=True))


def rows_of(r):
    return pl.ds(pl.multiple_of(r * BLK, BLK), BLK)


def column(row):
    return jnp.broadcast_to(row, (8, row.shape[-1])).T[:, 0:1]


class Refs:
    pass


def ln1(z):
    def body(r, c):
        xh, _ = normed(z.x[rows_of(r), :].astype(F32))
        n = (xh * z.ns[0:1, :] + z.nsh[0:1, :]).astype(BF16)
        z.n1T[:, rows_of(r)] = n.T
        return c

    lax.fori_loop(0, z.nb, body, 0)


def qkv(z, s):
    qb, vb = column(z.qb[s][...]), column(z.vb[s][...])
    for b in range(z.nb):
        sl = slice(b * BLK, (b + 1) * BLK)
        nt = z.n1T[:, sl]
        q = dot(z.hw[s, 0], nt, TN) + qb
        z.qT[s, :, sl] = (q * (LOG2E / 8.0)).astype(BF16)
        z.kT[s, :, sl] = dot(z.hw[s, 1], nt, TN).astype(BF16)
        v = (dot(z.hw[s, 2], nt, TN) + vb).astype(BF16)
        for h in range(NH):
            z.vT[s, h, 0:HD, sl] = v[h * HD : (h + 1) * HD]
            z.vT[s, h, HD : HD + 16, sl] = jnp.ones((16, BLK), BF16)


def attn_fwd(z, s, hook):
    def body(h, c):
        hr = pl.ds(pl.multiple_of(h * HD, HD), HD)
        kh = z.kT[s, hr, :].T
        for b in range(z.nb):
            nk = BLK * (b + 1)
            off = BLK * (b * (b + 1) // 2)
            sl = slice(b * BLK, nk)
            sc = dot(kh[:nk], z.qT[s, hr, sl])
            m = jnp.max(sc, 0, keepdims=True)
            e = jnp.exp2(sc - m).astype(BF16)
            z.E[s * NH + h, off : off + nk, :] = e
            o = dot(z.vT[s, h, :, 0:nk], e)
            rl = 1.0 / o[HD : HD + 1]
            z.rl[s * NH + h, 0:1, sl] = rl
            z.mixT[s, hr, sl] = (o[0:HD] * rl).astype(BF16)
        hook(h)
        return c

    lax.fori_loop(0, NH, body, 0)


def out_proj(z):
    for r in range(z.nb):
        sl = slice(r * BLK, (r + 1) * BLK)
        t = dot(z.mixT[0, :, sl], z.ow[0], TN) + dot(z.mixT[1, :, sl], z.ow[1], TN)
        res = z.x[sl, :].astype(F32) + (t + z.ob[...])
        z.res[sl, :] = res
        z.oacc[sl, :] = res + z.db[...]
        xh, _ = normed(res)
        z.n2[sl, :] = (xh * z.ns[1:2, :] + z.nsh[1:2, :]).astype(BF16)


def ffn(z, s, last, hook):
    def body(r, c):
        rr = rows_of(r)
        n2 = z.n2[rr, :]
        ct = z.cot[rr, :]
        for f in range(0, FH, 512):
            fs = slice(f, f + 512)
            u = dot(n2, z.uw[s, :, fs]) + z.ub[s][:, fs]
            da = dot(ct, z.dw[s, fs, :], NT)
            u2 = u * u
            t = jnp.tanh(u * (C0 + (C0 * C1) * u2))
            hp = 0.5 + 0.5 * t
            z.act[s, rr, fs] = (u * hp).astype(BF16)
            gp = hp + (u * (0.5 - 0.5 * t * t)) * (C0 + (3 * C0 * C1) * u2)
            z.dpre[s, rr, fs] = (da * gp).astype(BF16)
        g = dot(z.dpre[s, rr, :], z.uw[s], NT)
        if not last:
            z.g2[rr, :] = g
        else:
            g2 = z.g2[rr, :] + g
            xh, rs = normed(z.res[rr, :])
            gres = ct.astype(F32) + ln_back(g2, xh, rs, z.ns[1:2, :])
            br = gres.astype(BF16)
            z.res[rr, :] = gres
            z.br[rr, :] = br
            c = (
                c[0] + jnp.sum(g2 * xh, 0, keepdims=True),
                c[1] + jnp.sum(g2, 0, keepdims=True),
                c[2] + jnp.sum(br.astype(F32), 0, keepdims=True),
                c[3] + jnp.sum(ct.astype(F32), 0, keepdims=True),
            )
        hook(r)
        return c

    zero = jnp.zeros((1, D), F32)
    c = lax.fori_loop(0, z.nb, body, (zero,) * 4 if last else 0)
    if last:
        z.sm[1:2, :] = c[0]
        z.sm[3:4, :] = c[1]
        z.sm[4:5, :] = c[2]
        z.sm[5:6, :] = c[3]


def ffn_out(z):
    for r in range(z.nb):
        rr = slice(r * BLK, (r + 1) * BLK)
        o = dot(z.act[0, rr, :], z.dw[0]) + dot(z.act[1, rr, :], z.dw[1])
        z.lo[rr, :] = (z.oacc[rr, :] + o).astype(BF16)


def d_down(z, s, part):
    n = FH // 2
    for f in range(0, n, 256):
        a = part * n + f
        z.GD[part][s][f : f + 256, :] = dot(z.act[s, :, a : a + 256], z.cot[...], TN).astype(BF16)


def d_up(z, s, part):
    n = D // 2
    w = z.n2[:, part * n : (part + 1) * n]
    for f in range(0, FH, 512):
        z.GU[part][s][:, f : f + 512] = dot(w, z.dpre[s, :, f : f + 512], TN).astype(BF16)


def d_upb(z, s):
    ones = jnp.ones((8, z.dpre.shape[1]), BF16)
    for i in range(FH // 512):
        row = 9 + 8 * s + i
        z.sm[row : row + 1, :] = dot(ones, z.dpre[s, :, i * 512 : (i + 1) * 512])[0:1]


def d_out(z, s):
    z.GO[s][...] = dot(z.mixT[s], z.br[...]).astype(BF16)


def grad_mixed(z, s):
    for r in range(z.nb):
        sl = slice(r * BLK, (r + 1) * BLK)
        z.gmT[s, :, sl] = dot(z.ow[s], z.br[sl, :], NT).astype(BF16)


def attn_bwd(z, s, hook):
    def body(h, c):
        hr = pl.ds(pl.multiple_of(h * HD, HD), HD)
        hi = s * NH + h
        vh = z.vT[s, h, 0:HD, :].T
        gs = (z.gmT[s, hr, :].astype(F32) * z.rl[hi]).astype(BF16)
        delta = jnp.sum(gs.astype(F32) * z.mixT[s, hr, :].astype(F32), 0, keepdims=True)
        for b in range(z.nb):
            nk = BLK * (b + 1)
            off = BLK * (b * (b + 1) // 2)
            sl = slice(b * BLK, nk)
            gq = gs[:, sl]
            e = z.E[hi, off : off + nk, :]
            dp = dot(vh[:nk], gq)
            ds = (e.astype(F32) * (dp - delta[:, sl])).astype(BF16)
            z.dh[0:HD, sl] = (dot(z.kT[s, hr, 0:nk], ds) * 0.125).astype(BF16)
            dv = dot(gq, e, NT)
            dk = dot(z.qT[s, hr, sl], ds, NT)
            if b:
                z.dva[:, 0 : nk - BLK] = z.dva[:, 0 : nk - BLK] + dv[:, 0 : nk - BLK]
                z.dka[:, 0 : nk - BLK] = z.dka[:, 0 : nk - BLK] + dk[:, 0 : nk - BLK]
            z.dva[:, sl] = dv[:, nk - BLK : nk]
            z.dka[:, sl] = dk[:, nk - BLK : nk]
        z.dh[HD : 2 * HD, :] = (z.dka[...] * LN2).astype(BF16)
        z.dh[2 * HD : 3 * HD, :] = z.dva[...].astype(BF16)
        for j in range(3):
            z.dT[s, pl.ds(pl.multiple_of(j * HALF + h * HD, HD), HD), :] = z.dh[j * HD : (j + 1) * HD, :]
        g = dot(z.dh[...], z.n1T[...], NT).astype(BF16)
        for q in range(4):
            z.GH[s][h, q * 192 : (q + 1) * 192, :] = g[:, q * 128 : (q + 1) * 128]
        hook(h)
        return c

    lax.fori_loop(0, NH, body, 0)


def d_headb(z, s):
    ones = jnp.ones((8, z.dT.shape[2]), BF16)
    for i, j in enumerate((0, 2)):
        row = 8 + 8 * s
        z.sm[row : row + 1, i * HALF : (i + 1) * HALF] = dot(ones, z.dT[s, j * HALF : (j + 1) * HALF, :], NT)[0:1]


def grad_in(z):
    zero = jnp.zeros((1, D), F32)
    sc, sh = zero, zero
    for r in range(z.nb):
        sl = slice(r * BLK, (r + 1) * BLK)
        g = 0.0
        for s in (0, 1):
            for j in range(3):
                g = g + dot(z.hw[s, j], z.dT[s, j * HALF : (j + 1) * HALF, sl])
        g = g.T
        xh, rs = normed(z.x[sl, :].astype(F32))
        z.ig[sl, :] = (z.res[sl, :] + ln_back(g, xh, rs, z.ns[0:1, :])).astype(BF16)
        sc = sc + jnp.sum(g * xh, 0, keepdims=True)
        sh = sh + jnp.sum(g, 0, keepdims=True)
    z.sm[0:1, :] = sc
    z.sm[2:3, :] = sh


class Comm:
    def __init__(self, ndp, send, recv, local):
        self.send, self.recv, self.local = send, recv, local
        self.count, self.local_count, self.pending = 0, 0, []
        me = lax.axis_index("dp")
        self.levels = [1 << i for i in range(ndp.bit_length() - 1)]
        self.bit = {b: (me // b) % 2 for b in self.levels}
        self.dp = {b: me + b - 2 * b * self.bit[b] for b in self.levels}
        self.peer = 1 - lax.axis_index("tensor")

    def where(self, axis):
        return {"tensor": self.peer} if axis == "t" else {"dp": self.dp[axis]}

    def barrier_signal(self):
        sem = pltpu.get_barrier_semaphore()
        for axis in ["t"] + self.levels:
            pl.semaphore_signal(sem, inc=1, device_id=self.where(axis), device_id_type=MESH)

    def barrier_wait(self):
        pl.semaphore_wait(pltpu.get_barrier_semaphore(), 1 + len(self.levels))

    def copy(self, src, dst, axis, keep=True):
        i = self.count
        self.count += 1

        def make():
            return pltpu.make_async_remote_copy(
                src_ref=src(), dst_ref=dst(), send_sem=self.send.at[i], recv_sem=self.recv.at[i],
                device_id=self.where(axis), device_id_type=MESH)

        if keep:
            self.pending.append(make)
        return make

    def here(self, src, dst):
        i = self.local_count
        self.local_count += 1
        return lambda: pltpu.make_async_copy(src(), dst(), self.local.at[i])

    def drain(self):
        for make in self.pending:
            make().wait_send()


def add_rows(dst, src, at, n, cols):
    ch = next(c for c in (384, 256, 192, 128, 96, 64, 48, 32, 16, 8, 4) if n % c == 0 and c * cols <= 49152)

    def body(i, c):
        o = pl.ds(pl.multiple_of(at + i * ch, ch), ch)
        v = dst[o, :].astype(F32) + src[pl.ds(pl.multiple_of(i * ch, ch), ch), :].astype(F32)
        dst[o, :] = v.astype(dst.dtype)
        return c

    lax.fori_loop(0, n // ch, body, 0)


def job_scratch(rows, cols, pre, extra):
    V = pltpu.VMEM
    own = [V((rows >> (k + 1), cols), BF16) for k in range(4)]
    peer = [V((rows >> (k + 1), cols), BF16) for k in range(pre)]
    return own + peer + [V((rows >> pre, cols), BF16)] + [V((rows >> 4, cols), BF16) for _ in range(extra)] + [V((rows, cols), BF16)]


class Job:
    def __init__(self, c, own, peer, refs, rows, cols, pre, out):
        lv = c.levels
        extra = len(lv) - 4
        r_own, r_peer, r_t, r_x, full = refs[:4], refs[4 : 4 + pre], refs[4 + pre], refs[5 + pre : 5 + pre + extra], refs[-1]
        lo = [0]
        for k in range(4):
            lo.append(lo[k] + c.bit[lv[k]] * (rows >> (k + 1)))
        n = [rows >> k for k in range(5)]
        at = lambda k: pl.ds(pl.multiple_of(lo[k], n[k]) if k else 0, n[k])
        away = lambda k: pl.ds(pl.multiple_of(lo[k] + (1 - c.bit[lv[k]]) * n[k + 1], n[k + 1]), n[k + 1])
        half = lambda g, buf, k: c.copy(lambda: g().at[away(k)], lambda: buf, lv[k])
        s_own = [half(own, r_own[k], k) for k in range(4)]
        s_peer = [half(peer, r_peer[k], k) for k in range(pre)]
        s_t = c.copy(lambda: peer().at[at(pre)], lambda: r_t, "t")
        s_x = [c.copy(lambda: own().at[at(4)], lambda i=i: r_x[i], lv[4 + i], False) for i in range(extra)]
        s_g = [c.copy(lambda k=k: full.at[at(k + 1)], lambda k=k: full.at[at(k + 1)], lv[k]) for k in range(4)]
        s_out = c.here(lambda: full, lambda: out())
        self.wait_out = lambda: s_out().wait()

        def end(s, g, buf, k):
            s[k]().wait_recv()
            add_rows(g(), buf[k], lo[k + 1], n[k + 1], cols)

        def peer_step(i):
            if i:
                end(s_peer, peer, r_peer, i - 1)
            (s_peer[i] if i < pre else s_t)().start()

        def own_step(i):
            if i == 0:
                s_own[0]().start()
            elif i <= 4:
                end(s_own, own, r_own, i - 1)
                if i == pre:
                    s_t().wait_recv()
                    add_rows(own(), r_t, lo[pre], n[pre], cols)
                if i < 4:
                    s_own[i]().start()
                    return
                for j in range(extra):
                    s_x[j]().start()
                    s_x[j]().wait()
                    add_rows(own(), r_x[j], lo[4], n[4], cols)
                full[at(4), :] = own()[at(4), :]
                s_g[3]().start()
            else:
                k = 8 - i
                s_g[k]().wait_recv()
                if k:
                    s_g[k - 1]().start()
                else:
                    s_out().start()

        self.peer_steps = [lambda i=i: peer_step(i) for i in range(pre + 1)]
        self.own_steps = [lambda i=i: own_step(i) for i in range(9)]

    def own(self, m=1):
        for _ in range(m):
            self.own_steps.pop(0)()

    def peer(self, m=1):
        for _ in range(m):
            self.peer_steps.pop(0)()


class Small:
    def __init__(self, c, sm, bufs):
        s_a = c.copy(lambda: sm.at[0:8], lambda: bufs[0].at[0:8], "t", False)
        s_b = c.copy(lambda: sm.at[16:24], lambda: bufs[0].at[8:16], "t", False)
        s_l = [c.copy(lambda: sm.at[0:16], lambda i=i: bufs[i + 1], b, False) for i, b in enumerate(c.levels)]

        def step(i):
            if i == 0:
                s_a().start()
                s_b().start()
                return
            for s in (s_a, s_b) if i == 1 else (s_l[i - 2],):
                s().wait()
            sm[0:16, :] = sm[0:16, :] + bufs[i - 1][...]
            if i <= len(s_l):
                s_l[i - 1]().start()

        self.steps = [lambda i=i: step(i) for i in range(len(c.levels) + 2)]

    def go(self, m=1):
        for _ in range(m):
            self.steps.pop(0)()


INS = ["x_h", "cot_h", "hw_h", "ow_h", "uw_h", "dw_h", "ns", "nsh", "qb_o", "vb_o", "ob", "ub_o", "db"]
OUTS = ["lo_h", "ig_h", "FH_h", "FO_h", "FU_h", "FD_h", "smo"]
JOBS = [("D0", FH // 2, D, 1), ("D1", FH // 2, D, 1), ("U0", D // 2, FH, 2), ("U1", D // 2, FH, 2), ("O", HALF, D, 1),
        ("H0", 1536, 128, 1), ("H1", 1536, 128, 1)]


def scratch(T, ndp):
    nb = T // BLK
    V = pltpu.VMEM
    lv = ndp.bit_length() - 1
    s = dict(
        x=V((T, D), BF16), cot=V((T, D), BF16), hw=V((2, 3, D, HALF), BF16), ow=V((2, HALF, D), BF16),
        uw=V((2, D, FH), BF16), dw=V((2, FH, D), BF16),
        qb_p=V((1, HALF), F32), vb_p=V((1, HALF), F32), ub_p=V((1, FH), F32),
        n1T=V((D, T), BF16), qT=V((2, HALF, T), BF16), kT=V((2, HALF, T), BF16), vT=V((2, NH, 80, T), BF16),
        E=V((2 * NH, BLK * nb * (nb + 1) // 2, BLK), BF16), rl=V((2 * NH, 1, T), F32), mixT=V((2, HALF, T), BF16),
        res=V((T, D), F32), n2=V((T, D), BF16), act=V((2, T, FH), BF16), dpre=V((2, T, FH), BF16),
        oacc=V((T, D), F32), g2=V((T, D), F32), br=V((T, D), BF16), gmT=V((2, HALF, T), BF16),
        dh=V((3 * HD, T), BF16), dva=V((HD, T), F32), dka=V((HD, T), F32), sm=V((24, D), F32),
        GD0o=V((FH // 2, D), BF16), GD0p=V((FH // 2, D), BF16), GD1o=V((FH // 2, D), BF16), GD1p=V((FH // 2, D), BF16),
        GU0o=V((D // 2, FH), BF16), GU0p=V((D // 2, FH), BF16), GU1o=V((D // 2, FH), BF16), GU1p=V((D // 2, FH), BF16),
        GOo=V((HALF, D), BF16), GOp=V((HALF, D), BF16), GHo=V((NH, 768, 128), BF16), GHp=V((NH, 768, 128), BF16),
        s0=V((16, D), F32))
    for i in range(lv):
        s[f"s{i + 1}"] = V((16, D), F32)
    for name, rows, cols, pre in JOBS:
        for i, v in enumerate(job_scratch(rows, cols, pre, lv - 4)):
            s[f"{name}_{i}"] = v
    s["send"] = pltpu.SemaphoreType.DMA((96 + 32 * (lv - 4),))
    s["recv"] = pltpu.SemaphoreType.DMA((96 + 32 * (lv - 4),))
    s["local"] = pltpu.SemaphoreType.DMA((24,))
    return s


def run(z, ndp):
    c = Comm(ndp, z.send, z.recv, z.local)
    lv = c.levels
    c.barrier_signal()
    loads = {n: c.here(lambda n=n: getattr(z, n + "_h"), lambda n=n, d=d: d(getattr(z, n)))
             for n, d in (("x", lambda r: r), ("hw", lambda r: r.at[0]), ("cot", lambda r: r), ("ow", lambda r: r.at[0]),
                          ("uw", lambda r: r.at[0]), ("dw", lambda r: r.at[0]))}
    for n in ("x", "hw", "ow", "cot", "uw", "dw"):
        loads[n]().start()
    b0 = c.bit[1]

    def part(n):
        m = {"hw": D, "ow": HALF, "uw": D, "dw": FH}[n] // 2
        return pl.ds(pl.multiple_of(b0 * m, m), m)

    def view(r, n, lead):
        r = r.at[lead] if lead is not None else r
        return r.at[:, part(n)] if n == "hw" else r.at[part(n)]

    w1 = {n: c.copy(lambda n=n: view(getattr(z, n + "_h"), n, None), lambda n=n: view(getattr(z, n), n, 1), "t")
          for n in ("hw", "ow", "uw", "dw")}
    w2 = {n: c.copy(lambda n=n: view(getattr(z, n), n, 1), lambda n=n: view(getattr(z, n), n, 1), 1)
          for n in ("hw", "ow", "uw", "dw")}
    wb = [c.copy(lambda n=n: getattr(z, n + "_o"), lambda n=n: getattr(z, n + "_p"), "t") for n in ("qb", "vb", "ub")]

    def relay(n):
        w1[n]().wait_recv()
        w2[n]().start()

    def arrive(n):
        w2[n]().wait_recv()

    c.barrier_wait()
    w1["hw"]().start()
    for b in wb:
        b().start()
    for n in ("ow", "uw", "dw"):
        w1[n]().start()

    z.qb, z.vb, z.ub = (z.qb_o, z.qb_p), (z.vb_o, z.vb_p), (z.ub_o, z.ub_p)
    z.GD = ((z.GD0o, z.GD0p), (z.GD1o, z.GD1p))
    z.GU = ((z.GU0o, z.GU0p), (z.GU1o, z.GU1p))
    z.GO, z.GH = (z.GOo, z.GOp), (z.GHo, z.GHp)
    z.dT, z.lo, z.ig = z.dpre, z.br, z.n2
    ends = dict(D0=lambda: z.FD_h.at[0 : FH // 2], D1=lambda: z.FD_h.at[FH // 2 : FH], U0=lambda: z.FU_h.at[0 : D // 2],
                U1=lambda: z.FU_h.at[D // 2 : D], O=lambda: z.FO_h, H0=lambda: z.FH_h.at[0], H1=lambda: z.FH_h.at[1])
    flat = lambda r, i: (lambda: r.at[2 * i : 2 * i + 2].reshape(1536, 128))
    srcs = dict(D0=(lambda: z.GD0o, lambda: z.GD0p), D1=(lambda: z.GD1o, lambda: z.GD1p), U0=(lambda: z.GU0o, lambda: z.GU0p),
                U1=(lambda: z.GU1o, lambda: z.GU1p), O=(lambda: z.GOo, lambda: z.GOp),
                H0=(flat(z.GHo, 0), flat(z.GHp, 0)), H1=(flat(z.GHo, 1), flat(z.GHp, 1)))
    jobs = {}
    for name, rows, cols, pre in JOBS:
        refs = [getattr(z, f"{name}_{i}") for i in range(4 + pre + 1 + len(lv) - 4 + 1)]
        jobs[name] = Job(c, *srcs[name], refs, rows, cols, pre, ends[name])
    small = Small(c, z.sm, [getattr(z, f"s{i}") for i in range(len(lv) + 1)])
    D0, D1, U0, U1, O, H0, H1 = (jobs[n] for n in ("D0", "D1", "U0", "U1", "O", "H0", "H1"))
    s_lo, s_ig = c.here(lambda: z.lo, lambda: z.lo_h), c.here(lambda: z.ig, lambda: z.ig_h)

    def at(table):
        def hook(h):
            for k, fns in table.items():
                @pl.when(h == k)
                def _():
                    for fn in fns:
                        fn()
        return hook

    none = at({})
    z.sm[...] = jnp.zeros_like(z.sm)
    loads["x"]().wait()
    ln1(z)
    loads["hw"]().wait()
    qkv(z, 0)
    attn_fwd(z, 0, none)
    relay("hw")
    for b in wb:
        b().wait_recv()
    arrive("hw")
    qkv(z, 1)
    attn_fwd(z, 1, at({1: [lambda: relay("ow")]}))
    arrive("ow")
    loads["ow"]().wait()
    out_proj(z)
    for n in ("cot", "uw", "dw"):
        loads[n]().wait()
    ffn(z, 0, False, at({2: [lambda: relay("uw")]}))
    for part_ in (0, 1):
        d_down(z, 0, part_)
        (D0, D1)[part_].own()
    for part_ in (0, 1):
        d_up(z, 0, part_)
        (U0, U1)[part_].own()
    d_upb(z, 0)
    relay("dw")
    arrive("uw")
    arrive("dw")
    ffn(z, 1, True, none)
    d_down(z, 1, 0)
    D0.peer()
    d_down(z, 1, 1)
    D1.peer()
    D0.peer()
    d_up(z, 1, 0)
    U0.peer()
    D1.peer()
    d_up(z, 1, 1)
    U1.peer()
    U0.own()
    U0.peer()
    d_upb(z, 1)
    d_out(z, 1)
    O.peer()
    d_out(z, 0)
    O.own()
    grad_mixed(z, 1)
    grad_mixed(z, 0)
    U1.own()
    U1.peer()
    O.peer()
    attn_bwd(z, 1, at({
        0: [lambda: D0.own()],
        1: [lambda: (U0.peer(), H0.peer())],
        2: [lambda: (D1.own(), D0.own(), H0.peer())],
        3: [lambda: (U1.peer(), O.own(), H1.peer())]}))
    attn_bwd(z, 0, at({
        0: [lambda: (D0.own(), D1.own(), U0.own(), H1.peer())],
        1: [lambda: (D0.own(), D1.own(), U0.own(), U1.own(), O.own(), H0.own())],
        2: [lambda: (D0.own(), D1.own(), U0.own(), U1.own(), O.own(), H0.own())],
        3: [lambda: (H1.own(), D0.own(), D1.own(), U0.own(), U1.own(), O.own(), H0.own())]}))
    d_headb(z, 0)
    d_headb(z, 1)
    H1.own()
    every = (H1, H0, O, U1, U0, D1, D0)

    def push():
        for j in every:
            if j.own_steps:
                j.own()

    push()
    grad_in(z)
    s_ig().start()
    small.go()
    push()
    ffn_out(z)
    s_lo().start()
    while any(j.own_steps for j in every) or small.steps:
        if small.steps:
            small.go()
        push()
    z.smo[...] = z.sm[0:16, :]
    s_ig().wait()
    s_lo().wait()
    for j in every:
        j.wait_out()
    c.drain()


def main_call(args, T, ndp):
    scr = scratch(T, ndp)
    names = INS + OUTS + list(scr)

    def kernel(*refs):
        z = Refs()
        for n, r in zip(names, refs):
            setattr(z, n, r)
        z.nb = T // BLK
        run(z, ndp)

    S = jax.ShapeDtypeStruct
    outs = [S((T, D), BF16), S((T, D), BF16), S((2, 1536, 128), BF16), S((HALF, D), BF16), S((D, FH), BF16), S((FH, D), BF16),
            S((16, D), F32)]
    vm, hbm = pl.BlockSpec(memory_space=pltpu.VMEM), pl.BlockSpec(memory_space=pl.ANY)
    return pl.pallas_call(
        kernel, out_shape=outs, in_specs=[hbm] * 6 + [vm] * 7, out_specs=[hbm] * 6 + [vm], scratch_shapes=list(scr.values()),
        compiler_params=pltpu.CompilerParams(vmem_limit_bytes=VMEM_BYTES, collective_id=0, has_side_effects=True),
        name="layer")(*args)


def widen(FH_, FO_, FU_, FD_):
    def kernel(h, o, u, d, ho, oo, uo, do):
        oo[...] = o[...].astype(F32)
        uo[...] = u[...].astype(F32)
        do[...] = d[...].astype(F32)
        for q in range(4):
            for j in range(3):
                for p in range(2):
                    rows = [h[p, i * 768 + q * 192 + j * HD : i * 768 + q * 192 + (j + 1) * HD, :] for i in range(2)]
                    t = jnp.concatenate(rows, 0).astype(F32).T
                    ho[j, q * 128 : (q + 1) * 128, p * 128 : (p + 1) * 128] = t

    S = jax.ShapeDtypeStruct
    vm = pl.BlockSpec(memory_space=pltpu.VMEM)
    return pl.pallas_call(
        kernel, out_shape=[S((3, D, HALF), F32), S((HALF, D), F32), S((D, FH), F32), S((FH, D), F32)],
        in_specs=[vm] * 4, out_specs=[vm] * 4, name="widen")(FH_, FO_, FU_, FD_)


def solution(mesh):
    ndp = mesh.shape["dp"]

    def local(inputs, norm_scale, norm_shift, head_weight, query_bias, value_bias, out_weight, out_bias, up_weight, up_bias,
              down_weight, down_bias, cotangent):
        row = lambda b: b.reshape(1, b.shape[0])
        args = (inputs, cotangent, head_weight, out_weight, up_weight, down_weight, norm_scale, norm_shift, row(query_bias),
                row(value_bias), row(out_bias), row(up_bias), row(down_bias))
        lo, ig, gh, go, gu, gd, sm = main_call(args, inputs.shape[0], ndp)
        gh, go, gu, gd = widen(gh, go, gu, gd)
        return (lo, ig, sm[0:2], sm[2:4], gh, sm[8, 0:HALF], sm[8, HALF:D], go, sm[4], gu, sm[9:11].reshape(FH), gd, sm[5])

    rows, t0, t1 = P(("dp", "tensor"), None), P("tensor"), P(None, "tensor")
    tc = P("tensor", None)
    in_specs = (rows, P(), P(), P(None, None, "tensor"), t0, t0, tc, P(), t1, t0, tc, P(), rows)
    out_specs = (rows, rows, P(), P(), P(None, None, "tensor"), t0, t0, tc, P(), t1, t0, tc, P())
    return jax.shard_map(local, mesh=mesh, in_specs=in_specs, out_specs=out_specs, check_vma=False)
```

time: 520 us -> 133 us (0.26)
  waiting for transfers between devices: 348 us -> 0 us
  blocking collectives: 69.1 us -> 0 us
  Pallas kernels: 64.5 us -> 125 us
  between operations: 14.2 us -> 0.67 us
  other arithmetic: 9.28 us -> 0 us
  local copies, waits for them, and re-layouts: 13.5 us -> 6.68 us
    reduce_scatter x4 -> x0, waiting for transfers between devices: 169 us -> none  [local(): lax.psum_scatter(g.astype(F32), 'tensor', scatter_dimension=0)]
    psum x1 -> x0, waiting for transfers between devices: 100 us -> none  [local(): big = lax.psum(tuple((scat(g) for g in (GH, GO, GU, GD))), 'dp')]
    all_gather x3 -> x0, waiting for transfers between devices: 76.9 us -> none  [local(): gather = lambda w: lax.all_gather(w, 'tensor', axis=0)]
    pallas_call x1 -> x2, Pallas kernels: 64.5 us -> 125 us  [the longest x1 120 us: main_call(): pl.pallas_call(kernel, out_shape=outs, in_specs=[hbm] * 6 + [vm] * 7, out...]
    psum x1 -> x0, blocking collectives: 41 us -> none  [local(): sm = lax.psum(sm, ('dp', 'tensor'))]
    all_gather x4 -> x0, blocking collectives: 28.1 us -> none  [local(): gather = lambda w: lax.all_gather(w, 'tensor', axis=0)]
    convert_element_type x4 -> x0, other arithmetic: 9.28 us -> none  [local(): g.astype(F32)]
    unnamed x26 -> x8, local copies, waits for them, and re-layouts: 11.1 us -> 3.94 us
  transfers between devices with their start and end apart: 8 -> 0, of which waited for: 8 -> 0; matrix products, arithmetic and copies ran while one was open for 2% -> 0% of each run, Pallas kernels for 0% -> 0%
where the time goes in v3:
time: 133 us; the launch traced here: 132 us
  Pallas kernels  125 us (94%)
  local copies, waits for them, and re-layouts  6.68 us (5%)
    pallas_call x1, Pallas kernels, main_call(): pl.pallas_call(kernel, out_shape=outs, in_specs=[hbm] * 6 + [vm] * 7, out...  120 us
    pallas_call x1, Pallas kernels, widen(): pl.pallas_call(kernel, out_shape=[S((3, D, HALF), F32), S((HALF, D), F32)...  4.89 us
    unnamed x8, local copies, waits for them, and re-layouts  3.94 us

profile of v3, /device:TPU:0, one launch (start us, length us, event | category | flops | bytes accessed | tf_op | source)
XLA Modules:
  0.0 131.9 jit_solution(442817456537705861)
XLA Ops:
  0.6 119.7 %layer.1 = (bf16[1024,512]{1,0:T(8,128)(2,1)}, bf16[1024,512]{1,0:T(8,128)(2,1)}, bf16[2,1536,128]{2,1,0:T(8,128)(2,1)}, bf16[256,512]{1,0:T(8,128)(2,1)}, bf16[...) custom-call(bf16[1024,512]{1,0:T(8,128)(2,1)} %refs_0_.1, bf16[1024,512]{1,0:T(8,128)(2,1)} %refs_1_.1, ...), custom_call_target="tpu_custom_call" | custom-call | tf_op jit(solution)/shard_map/layer/pallas_call | solution.py:606
  120.3 0.0 copy-start.1
  120.3 1.4 %fusion.1 = (f32[1,256]{1,0:T(1,128)}, f32[1,256]{1,0:T(1,128)}) fusion(f32[16,512]{1,0:T(8,128)} %get-tuple-element.26), kind=kLoop, calls=%fused_computation.2 | loop fusion | bytes 4096 | tf_op jit(solution)/shard_map/slice | solution.py:641
  121.7 1.4 %fusion = (f32[1,512]{1,0:T(1,128)}, f32[1,512]{1,0:T(1,128)}) fusion(f32[16,512]{1,0:T(8,128)} %get-tuple-element.26), kind=kLoop, calls=%fused_computation.1 | loop fusion | bytes 8192 | tf_op jit(solution)/shard_map/slice | solution.py:641
  123.1 1.4 %slice_bitcast_fusion = (f32[1,4,2,128]{3,2,1,0:T(2,128)S(1)}, f32[2,512]{1,0:T(2,128)}, f32[2,512]{1,0:T(2,128)}) fusion(f32[16,512]{1,0:T(8,128)} %get-tuple-element.26), kind=kLoop, calls=%fused_computation | loop fusion | bytes 24576
  124.5 0.6 copy.26
  125.1 0.0 copy-start
  125.1 4.9 %widen.1 = (f32[3,512,256]{2,1,0:T(8,128)}, f32[256,512]{1,0:T(8,128)}, f32[512,1024]{1,0:T(8,128)}, f32[1024,512]{1,0:T(8,128)}) custom-call(bf16[2,1536,128]{2,1,0:T(8,128)(2,1)} %get-tuple-element.27.h, bf16[256,512]{1,0:T(8,128)(2,1)} %get-tuple-element.28.o, bf16[512,1024]{1,0:T(8,128)(2,1)} %get-tuple-element.29.u, bf16[1024,512]{1,0:T(8,128)(2,1)} %get-tuple-element.30.d), custom_call_target="tpu_custom_call" | custom-call | tf_op jit(solution)/shard_map/widen/pallas_call | solution.py:626
  130.0 0.0 copy-done.1
  130.0 1.0 copy.29
  130.9 0.0 copy-done
  130.9 1.0 copy.30
Async XLA Ops:
  120.3 9.6 %copy-start.1 = (bf16[1024,512]{1,0:T(8,128)(2,1)S(1)}, bf16[1024,512]{1,0:T(8,128)(2,1)}, u32[]{:S(2)}) copy-start(bf16[1024,512]{1,0:T(8,128)(2,1)} %get-tuple-element.55) | copy-start | bytes 3145732
  125.1 5.9 %copy-start = (bf16[1024,512]{1,0:T(8,128)(2,1)S(1)}, bf16[1024,512]{1,0:T(8,128)(2,1)}, u32[]{:S(2)}) copy-start(bf16[1024,512]{1,0:T(8,128)(2,1)} %get-tuple-element.56) | copy-start | bytes 3145732

commit v4 on v3

v4 whole, which is shorter than its diff:
```python
import jax
import jax.numpy as jnp
from jax import lax
from jax.experimental import pallas as pl
from jax.experimental.pallas import tpu as pltpu
from jax.sharding import PartitionSpec as P

F32, BF16 = jnp.float32, jnp.bfloat16
NN, NT, TN = ((1,), (0,)), ((1,), (1,)), ((0,), (0,))
EPS = 1e-5
LOG2E = 1.4426950408889634
LN2 = 0.6931471805599453
C0, C1 = 0.7978845608, 0.044715
HD, BLK, D, HALF, FH, NH = 64, 256, 512, 256, 1024, 4
MESH = pl.DeviceIdType.MESH
VMEM_BYTES = 67043328


def dot(a, b, dims=NN):
    return lax.dot_general(a, b, (dims, ((), ())), preferred_element_type=F32)


def normed(v):
    c = jnp.mean(v, -1, keepdims=True)
    d = v - c
    r = lax.rsqrt(jnp.mean(d * d, -1, keepdims=True) + EPS)
    return d * r, r


def ln_back(g, xhat, r, gain):
    gx = g * gain
    return r * (gx - jnp.mean(gx, -1, keepdims=True) - xhat * jnp.mean(gx * xhat, -1, keepdims=True))


def rows_of(r):
    return pl.ds(pl.multiple_of(r * BLK, BLK), BLK)


def column(row):
    return jnp.broadcast_to(row, (8, row.shape[-1])).T[:, 0:1]


class Refs:
    pass


def ln1(z):
    def body(r, c):
        xh, _ = normed(z.x[rows_of(r), :].astype(F32))
        n = (xh * z.ns[0:1, :] + z.nsh[0:1, :]).astype(BF16)
        z.n1T[:, rows_of(r)] = n.T
        return c

    lax.fori_loop(0, z.nb, body, 0)


def qkv(z, s, h0, h1):
    cs = slice(h0 * HD, h1 * HD)
    qb, vb = column(z.qb[s][:, cs]), column(z.vb[s][:, cs])
    for b in range(z.nb):
        sl = slice(b * BLK, (b + 1) * BLK)
        nt = z.n1T[:, sl]
        q = dot(z.hw[s, 0, :, cs], nt, TN) + qb
        z.qT[s, cs, sl] = (q * (LOG2E / 8.0)).astype(BF16)
        z.kT[s, cs, sl] = dot(z.hw[s, 1, :, cs], nt, TN).astype(BF16)
        v = (dot(z.hw[s, 2, :, cs], nt, TN) + vb).astype(BF16)
        for h in range(h0, h1):
            z.vT[s, h, 0:HD, sl] = v[(h - h0) * HD : (h - h0 + 1) * HD]
            z.vT[s, h, HD : HD + 16, sl] = jnp.ones((16, BLK), BF16)


def attn_fwd(z, s, h0, h1, hook):
    def body(h, c):
        hr = pl.ds(pl.multiple_of(h * HD, HD), HD)
        kh = z.kT[s, hr, :].T
        for b in range(z.nb):
            nk = BLK * (b + 1)
            off = BLK * (b * (b + 1) // 2)
            sl = slice(b * BLK, nk)
            sc = dot(kh[:nk], z.qT[s, hr, sl])
            m = jnp.max(sc, 0, keepdims=True)
            e = jnp.exp2(sc - m).astype(BF16)
            z.E[s * NH + h, off : off + nk, :] = e
            o = dot(z.vT[s, h, :, 0:nk], e)
            rl = 1.0 / o[HD : HD + 1]
            z.rl[s * NH + h, 0:1, sl] = rl
            z.mixT[s, hr, sl] = (o[0:HD] * rl).astype(BF16)
        hook(h)
        return c

    lax.fori_loop(h0, h1, body, 0)


def out_proj(z):
    for r in range(z.nb):
        sl = slice(r * BLK, (r + 1) * BLK)
        t = dot(z.mixT[0, :, sl], z.ow[0], TN) + dot(z.mixT[1, :, sl], z.ow[1], TN)
        res = z.x[sl, :].astype(F32) + (t + z.ob[...])
        z.res[sl, :] = res
        z.oacc[sl, :] = res + z.db[...]
        xh, _ = normed(res)
        z.n2[sl, :] = (xh * z.ns[1:2, :] + z.nsh[1:2, :]).astype(BF16)


def ffn(z, part, s, hook):
    first, last = (part, s) == (0, 0), (part, s) == (1, 1)
    fs = slice(part * 512, part * 512 + 512)

    def body(r, c):
        rr = rows_of(r)
        ct = z.cot[rr, :]
        u = dot(z.n2[rr, :], z.uw[s, :, fs]) + z.ub[s][:, fs]
        da = dot(ct, z.dw[s, fs, :], NT)
        u2 = u * u
        t = jnp.tanh(u * (C0 + (C0 * C1) * u2))
        hp = 0.5 + 0.5 * t
        z.act[s, rr, fs] = (u * hp).astype(BF16)
        gp = hp + (u * (0.5 - 0.5 * t * t)) * (C0 + (3 * C0 * C1) * u2)
        dp = (da * gp).astype(BF16)
        z.dpre[s, rr, fs] = dp
        g = dot(dp, z.uw[s, :, fs], NT)
        g2 = g if first else z.g2[rr, :] + g
        if not last:
            z.g2[rr, :] = g2
        else:
            xh, rs = normed(z.res[rr, :])
            gres = ct.astype(F32) + ln_back(g2, xh, rs, z.ns[1:2, :])
            br = gres.astype(BF16)
            z.res[rr, :] = gres
            z.br[rr, :] = br
            c = (
                c[0] + jnp.sum(g2 * xh, 0, keepdims=True),
                c[1] + jnp.sum(g2, 0, keepdims=True),
                c[2] + jnp.sum(br.astype(F32), 0, keepdims=True),
                c[3] + jnp.sum(ct.astype(F32), 0, keepdims=True),
            )
        hook(r)
        return c

    zero = jnp.zeros((1, D), F32)
    c = lax.fori_loop(0, z.nb, body, (zero,) * 4 if last else 0)
    if last:
        z.sm[1:2, :] = c[0]
        z.sm[3:4, :] = c[1]
        z.sm[4:5, :] = c[2]
        z.sm[5:6, :] = c[3]


def ffn_out(z, blocks):
    for r in blocks:
        rr = slice(r * BLK, (r + 1) * BLK)
        o = dot(z.act[0, rr, :], z.dw[0]) + dot(z.act[1, rr, :], z.dw[1])
        z.lo[rr, :] = (z.oacc[rr, :] + o).astype(BF16)


def d_down(z, part, s):
    for f in range(0, 512, 256):
        a = part * 512 + f
        z.GD[part][s][f : f + 256, :] = dot(z.act[s, :, a : a + 256], z.cot[...], TN).astype(BF16)


def d_up(z, part, s):
    z.GU[part][s][...] = dot(z.n2[...], z.dpre[s, :, part * 512 : part * 512 + 512], TN).astype(BF16)


def d_upb(z, s):
    ones = jnp.ones((8, z.dpre.shape[1]), BF16)
    for i in range(FH // 512):
        row = 9 + 8 * s + i
        z.sm[row : row + 1, :] = dot(ones, z.dpre[s, :, i * 512 : (i + 1) * 512])[0:1]


def d_out(z, s):
    z.GO[s][...] = dot(z.mixT[s], z.br[...]).astype(BF16)


def grad_mixed(z, s):
    for r in range(z.nb):
        sl = slice(r * BLK, (r + 1) * BLK)
        z.gmT[s, :, sl] = dot(z.ow[s], z.br[sl, :], NT).astype(BF16)


def attn_bwd(z, s, hook):
    def body(h, c):
        hr = pl.ds(pl.multiple_of(h * HD, HD), HD)
        hi = s * NH + h
        vh = z.vT[s, h, 0:HD, :].T
        gs = (z.gmT[s, hr, :].astype(F32) * z.rl[hi]).astype(BF16)
        delta = jnp.sum(gs.astype(F32) * z.mixT[s, hr, :].astype(F32), 0, keepdims=True)
        for b in range(z.nb):
            nk = BLK * (b + 1)
            off = BLK * (b * (b + 1) // 2)
            sl = slice(b * BLK, nk)
            gq = gs[:, sl]
            e = z.E[hi, off : off + nk, :]
            dp = dot(vh[:nk], gq)
            ds = (e.astype(F32) * (dp - delta[:, sl])).astype(BF16)
            z.dh[0:HD, sl] = (dot(z.kT[s, hr, 0:nk], ds) * 0.125).astype(BF16)
            dv = dot(gq, e, NT)
            dk = dot(z.qT[s, hr, sl], ds, NT)
            if b:
                z.dva[:, 0 : nk - BLK] = z.dva[:, 0 : nk - BLK] + dv[:, 0 : nk - BLK]
                z.dka[:, 0 : nk - BLK] = z.dka[:, 0 : nk - BLK] + dk[:, 0 : nk - BLK]
            z.dva[:, sl] = dv[:, nk - BLK : nk]
            z.dka[:, sl] = dk[:, nk - BLK : nk]
        z.dh[HD : 2 * HD, :] = (z.dka[...] * LN2).astype(BF16)
        z.dh[2 * HD : 3 * HD, :] = z.dva[...].astype(BF16)
        for j in range(3):
            z.dT[s, pl.ds(pl.multiple_of(j * HALF + h * HD, HD), HD), :] = z.dh[j * HD : (j + 1) * HD, :]
        g = dot(z.dh[...], z.n1T[...], NT).astype(BF16)
        for q in range(4):
            z.GH[s][h, q * 192 : (q + 1) * 192, :] = g[:, q * 128 : (q + 1) * 128]
        hook(h)
        return c

    lax.fori_loop(0, NH, body, 0)


def d_headb(z, s):
    ones = jnp.ones((8, z.dT.shape[2]), BF16)
    for i, j in enumerate((0, 2)):
        row = 8 + 8 * s
        z.sm[row : row + 1, i * HALF : (i + 1) * HALF] = dot(ones, z.dT[s, j * HALF : (j + 1) * HALF, :], NT)[0:1]


def grad_in(z):
    zero = jnp.zeros((1, D), F32)
    sc, sh = zero, zero
    for r in range(z.nb):
        sl = slice(r * BLK, (r + 1) * BLK)
        g = 0.0
        for s in (0, 1):
            for j in range(3):
                g = g + dot(z.hw[s, j], z.dT[s, j * HALF : (j + 1) * HALF, sl])
        g = g.T
        xh, rs = normed(z.x[sl, :].astype(F32))
        z.ig[sl, :] = (z.res[sl, :] + ln_back(g, xh, rs, z.ns[0:1, :])).astype(BF16)
        sc = sc + jnp.sum(g * xh, 0, keepdims=True)
        sh = sh + jnp.sum(g, 0, keepdims=True)
    z.sm[0:1, :] = sc
    z.sm[2:3, :] = sh


class Comm:
    def __init__(self, ndp, groups, send, recv, local):
        self.send, self.recv, self.local = send, recv, local
        self.count, self.local_count, self.pending = 0, 0, []
        me = lax.axis_index("dp")
        self.levels = [1 << i for i in range(ndp.bit_length() - 1)]
        self.bit = {b: (me // b) % 2 for b in self.levels}
        self.me = me
        self.greet = ["t"] + [([b], 1) for b in self.levels] + [(g, d) for g in groups for d in range(1, 1 << len(g)) if d & (d - 1)]
        self.peer = 1 - lax.axis_index("tensor")

    def where(self, axis):
        if axis == "t":
            return {"tensor": self.peer}
        bits, delta = axis
        return {"dp": self.me + sum(b - 2 * b * self.bit[b] for i, b in enumerate(bits) if delta >> i & 1)}

    def barrier_signal(self):
        sem = pltpu.get_barrier_semaphore()
        for axis in self.greet:
            pl.semaphore_signal(sem, inc=1, device_id=self.where(axis), device_id_type=MESH)

    def barrier_wait(self):
        pl.semaphore_wait(pltpu.get_barrier_semaphore(), len(self.greet))

    def copy(self, src, dst, axis, keep=True):
        i = self.count
        self.count += 1

        def make():
            return pltpu.make_async_remote_copy(
                src_ref=src(), dst_ref=dst(), send_sem=self.send.at[i], recv_sem=self.recv.at[i],
                device_id=self.where(axis), device_id_type=MESH)

        if keep:
            self.pending.append(make)
        return make

    def here(self, src, dst):
        i = self.local_count
        self.local_count += 1
        return lambda: pltpu.make_async_copy(src(), dst(), self.local.at[i])

    def drain(self):
        for make in self.pending:
            make().wait_send()


def add_rows(dst, srcs, at, n, cols):
    ch = next(c for c in (384, 256, 192, 128, 96, 64, 48, 32, 16, 8, 4) if n % c == 0 and c * cols <= 49152)

    def body(i, c):
        o = pl.ds(pl.multiple_of(at + i * ch, ch), ch)
        f = pl.ds(pl.multiple_of(i * ch, ch), ch)
        if len(srcs) == 1:
            dst[o, :] = dst[o, :] + srcs[0][f, :]
        else:
            dst[o, :] = pairwise([dst[o, :].astype(F32)] + [s[f, :].astype(F32) for s in srcs]).astype(dst.dtype)
        return c

    lax.fori_loop(0, n // ch, body, 0)


def pairwise(v):
    while len(v) > 1:
        v = [v[i] + v[i + 1] for i in range(0, len(v), 2)]
    return v[0]


def sizes_of(rows, stages):
    n = [rows]
    for bits in stages:
        n.append(n[-1] >> len(bits))
    return n


def job_scratch(rows, cols, stages, pre, extra):
    V = pltpu.VMEM
    n = sizes_of(rows, stages)
    bufs = lambda ss: [V((n[k + 1], cols), BF16) for k in range(ss) for _ in range((1 << len(stages[k])) - 1)]
    return bufs(len(stages)) + bufs(pre) + [V((n[pre], cols), BF16)] + [V((n[-1], cols), BF16) for _ in range(extra)] + [V((rows, cols), BF16)]


class Job:
    def __init__(self, c, own, peer, refs, rows, cols, stages, pre, out):
        S = len(stages)
        done = sum(len(b) for b in stages)
        extra = c.levels[done:]
        n = sizes_of(rows, stages)
        refs = list(refs)
        take = lambda m: [refs.pop(0) for _ in range(m)]
        r_own = [take((1 << len(b)) - 1) for b in stages]
        r_peer = [take((1 << len(b)) - 1) for b in stages[:pre]]
        r_t, r_x, full = take(1)[0], take(len(extra)), refs.pop(0)

        def code(bits, delta):
            return sum((c.bit[b] if not delta >> i & 1 else 1 - c.bit[b]) * (1 << i) for i, b in enumerate(bits))

        lo = [0]
        for k, b in enumerate(stages):
            lo.append(lo[k] + code(b, 0) * n[k + 1])
        at = lambda k: pl.ds(pl.multiple_of(lo[k], n[k]) if k else 0, n[k])
        theirs = lambda k, d: pl.ds(pl.multiple_of(lo[k] + code(stages[k], d) * n[k + 1], n[k + 1]), n[k + 1])

        def scatter(g, bufs, k):
            return [c.copy(lambda d=d: g().at[theirs(k, d)], lambda d=d: bufs[d - 1], (stages[k], d)) for d in range(1, len(bufs) + 1)]

        s_own = [scatter(own, r_own[k], k) for k in range(S)]
        s_peer = [scatter(peer, r_peer[k], k) for k in range(pre)]
        s_t = c.copy(lambda: peer().at[at(pre)], lambda: r_t, "t")
        s_x = [c.copy(lambda: own().at[at(S)], lambda i=i: r_x[i], ([b], 1), False) for i, b in enumerate(extra)]
        s_g = [[c.copy(lambda k=k: full.at[at(k + 1)], lambda k=k: full.at[at(k + 1)], (stages[k], d)) for d in range(1, 1 << len(stages[k]))]
               for k in range(S)]
        s_out = c.here(lambda: full, lambda: out())
        self.wait_out = lambda: s_out().wait()
        start = lambda ss: [s().start() for s in ss]
        arrived = lambda ss: [s().wait_recv() for s in ss]

        def end(s, g, buf, k):
            arrived(s[k])
            add_rows(g(), buf[k], lo[k + 1], n[k + 1], cols)

        def peer_step(i):
            if i:
                end(s_peer, peer, r_peer, i - 1)
            start(s_peer[i] if i < pre else [s_t])

        def own_step(i):
            if i == 0:
                start(s_own[0])
            elif i <= S:
                end(s_own, own, r_own, i - 1)
                if i == pre:
                    assert not self.peer_steps
                    s_t().wait_recv()
                    add_rows(own(), [r_t], lo[pre], n[pre], cols)
                if i < S:
                    start(s_own[i])
                    return
                for j in range(len(extra)):
                    s_x[j]().start()
                    s_x[j]().wait()
                    add_rows(own(), [r_x[j]], lo[S], n[S], cols)
                full[at(S), :] = own()[at(S), :]
                start(s_g[S - 1])
            else:
                k = 2 * S - i
                arrived(s_g[k])
                if k:
                    start(s_g[k - 1])
                else:
                    s_out().start()

        self.peer_steps = [lambda i=i: peer_step(i) for i in range(pre + 1)]
        self.own_steps = [lambda i=i: own_step(i) for i in range(2 * S + 1)]

    def own(self):
        self.own_steps.pop(0)()

    def peer(self):
        self.peer_steps.pop(0)()


SMALL_STAGES = [[1], [2], [4, 8]]


class Small:
    def __init__(self, c, sm, bufs):
        bufs = list(bufs)
        r_t = bufs.pop(0)
        st = SMALL_STAGES + [[b] for b in c.levels[4:]]
        s_t = [c.copy(lambda: sm.at[0:8], lambda: r_t.at[0:8], "t", False), c.copy(lambda: sm.at[16:24], lambda: r_t.at[8:16], "t", False)]
        rs, ss = [[r_t]], [s_t]
        for bits in st:
            r = [bufs.pop(0) for _ in range((1 << len(bits)) - 1)]
            rs.append(r)
            ss.append([c.copy(lambda: sm.at[0:16], lambda b=b: b, (bits, d + 1), False) for d, b in enumerate(r)])

        def step(i):
            if i:
                for s in ss[i - 1]:
                    s().wait()
                sm[0:16, :] = pairwise([sm[0:16, :]] + [r[...] for r in rs[i - 1]])
            if i < len(ss):
                for s in ss[i]:
                    s().start()

        self.steps = [lambda i=i: step(i) for i in range(len(ss) + 1)]

    def own(self):
        self.steps.pop(0)()


INS = ["x_h", "cot_h", "hw_h", "ow_h", "uw_h", "dw_h", "ns", "nsh", "qb_o", "vb_o", "ob", "ub_o", "db"]
OUTS = ["lo_h", "ig_h", "FH_h", "FO_h", "FU_h", "FD_h", "smo"]
Y4, Z14, G8 = [[1], [2], [4, 8]], [[1], [4], [2], [8]], [[1], [2, 4, 8]]
JOBS = [("D0", 512, 512, [[1], [2], [4, 8]], 1),
        ("U0", 512, 512, [[1], [2], [4, 8]], 2),
        ("D1", 512, 512, [[1], [2], [4, 8]], 1),
        ("U1", 512, 512, [[1], [2], [4, 8]], 2),
        ("O", 256, 512, [[1], [2], [4, 8]], 1),
        ("H0", 1536, 128, [[1], [2], [4, 8]], 1),
        ("H1", 1536, 128, [[1], [2], [4, 8]], 1)]

HOOKS = {
    "f0_0": ["WhwA"],
    "f0_2": ["WhwB", "Wow", "WhwA"],
    "qkv1a": ["Wu0"],
    "f1_0": ["WhwB"],
    "f1_1": ["Wow", "Wd0"],
    "f1_2": ["Wu0", "Wu1"],
    "f1_3": ["Wd0", "Wd1"],
    "ffn00_1": ["Wu1"],
    "dD00": ["D0o"],
    "dU00": ["Wd1", "U0o"],
    "ffn01_2": ["U0o"],
    "dD01": ["D0p"],
    "dU01": ["U0p"],
    "ffn10_0": ["D0p"],
    "ffn10_1": ["U0p"],
    "dD10": ["D1o"],
    "dU10": ["U1o"],
    "ffn11_1": ["U1o", "U0p"],
    "ffn11_3": ["D0o"],
    "dD11": ["D1p"],
    "dU11": ["U1p"],
    "dO1": ["Op"],
    "dO0": ["D1p", "U0o", "U1p", "Op", "Oo"],
    "b1_0": ["D0o"],
    "b1_1": ["U1p", "H0p", "U0o"],
    "b1_2": ["H0p", "D1o", "D0o"],
    "b1_3": ["H1p", "U0o", "Oo"],
    "b0_0": ["H1p", "D1o", "D0o", "U1o"],
    "b0_1": ["U0o", "H0o"],
    "b0_2": ["U0o", "Oo", "H0o", "D1o"],
    "b0_3": ["D0o", "H1o"],
    "hb": ["U1o"],
    "gin": ["D0o", "Oo", "H0o", "H1o", "So", "D1o"],
    "tail": ["So", "U1o", "So", "H1o", "Oo", "H0o", "D1o", "D1o", "H1o", "U1o", "So", "U1o", "H0o", "Oo", "Oo", "H1o", "H0o", "So", "H0o", "H1o", "H1o"],
}
BEFORE = {
}


def scratch(T, ndp):
    nb = T // BLK
    V = pltpu.VMEM
    lv = ndp.bit_length() - 1
    s = dict(
        x=V((T, D), BF16), cot=V((T, D), BF16), hw=V((2, 3, D, HALF), BF16), ow=V((2, HALF, D), BF16),
        uw=V((2, D, FH), BF16), dw=V((2, FH, D), BF16),
        qb_p=V((1, HALF), F32), vb_p=V((1, HALF), F32), ub_p=V((1, FH), F32),
        n1T=V((D, T), BF16), qT=V((2, HALF, T), BF16), kT=V((2, HALF, T), BF16), vT=V((2, NH, 80, T), BF16),
        E=V((2 * NH, BLK * nb * (nb + 1) // 2, BLK), BF16), rl=V((2 * NH, 1, T), F32), mixT=V((2, HALF, T), BF16),
        res=V((T, D), F32), n2=V((T, D), BF16), act=V((2, T, FH), BF16), dpre=V((2, T, FH), BF16),
        oacc=V((T, D), F32), g2=V((T, D), F32), br=V((T, D), BF16), gmT=V((2, HALF, T), BF16),
        dh=V((3 * HD, T), BF16), dva=V((HD, T), F32), dka=V((HD, T), F32), sm=V((24, D), F32),
        GD0o=V((FH // 2, D), BF16), GD0p=V((FH // 2, D), BF16), GD1o=V((FH // 2, D), BF16), GD1p=V((FH // 2, D), BF16),
        GU0o=V((D, FH // 2), BF16), GU0p=V((D, FH // 2), BF16), GU1o=V((D, FH // 2), BF16), GU1p=V((D, FH // 2), BF16),
        GOo=V((HALF, D), BF16), GOp=V((HALF, D), BF16), GHo=V((NH, 768, 128), BF16), GHp=V((NH, 768, 128), BF16),
        s0=V((16, D), F32))
    for i in range(5 + lv - 4):
        s[f"s{i + 1}"] = V((16, D), F32)
    for name, rows, cols, stages, pre in JOBS:
        for i, v in enumerate(job_scratch(rows, cols, stages, pre, lv - 4)):
            s[f"{name}_{i}"] = v
    s["send"] = pltpu.SemaphoreType.DMA((160 + 16 * (lv - 4),))
    s["recv"] = pltpu.SemaphoreType.DMA((160 + 16 * (lv - 4),))
    s["local"] = pltpu.SemaphoreType.DMA((24,))
    return s


def run(z, ndp):
    c = Comm(ndp, [[4, 8], [2, 4, 8]], z.send, z.recv, z.local)
    lv = c.levels
    c.barrier_signal()
    slot0 = lambda r: r.at[0]
    loads = {n: c.here(lambda n=n: getattr(z, n + "_h"), lambda n=n, d=d: d(getattr(z, n)))
             for n, d in (("x", lambda r: r), ("hw", slot0), ("cot", lambda r: r), ("ow", slot0), ("uw", slot0), ("dw", slot0))}
    for n in ("x", "hw", "ow", "cot", "uw", "dw"):
        loads[n]().start()

    pieces = {"hwA": ("hw", D, 0, slice(0, 128)), "hwB": ("hw", D, 0, slice(128, 256)), "ow": ("ow", HALF, 0, slice(None)),
              "u0": ("uw", D, 0, slice(0, 512)), "d0": ("dw", 512, 0, slice(None)), "u1": ("uw", D, 0, slice(512, 1024)),
              "d1": ("dw", 512, 512, slice(None))}

    def view(name, flip, lead):
        n, m, base, cols = pieces[name]
        q = (c.bit[1] if not flip & 1 else 1 - c.bit[1]) + 2 * (c.bit[2] if not flip & 2 else 1 - c.bit[2])
        rows = pl.ds(pl.multiple_of(base + q * (m // 4), m // 4), m // 4)
        r = getattr(z, n).at[1] if lead else getattr(z, n + "_h")
        return r.at[:, rows, cols] if n == "hw" else r.at[rows, cols]

    W = {}
    for name in pieces:
        put = lambda flip, name=name: view(name, flip, True)
        W[name] = dict(
            x=c.copy(lambda name=name: view(name, 0, False), lambda put=put: put(0), "t"),
            s=c.copy(lambda put=put: put(0), lambda put=put: put(0), ([1], 1)),
            y=c.copy(lambda put=put: put(0), lambda put=put: put(0), ([2], 1)),
            r=c.copy(lambda put=put: put(2), lambda put=put: put(2), ([1], 1)))
    wb = [c.copy(lambda n=n: getattr(z, n + "_o"), lambda n=n: getattr(z, n + "_p"), "t") for n in ("qb", "vb", "ub")]

    def relay1(n):
        W[n]["x"]().wait_recv()
        W[n]["y"]().start()
        W[n]["s"]().start()

    def relay2(n):
        W[n]["y"]().wait_recv()
        W[n]["r"]().start()

    def arrive(n):
        W[n]["s"]().wait_recv()
        W[n]["r"]().wait_recv()

    c.barrier_wait()
    W["hwA"]["x"]().start()
    for b in wb:
        b().start()
    for n in list(pieces)[1:]:
        W[n]["x"]().start()

    z.qb, z.vb, z.ub = (z.qb_o, z.qb_p), (z.vb_o, z.vb_p), (z.ub_o, z.ub_p)
    z.GD = ((z.GD0o, z.GD0p), (z.GD1o, z.GD1p))
    z.GU = ((z.GU0o, z.GU0p), (z.GU1o, z.GU1p))
    z.GO, z.GH = (z.GOo, z.GOp), (z.GHo, z.GHp)
    z.dT, z.lo, z.ig = z.dpre, z.br, z.n2
    ends = dict(D0=lambda: z.FD_h.at[0 : FH // 2], D1=lambda: z.FD_h.at[FH // 2 : FH], U0=lambda: z.FU_h.at[:, 0 : FH // 2],
                U1=lambda: z.FU_h.at[:, FH // 2 : FH], O=lambda: z.FO_h, H0=lambda: z.FH_h.at[0], H1=lambda: z.FH_h.at[1])
    flat = lambda r, i: (lambda: r.at[2 * i : 2 * i + 2].reshape(1536, 128))
    srcs = dict(D0=(lambda: z.GD0o, lambda: z.GD0p), D1=(lambda: z.GD1o, lambda: z.GD1p), U0=(lambda: z.GU0o, lambda: z.GU0p),
                U1=(lambda: z.GU1o, lambda: z.GU1p), O=(lambda: z.GOo, lambda: z.GOp),
                H0=(flat(z.GHo, 0), flat(z.GHp, 0)), H1=(flat(z.GHo, 1), flat(z.GHp, 1)))
    jobs = {}
    for name, rows, cols, stages, pre in JOBS:
        refs = [getattr(z, f"{name}_{i}") for i in range(len(job_scratch(rows, cols, stages, pre, len(lv) - 4)))]
        jobs[name] = Job(c, *srcs[name], refs, rows, cols, stages, pre, ends[name])
    jobs["S"] = small = Small(c, z.sm, [getattr(z, f"s{i}") for i in range(6 + len(lv) - 4)])
    s_lo, s_ig = c.here(lambda: z.lo, lambda: z.lo_h), c.here(lambda: z.ig, lambda: z.ig_h)

    relays = {n: [relay1, relay2] for n in W}

    def go(words):
        for word in words:
            if word[1:] in relays:
                relays[word[1:]].pop(0)(word[1:])
            else:
                (jobs[word[:-1]].own if word[-1] == "o" else jobs[word[:-1]].peer)()

    def at(name, n):
        table = {k: HOOKS.get(f"{name}_{k}", ()) for k in (range(n) if isinstance(n, int) else n)}

        def hook(h):
            for k, what in table.items():
                if what:
                    @pl.when(h == k)
                    def _():
                        go(what)
        return hook

    def before(name):
        go(BEFORE.get(name, ()))

    def after(name):
        go(HOOKS.get(name, ()))

    z.sm[...] = jnp.zeros_like(z.sm)
    loads["x"]().wait()
    ln1(z)
    loads["hw"]().wait()
    qkv(z, 0, 0, NH)
    after("qkv0")
    attn_fwd(z, 0, 0, NH, at("f0", 4))
    before("qkv1a")
    for b in wb:
        b().wait_recv()
    arrive("hwA")
    qkv(z, 1, 0, 2)
    after("qkv1a")
    attn_fwd(z, 1, 0, 2, at("f1", range(0, 2)))
    before("qkv1b")
    arrive("hwB")
    qkv(z, 1, 2, 4)
    after("qkv1b")
    attn_fwd(z, 1, 2, 4, at("f1", range(2, 4)))
    before("out")
    arrive("ow")
    loads["ow"]().wait()
    out_proj(z)
    for n in ("cot", "uw", "dw"):
        loads[n]().wait()
    after("out")
    for part in (0, 1):
        for s in (0, 1):
            name = f"ffn{part}{s}"
            before(name + "_0")
            if s:
                arrive(f"u{part}")
                arrive(f"d{part}")
            ffn(z, part, s, at(name, z.nb))
            d_down(z, part, s)
            after(f"dD{part}{s}")
            d_up(z, part, s)
            if part:
                d_upb(z, s)
            after(f"dU{part}{s}")
    for s in (1, 0):
        d_out(z, s)
        after(f"dO{s}")
    grad_mixed(z, 1)
    grad_mixed(z, 0)
    after("gm")
    attn_bwd(z, 1, at("b1", NH))
    attn_bwd(z, 0, at("b0", NH))
    d_headb(z, 0)
    d_headb(z, 1)
    after("hb")
    grad_in(z)
    s_ig().start()
    after("gin")
    ffn_out(z, (0, 1))
    after("fo0")
    ffn_out(z, (2, 3))
    s_lo().start()
    after("fo1")
    after("tail")
    while small.steps:
        small.own()
    assert not any(v for v in relays.values()) and not any(jobs[n].own_steps for n in jobs if n != "S")
    z.smo[...] = z.sm[0:16, :]
    s_ig().wait()
    s_lo().wait()
    for n in jobs:
        if n != "S":
            jobs[n].wait_out()
    c.drain()


def main_call(args, T, ndp):
    scr = scratch(T, ndp)
    names = INS + OUTS + list(scr)

    def kernel(*refs):
        z = Refs()
        for n, r in zip(names, refs):
            setattr(z, n, r)
        z.nb = T // BLK
        run(z, ndp)

    S = jax.ShapeDtypeStruct
    outs = [S((T, D), BF16), S((T, D), BF16), S((2, 1536, 128), BF16), S((HALF, D), BF16), S((D, FH), BF16), S((FH, D), BF16),
            S((16, D), F32)]
    vm, hbm = pl.BlockSpec(memory_space=pltpu.VMEM), pl.BlockSpec(memory_space=pl.ANY)
    return pl.pallas_call(
        kernel, out_shape=outs, in_specs=[hbm] * 6 + [vm] * 7, out_specs=[hbm] * 6 + [vm], scratch_shapes=list(scr.values()),
        compiler_params=pltpu.CompilerParams(vmem_limit_bytes=VMEM_BYTES, collective_id=0, has_side_effects=True),
        name="layer")(*args)


def widen(FH_, FO_, FU_, FD_, sm):
    def kernel(h, o, u, d, m, ho, oo, uo, do, sc, sh, qb, vb, ob, ub, db):
        oo[...] = o[...].astype(F32)
        uo[...] = u[...].astype(F32)
        do[...] = d[...].astype(F32)
        for q in range(4):
            for j in range(3):
                for p in range(2):
                    rows = [h[p, i * 768 + q * 192 + j * HD : i * 768 + q * 192 + (j + 1) * HD, :] for i in range(2)]
                    t = jnp.concatenate(rows, 0).astype(F32).T
                    ho[j, q * 128 : (q + 1) * 128, p * 128 : (p + 1) * 128] = t
        sc[...] = m[0:2, :]
        sh[...] = m[2:4, :]
        qb[...] = m[8:9, 0:HALF]
        vb[...] = m[8:9, HALF:D]
        ob[...] = m[4:5, :]
        ub[:, 0:D] = m[9:10, :]
        ub[:, D:FH] = m[10:11, :]
        db[...] = m[5:6, :]

    S = jax.ShapeDtypeStruct
    vm = pl.BlockSpec(memory_space=pltpu.VMEM)
    shapes = [(3, D, HALF), (HALF, D), (D, FH), (FH, D), (2, D), (2, D), (1, HALF), (1, HALF), (1, D), (1, FH), (1, D)]
    return pl.pallas_call(kernel, out_shape=[S(t, F32) for t in shapes], in_specs=[vm] * 5, out_specs=[vm] * 11, name="widen")(
        FH_, FO_, FU_, FD_, sm)


def solution(mesh):
    ndp = mesh.shape["dp"]

    def local(inputs, norm_scale, norm_shift, head_weight, query_bias, value_bias, out_weight, out_bias, up_weight, up_bias,
              down_weight, down_bias, cotangent):
        row = lambda b: b.reshape(1, b.shape[0])
        args = (inputs, cotangent, head_weight, out_weight, up_weight, down_weight, norm_scale, norm_shift, row(query_bias),
                row(value_bias), row(out_bias), row(up_bias), row(down_bias))
        lo, ig, gh, go, gu, gd, sm = main_call(args, inputs.shape[0], ndp)
        gh, go, gu, gd, sc, sh, qb, vb, ob, ub, db = widen(gh, go, gu, gd, sm)
        flat = lambda v: v.reshape(v.shape[1])
        return (lo, ig, sc, sh, gh, flat(qb), flat(vb), go, flat(ob), gu, flat(ub), gd, flat(db))

    rows, t0, t1 = P(("dp", "tensor"), None), P("tensor"), P(None, "tensor")
    tc = P("tensor", None)
    in_specs = (rows, P(), P(), P(None, None, "tensor"), t0, t0, tc, P(), t1, t0, tc, P(), rows)
    out_specs = (rows, rows, P(), P(), P(None, None, "tensor"), t0, t0, tc, P(), t1, t0, tc, P())
    return jax.shard_map(local, mesh=mesh, in_specs=in_specs, out_specs=out_specs, check_vma=False)
```

time: 133 us -> 110 us (0.83)
  Pallas kernels: 125 us -> 106 us
  local copies, waits for them, and re-layouts: 6.68 us -> 1.95 us
    pallas_call x1, Pallas kernels: 120 us -> 101 us  [main_call(): pl.pallas_call(kernel, out_shape=outs, in_specs=[hbm] * 6 + [vm] * 7, out...]
    slice x2 -> x0, local copies, waits for them, and re-layouts: 2.75 us -> none  [the longest x1 1.38 us: local(): sm[5]]
    unnamed x8 -> x6, local copies, waits for them, and re-layouts: 3.94 us -> 1.95 us
where the time goes in v4:
time: 110 us; the launch traced here: 109 us
  Pallas kernels  106 us (96%)
  local copies, waits for them, and re-layouts  1.95 us (2%)
    pallas_call x1, Pallas kernels, main_call(): pl.pallas_call(kernel, out_shape=outs, in_specs=[hbm] * 6 + [vm] * 7, out...  101 us
    pallas_call x1, Pallas kernels, widen(): pl.pallas_call(kernel, out_shape=[S(t, F32) for t in shapes], in_specs=[v...  4.99 us

profile of v4, /device:TPU:0, one launch (start us, length us, event | category | flops | bytes accessed | tf_op | source)
XLA Modules:
  0.0 108.5 jit_solution(9121674514938430891)
XLA Ops:
  0.6 100.9 %layer.1 = (bf16[1024,512]{1,0:T(8,128)(2,1)}, bf16[1024,512]{1,0:T(8,128)(2,1)}, bf16[2,1536,128]{2,1,0:T(8,128)(2,1)}, bf16[256,512]{1,0:T(8,128)(2,1)}, bf16[...) custom-call(bf16[1024,512]{1,0:T(8,128)(2,1)} %refs_0_.1, bf16[1024,512]{1,0:T(8,128)(2,1)} %refs_1_.1, ...), custom_call_target="tpu_custom_call" | custom-call | tf_op jit(solution)/shard_map/layer/pallas_call | solution.py:698
  101.6 0.0 copy-start.1
  101.6 0.0 copy-start
  101.6 5.0 %widen.1 = (f32[3,512,256]{2,1,0:T(8,128)}, f32[256,512]{1,0:T(8,128)}, f32[512,1024]{1,0:T(8,128)}, f32[1024,512]{1,0:T(8,128)}, f32[2,512]{1,0:T(2,128)}, /*in...) custom-call(bf16[2,1536,128]{2,1,0:T(8,128)(2,1)} %get-tuple-element, ...), custom_call_target="tpu_custom_call" | custom-call | tf_op jit(solution)/shard_map/widen/pallas_call | solution.py:727
  106.6 0.0 copy-done.1
  106.6 1.0 copy.28
  107.5 0.0 copy-done
  107.6 1.0 copy.29
Async XLA Ops:
  101.6 5.0 %copy-start.1 = (bf16[1024,512]{1,0:T(8,128)(2,1)S(1)}, bf16[1024,512]{1,0:T(8,128)(2,1)}, u32[]{:S(2)}) copy-start(bf16[1024,512]{1,0:T(8,128)(2,1)} %get-tuple-element.62) | copy-start | bytes 3145732
  101.6 6.0 %copy-start = (bf16[1024,512]{1,0:T(8,128)(2,1)S(1)}, bf16[1024,512]{1,0:T(8,128)(2,1)}, u32[]{:S(2)}) copy-start(bf16[1024,512]{1,0:T(8,128)(2,1)} %get-tuple-element.63) | copy-start | bytes 3145732

commit v5 on v4

--- a/solution.py
+++ b/solution.py
@@ -70,14 +70,23 @@
 
 
 def attn_fwd(z, s, h0, h1, hook):
-    def body(h, c):
-        hr = pl.ds(pl.multiple_of(h * HD, HD), HD)
-        kh = z.kT[s, hr, :].T
-        for b in range(z.nb):
+    def body(p, c):
+        hrs = [pl.ds(pl.multiple_of(p * 2 * HD + j * HD, HD), HD) for j in (0, 1)]
+        khs = [z.kT[s, hr, :].T for hr in hrs]
+
+        def scores(j, b):
+            return dot(khs[j][: BLK * (b + 1)], z.qT[s, hrs[j], b * BLK : (b + 1) * BLK])
+
+        items = [(j, b) for j in (0, 1) for b in range(z.nb)]
+        ahead = scores(*items[0])
+        for i, (j, b) in enumerate(items):
+            sc = ahead
+            if i + 1 < len(items):
+                ahead = scores(*items[i + 1])
+            h, hr = 2 * p + j, hrs[j]
             nk = BLK * (b + 1)
             off = BLK * (b * (b + 1) // 2)
             sl = slice(b * BLK, nk)
-            sc = dot(kh[:nk], z.qT[s, hr, sl])
             m = jnp.max(sc, 0, keepdims=True)
             e = jnp.exp2(sc - m).astype(BF16)
             z.E[s * NH + h, off : off + nk, :] = e
@@ -85,10 +94,10 @@
             rl = 1.0 / o[HD : HD + 1]
             z.rl[s * NH + h, 0:1, sl] = rl
             z.mixT[s, hr, sl] = (o[0:HD] * rl).astype(BF16)
-        hook(h)
+        hook(p)
         return c
 
-    lax.fori_loop(h0, h1, body, 0)
+    lax.fori_loop(h0 // 2, h1 // 2, body, 0)
 
 
 def out_proj(z):
@@ -103,42 +112,48 @@
 
 
 def ffn(z, part, s, hook):
-    first, last = (part, s) == (0, 0), (part, s) == (1, 1)
+    first, last = (part, s) == (0, 1), (part, s) == (1, 0)
     fs = slice(part * 512, part * 512 + 512)
 
-    def body(r, c):
-        rr = rows_of(r)
+    def products(rr):
         ct = z.cot[rr, :]
-        u = dot(z.n2[rr, :], z.uw[s, :, fs]) + z.ub[s][:, fs]
-        da = dot(ct, z.dw[s, fs, :], NT)
-        u2 = u * u
-        t = jnp.tanh(u * (C0 + (C0 * C1) * u2))
-        hp = 0.5 + 0.5 * t
-        z.act[s, rr, fs] = (u * hp).astype(BF16)
-        gp = hp + (u * (0.5 - 0.5 * t * t)) * (C0 + (3 * C0 * C1) * u2)
-        dp = (da * gp).astype(BF16)
-        z.dpre[s, rr, fs] = dp
-        g = dot(dp, z.uw[s, :, fs], NT)
-        g2 = g if first else z.g2[rr, :] + g
-        if not last:
-            z.g2[rr, :] = g2
-        else:
-            xh, rs = normed(z.res[rr, :])
-            gres = ct.astype(F32) + ln_back(g2, xh, rs, z.ns[1:2, :])
-            br = gres.astype(BF16)
-            z.res[rr, :] = gres
-            z.br[rr, :] = br
-            c = (
-                c[0] + jnp.sum(g2 * xh, 0, keepdims=True),
-                c[1] + jnp.sum(g2, 0, keepdims=True),
-                c[2] + jnp.sum(br.astype(F32), 0, keepdims=True),
-                c[3] + jnp.sum(ct.astype(F32), 0, keepdims=True),
-            )
-        hook(r)
+        return ct, dot(z.n2[rr, :], z.uw[s, :, fs]) + z.ub[s][:, fs], dot(ct, z.dw[s, fs, :], NT)
+
+    def body(p, c):
+        blocks = [rows_of(2 * p), rows_of(2 * p + 1)]
+        ahead = products(blocks[0])
+        for i, rr in enumerate(blocks):
+            ct, u, da = ahead
+            if i == 0:
+                ahead = products(blocks[1])
+            u2 = u * u
+            t = jnp.tanh(u * (C0 + (C0 * C1) * u2))
+            hp = 0.5 + 0.5 * t
+            z.act[s, rr, fs] = (u * hp).astype(BF16)
+            gp = hp + (u * (0.5 - 0.5 * t * t)) * (C0 + (3 * C0 * C1) * u2)
+            dp = (da * gp).astype(BF16)
+            z.dpre[s, rr, fs] = dp
+            g = dot(dp, z.uw[s, :, fs], NT)
+            g2 = g if first else z.g2[rr, :] + g
+            if not last:
+                z.g2[rr, :] = g2
+            else:
+                xh, rs = normed(z.res[rr, :])
+                gres = ct.astype(F32) + ln_back(g2, xh, rs, z.ns[1:2, :])
+                br = gres.astype(BF16)
+                z.res[rr, :] = gres
+                z.br[rr, :] = br
+                c = (
+                    c[0] + jnp.sum(g2 * xh, 0, keepdims=True),
+                    c[1] + jnp.sum(g2, 0, keepdims=True),
+                    c[2] + jnp.sum(br.astype(F32), 0, keepdims=True),
+                    c[3] + jnp.sum(ct.astype(F32), 0, keepdims=True),
+                )
+        hook(p)
         return c
 
     zero = jnp.zeros((1, D), F32)
-    c = lax.fori_loop(0, z.nb, body, (zero,) * 4 if last else 0)
+    c = lax.fori_loop(0, z.nb // 2, body, (zero,) * 4 if last else 0)
     if last:
         z.sm[1:2, :] = c[0]
         z.sm[3:4, :] = c[1]
@@ -187,16 +202,20 @@
         vh = z.vT[s, h, 0:HD, :].T
         gs = (z.gmT[s, hr, :].astype(F32) * z.rl[hi]).astype(BF16)
         delta = jnp.sum(gs.astype(F32) * z.mixT[s, hr, :].astype(F32), 0, keepdims=True)
+        dprob = lambda b: dot(vh[: BLK * (b + 1)], gs[:, b * BLK : (b + 1) * BLK])
+        ahead = dprob(0)
         for b in range(z.nb):
+            dp = ahead
+            if b + 1 < z.nb:
+                ahead = dprob(b + 1)
             nk = BLK * (b + 1)
             off = BLK * (b * (b + 1) // 2)
             sl = slice(b * BLK, nk)
             gq = gs[:, sl]
             e = z.E[hi, off : off + nk, :]
-            dp = dot(vh[:nk], gq)
+            dv = dot(gq, e, NT)
             ds = (e.astype(F32) * (dp - delta[:, sl])).astype(BF16)
             z.dh[0:HD, sl] = (dot(z.kT[s, hr, 0:nk], ds) * 0.125).astype(BF16)
-            dv = dot(gq, e, NT)
             dk = dot(z.qT[s, hr, sl], ds, NT)
             if b:
                 z.dva[:, 0 : nk - BLK] = z.dva[:, 0 : nk - BLK] + dv[:, 0 : nk - BLK]
@@ -223,7 +242,7 @@
         z.sm[row : row + 1, i * HALF : (i + 1) * HALF] = dot(ones, z.dT[s, j * HALF : (j + 1) * HALF, :], NT)[0:1]
 
 
-def grad_in(z):
+def grad_in(z, hook):
     zero = jnp.zeros((1, D), F32)
     sc, sh = zero, zero
     for r in range(z.nb):
@@ -237,8 +256,10 @@
         z.ig[sl, :] = (z.res[sl, :] + ln_back(g, xh, rs, z.ns[0:1, :])).astype(BF16)
         sc = sc + jnp.sum(g * xh, 0, keepdims=True)
         sh = sh + jnp.sum(g, 0, keepdims=True)
-    z.sm[0:1, :] = sc
-    z.sm[2:3, :] = sh
+        if r == z.nb - 1:
+            z.sm[0:1, :] = sc
+            z.sm[2:3, :] = sh
+        hook(f"gin{r}")
 
 
 class Comm:
@@ -442,46 +463,51 @@
         ("D1", 512, 512, [[1], [2], [4, 8]], 1),
         ("U1", 512, 512, [[1], [2], [4, 8]], 2),
         ("O", 256, 512, [[1], [2], [4, 8]], 1),
-        ("H0", 1536, 128, [[1], [2], [4, 8]], 1),
-        ("H1", 1536, 128, [[1], [2], [4, 8]], 1)]
+        ("H0", 768, 128, [[1], [2], [4, 8]], 1),
+        ("H1", 768, 128, [[1], [2], [4, 8]], 1),
+        ("H2", 768, 128, [[1], [2], [4, 8]], 2),
+        ("H3", 768, 128, [[1], [2], [4, 8]], 1)]
 
 HOOKS = {
     "f0_0": ["WhwA"],
-    "f0_2": ["WhwB", "Wow", "WhwA"],
+    "f0_1": ["WhwB", "Wow"],
     "qkv1a": ["Wu0"],
-    "f1_0": ["WhwB"],
-    "f1_1": ["Wow", "Wd0"],
-    "f1_2": ["Wu0", "Wu1"],
-    "f1_3": ["Wd0", "Wd1"],
-    "ffn00_1": ["Wu1"],
+    "f1_0": ["Wd0", "WhwB", "Wow"],
+    "qkv1b": ["Wu1", "Wu0"],
+    "f1_1": ["Wd0", "Wd1"],
+    "ffn01_0": ["Wu1"],
+    "dD01": ["D0p"],
+    "dU01": ["Wd1", "U0p"],
+    "ffn00_0": ["D0p"],
+    "ffn00_1": ["U0p"],
     "dD00": ["D0o"],
-    "dU00": ["Wd1", "U0o"],
-    "ffn01_2": ["U0o"],
-    "dD01": ["D0p"],
-    "dU01": ["U0p"],
-    "ffn10_0": ["D0p"],
-    "ffn10_1": ["U0p"],
+    "dU00": ["U0o"],
+    "ffn11_1": ["U0o"],
+    "dD11": ["U0p", "D1p"],
+    "dU11": ["U1p"],
+    "ffn10_0": ["D0o", "D1p", "U1p"],
     "dD10": ["D1o"],
-    "dU10": ["U1o"],
-    "ffn11_1": ["U1o", "U0p"],
-    "ffn11_3": ["D0o"],
-    "dD11": ["D1p"],
-    "dU11": ["U1p"],
+    "dU10": ["U0o", "U1o"],
     "dO1": ["Op"],
-    "dO0": ["D1p", "U0o", "U1p", "Op", "Oo"],
-    "b1_0": ["D0o"],
-    "b1_1": ["U1p", "H0p", "U0o"],
-    "b1_2": ["H0p", "D1o", "D0o"],
-    "b1_3": ["H1p", "U0o", "Oo"],
-    "b0_0": ["H1p", "D1o", "D0o", "U1o"],
-    "b0_1": ["U0o", "H0o"],
-    "b0_2": ["U0o", "Oo", "H0o", "D1o"],
-    "b0_3": ["D0o", "H1o"],
-    "hb": ["U1o"],
-    "gin": ["D0o", "Oo", "H0o", "H1o", "So", "D1o"],
-    "tail": ["So", "U1o", "So", "H1o", "Oo", "H0o", "D1o", "D1o", "H1o", "U1o", "So", "U1o", "H0o", "Oo", "Oo", "H1o", "H0o", "So", "H0o", "H1o", "H1o"],
+    "gm": ["U1o", "D0o", "Op"],
+    "b1_0": ["H0p"],
+    "b1_1": ["U0o", "U1p", "H0p", "H1p", "D1o"],
+    "b1_2": ["D0o", "Oo", "H2p"],
+    "b1_3": ["H1p", "H3p", "H2p", "U1o", "Oo"],
+    "b0_0": ["D1o", "H0o", "H3p"],
+    "b0_1": ["U0o", "H2p", "H1o", "H0o", "D0o", "Oo"],
+    "b0_2": ["U1o", "H2o", "H1o"],
+    "b0_3": ["D1o", "U0o", "H2o", "H3o"],
+    "gin0": ["H0o", "Oo"],
+    "gin1": ["U0o", "H3o"],
+    "gin3": ["D0o", "So", "U1o"],
+    "fo1": ["H1o"],
+    "fo2": ["D0o"],
+    "fo3": ["H2o", "So"],
+    "tail": ["D1o", "H3o", "H0o", "So", "Oo", "U1o", "H1o", "H2o", "U1o", "H3o", "D1o", "H0o", "So", "H1o", "Oo", "H2o", "Oo", "H0o", "H3o", "D1o", "H1o", "H0o", "H2o", "H1o", "So", "H3o", "H2o", "H3o"],
 }
 BEFORE = {
+    "qkv1a": ["WhwA"],
 }
 
 
@@ -507,9 +533,9 @@
     for name, rows, cols, stages, pre in JOBS:
         for i, v in enumerate(job_scratch(rows, cols, stages, pre, lv - 4)):
             s[f"{name}_{i}"] = v
-    s["send"] = pltpu.SemaphoreType.DMA((160 + 16 * (lv - 4),))
-    s["recv"] = pltpu.SemaphoreType.DMA((160 + 16 * (lv - 4),))
-    s["local"] = pltpu.SemaphoreType.DMA((24,))
+    s["send"] = pltpu.SemaphoreType.DMA((224 + 24 * (lv - 4),))
+    s["recv"] = pltpu.SemaphoreType.DMA((224 + 24 * (lv - 4),))
+    s["local"] = pltpu.SemaphoreType.DMA((32,))
     return s
 
 
@@ -570,11 +596,12 @@
     z.GO, z.GH = (z.GOo, z.GOp), (z.GHo, z.GHp)
     z.dT, z.lo, z.ig = z.dpre, z.br, z.n2
     ends = dict(D0=lambda: z.FD_h.at[0 : FH // 2], D1=lambda: z.FD_h.at[FH // 2 : FH], U0=lambda: z.FU_h.at[:, 0 : FH // 2],
-                U1=lambda: z.FU_h.at[:, FH // 2 : FH], O=lambda: z.FO_h, H0=lambda: z.FH_h.at[0], H1=lambda: z.FH_h.at[1])
-    flat = lambda r, i: (lambda: r.at[2 * i : 2 * i + 2].reshape(1536, 128))
+                U1=lambda: z.FU_h.at[:, FH // 2 : FH], O=lambda: z.FO_h)
     srcs = dict(D0=(lambda: z.GD0o, lambda: z.GD0p), D1=(lambda: z.GD1o, lambda: z.GD1p), U0=(lambda: z.GU0o, lambda: z.GU0p),
-                U1=(lambda: z.GU1o, lambda: z.GU1p), O=(lambda: z.GOo, lambda: z.GOp),
-                H0=(flat(z.GHo, 0), flat(z.GHp, 0)), H1=(flat(z.GHo, 1), flat(z.GHp, 1)))
+                U1=(lambda: z.GU1o, lambda: z.GU1p), O=(lambda: z.GOo, lambda: z.GOp))
+    for i in range(NH):
+        ends[f"H{i}"] = lambda i=i: z.FH_h.at[i]
+        srcs[f"H{i}"] = (lambda i=i: z.GHo.at[i], lambda i=i: z.GHp.at[i])
     jobs = {}
     for name, rows, cols, stages, pre in JOBS:
         refs = [getattr(z, f"{name}_{i}") for i in range(len(job_scratch(rows, cols, stages, pre, len(lv) - 4)))]
@@ -614,19 +641,19 @@
     loads["hw"]().wait()
     qkv(z, 0, 0, NH)
     after("qkv0")
-    attn_fwd(z, 0, 0, NH, at("f0", 4))
+    attn_fwd(z, 0, 0, NH, at("f0", NH // 2))
     before("qkv1a")
     for b in wb:
         b().wait_recv()
     arrive("hwA")
     qkv(z, 1, 0, 2)
     after("qkv1a")
-    attn_fwd(z, 1, 0, 2, at("f1", range(0, 2)))
+    attn_fwd(z, 1, 0, 2, at("f1", range(0, 1)))
     before("qkv1b")
     arrive("hwB")
     qkv(z, 1, 2, 4)
     after("qkv1b")
-    attn_fwd(z, 1, 2, 4, at("f1", range(2, 4)))
+    attn_fwd(z, 1, 2, 4, at("f1", range(1, 2)))
     before("out")
     arrive("ow")
     loads["ow"]().wait()
@@ -635,13 +662,13 @@
         loads[n]().wait()
     after("out")
     for part in (0, 1):
-        for s in (0, 1):
+        for s in (1, 0):
             name = f"ffn{part}{s}"
             before(name + "_0")
             if s:
                 arrive(f"u{part}")
                 arrive(f"d{part}")
-            ffn(z, part, s, at(name, z.nb))
+            ffn(z, part, s, at(name, z.nb // 2))
             d_down(z, part, s)
             after(f"dD{part}{s}")
             d_up(z, part, s)
@@ -659,14 +686,12 @@
     d_headb(z, 0)
     d_headb(z, 1)
     after("hb")
-    grad_in(z)
+    grad_in(z, after)
     s_ig().start()
-    after("gin")
-    ffn_out(z, (0, 1))
-    after("fo0")
-    ffn_out(z, (2, 3))
+    for r in range(z.nb):
+        ffn_out(z, (r,))
+        after(f"fo{r}")
     s_lo().start()
-    after("fo1")
     after("tail")
     while small.steps:
         small.own()
@@ -692,7 +717,7 @@
         run(z, ndp)
 
     S = jax.ShapeDtypeStruct
-    outs = [S((T, D), BF16), S((T, D), BF16), S((2, 1536, 128), BF16), S((HALF, D), BF16), S((D, FH), BF16), S((FH, D), BF16),
+    outs = [S((T, D), BF16), S((T, D), BF16), S((NH, 768, 128), BF16), S((HALF, D), BF16), S((D, FH), BF16), S((FH, D), BF16),
             S((16, D), F32)]
     vm, hbm = pl.BlockSpec(memory_space=pltpu.VMEM), pl.BlockSpec(memory_space=pl.ANY)
     return pl.pallas_call(
@@ -701,17 +726,28 @@
         name="layer")(*args)
 
 
-def widen(FH_, FO_, FU_, FD_, sm):
-    def kernel(h, o, u, d, m, ho, oo, uo, do, sc, sh, qb, vb, ob, ub, db):
-        oo[...] = o[...].astype(F32)
-        uo[...] = u[...].astype(F32)
-        do[...] = d[...].astype(F32)
-        for q in range(4):
-            for j in range(3):
-                for p in range(2):
-                    rows = [h[p, i * 768 + q * 192 + j * HD : i * 768 + q * 192 + (j + 1) * HD, :] for i in range(2)]
-                    t = jnp.concatenate(rows, 0).astype(F32).T
-                    ho[j, q * 128 : (q + 1) * 128, p * 128 : (p + 1) * 128] = t
+def widen(FH_, FO_, FU_, FD_, sm, lo, ig):
+    def kernel(h, o, u, d, m, l, g, ho, oo, uo, do, lo_, go, sc, sh, qb, vb, ob, ub, db, hv, ov, uv, dv, lv, gv, hf, of, uf, df, si, so):
+        ins, outs = [], []
+
+        def load(src, dst):
+            c = pltpu.make_async_copy(src, dst, si.at[len(ins)])
+            ins.append(c)
+            c.start()
+            return c
+
+        def store(src, dst):
+            c = pltpu.make_async_copy(src, dst, so.at[len(outs)])
+            outs.append(c)
+            c.start()
+
+        top, bottom = slice(0, 512), slice(512, 1024)
+        left, right = slice(0, 256), slice(256, 512)
+        i_g, i_l = load(g, gv), load(l, lv)
+        i_d0, i_h = load(d.at[top], dv.at[top]), load(h, hv)
+        i_d1 = load(d.at[bottom], dv.at[bottom])
+        i_u0, i_u1 = load(u.at[left], uv.at[left]), load(u.at[right], uv.at[right])
+        i_o = load(o, ov)
         sc[...] = m[0:2, :]
         sh[...] = m[2:4, :]
         qb[...] = m[8:9, 0:HALF]
@@ -720,12 +756,42 @@
         ub[:, 0:D] = m[9:10, :]
         ub[:, D:FH] = m[10:11, :]
         db[...] = m[5:6, :]
-
-    S = jax.ShapeDtypeStruct
-    vm = pl.BlockSpec(memory_space=pltpu.VMEM)
-    shapes = [(3, D, HALF), (HALF, D), (D, FH), (FH, D), (2, D), (2, D), (1, HALF), (1, HALF), (1, D), (1, FH), (1, D)]
-    return pl.pallas_call(kernel, out_shape=[S(t, F32) for t in shapes], in_specs=[vm] * 5, out_specs=[vm] * 11, name="widen")(
-        FH_, FO_, FU_, FD_, sm)
+        i_g.wait()
+        store(gv, go)
+        i_l.wait()
+        store(lv, lo_)
+
+        def piece(c, v, f, out, rows):
+            c.wait()
+            f[rows, :] = v[rows, :].astype(F32)
+            store(f.at[rows], out.at[rows])
+
+        piece(i_d0, dv, df, do, top)
+        i_h.wait()
+        for j in range(3):
+            for q in range(4):
+                for p in range(2):
+                    rows = [hv[2 * p + i, q * 192 + j * HD : q * 192 + (j + 1) * HD, :] for i in range(2)]
+                    hf[j, q * 128 : (q + 1) * 128, p * 128 : (p + 1) * 128] = jnp.concatenate(rows, 0).astype(F32).T
+            store(hf.at[j], ho.at[j])
+        piece(i_d1, dv, df, do, bottom)
+        piece(i_u0, uv, uf, uo, left)
+        piece(i_u1, uv, uf, uo, right)
+        piece(i_o, ov, of, oo, left)
+        for c in outs:
+            c.wait()
+
+    S, V = jax.ShapeDtypeStruct, pltpu.VMEM
+    vm, hbm = pl.BlockSpec(memory_space=pltpu.VMEM), pl.BlockSpec(memory_space=pl.ANY)
+    big = [(3, D, HALF), (HALF, D), (D, FH), (FH, D)]
+    small = [(2, D), (2, D), (1, HALF), (1, HALF), (1, D), (1, FH), (1, D)]
+    rows = S(lo.shape, BF16)
+    out_shape = [S(t, F32) for t in big] + [rows, rows] + [S(t, F32) for t in small]
+    bufs = [V((NH, 768, 128), BF16)] + [V(t, BF16) for t in big[1:]] + [V(lo.shape, BF16)] * 2 + [V(t, F32) for t in big]
+    return pl.pallas_call(
+        kernel, out_shape=out_shape, in_specs=[hbm] * 4 + [vm] + [hbm] * 2, out_specs=[hbm] * 6 + [vm] * 7,
+        scratch_shapes=bufs + [pltpu.SemaphoreType.DMA((8,)), pltpu.SemaphoreType.DMA((10,))],
+        compiler_params=pltpu.CompilerParams(vmem_limit_bytes=VMEM_BYTES), name="widen")(FH_, FO_, FU_, FD_, sm, lo, ig)
 
 
 def solution(mesh):
@@ -737,7 +803,7 @@
         args = (inputs, cotangent, head_weight, out_weight, up_weight, down_weight, norm_scale, norm_shift, row(query_bias),
                 row(value_bias), row(out_bias), row(up_bias), row(down_bias))
         lo, ig, gh, go, gu, gd, sm = main_call(args, inputs.shape[0], ndp)
-        gh, go, gu, gd, sc, sh, qb, vb, ob, ub, db = widen(gh, go, gu, gd, sm)
+        gh, go, gu, gd, lo, ig, sc, sh, qb, vb, ob, ub, db = widen(gh, go, gu, gd, sm, lo, ig)
         flat = lambda v: v.reshape(v.shape[1])
         return (lo, ig, sc, sh, gh, flat(qb), flat(vb), go, flat(ob), gu, flat(ub), gd, flat(db))
 

time: 110 us -> 103 us (0.936)
  Pallas kernels: 106 us -> 101 us
  local copies, waits for them, and re-layouts: 1.95 us -> 0 us
    pallas_call x1, Pallas kernels: 101 us -> 94.8 us  [main_call(): pl.pallas_call(kernel, out_shape=outs, in_specs=[hbm] * 6 + [vm] * 7, out...]
    unnamed x6 -> x0, local copies, waits for them, and re-layouts: 1.95 us -> none
where the time goes in v5:
time: 103 us; the launch traced here: 102 us
  Pallas kernels  101 us (98%)
    pallas_call x1, Pallas kernels, main_call(): pl.pallas_call(kernel, out_shape=outs, in_specs=[hbm] * 6 + [vm] * 7, out...  94.8 us
    pallas_call x1, Pallas kernels, widen(): pl.pallas_call(kernel, out_shape=out_shape, in_specs=[hbm] * 4 + [vm] + [...  6.03 us

profile of v5, /device:TPU:0, one launch (start us, length us, event | category | flops | bytes accessed | tf_op | source)
XLA Modules:
  0.0 101.6 jit_solution(205631030158491982)
XLA Ops:
  0.6 94.8 %layer.1 = (bf16[1024,512]{1,0:T(8,128)(2,1)}, bf16[1024,512]{1,0:T(8,128)(2,1)}, bf16[4,768,128]{2,1,0:T(8,128)(2,1)}, bf16[256,512]{1,0:T(8,128)(2,1)}, bf16[5...) custom-call(bf16[1024,512]{1,0:T(8,128)(2,1)} %refs_0_.1, bf16[1024,512]{1,0:T(8,128)(2,1)} %refs_1_.1, ...), custom_call_target="tpu_custom_call" | custom-call | tf_op jit(solution)/shard_map/layer/pallas_call | solution.py:723
  95.4 6.0 %widen.1 = (f32[3,512,256]{2,1,0:T(8,128)}, f32[256,512]{1,0:T(8,128)}, f32[512,1024]{1,0:T(8,128)}, f32[1024,512]{1,0:T(8,128)}, bf16[1024,512]{1,0:T(8,128)(2,...) custom-call(bf16[4,768,128]{2,1,0:T(8,128)(2,1)} %get-tuple-element., ...), custom_call_target="tpu_custom_call" | custom-call | tf_op jit(solution)/shard_map/widen/pallas_call | solution.py:791

commit v6 on v5

--- a/solution.py
+++ b/solution.py
@@ -203,30 +203,35 @@
         gs = (z.gmT[s, hr, :].astype(F32) * z.rl[hi]).astype(BF16)
         delta = jnp.sum(gs.astype(F32) * z.mixT[s, hr, :].astype(F32), 0, keepdims=True)
         dprob = lambda b: dot(vh[: BLK * (b + 1)], gs[:, b * BLK : (b + 1) * BLK])
-        ahead = dprob(0)
-        for b in range(z.nb):
+        head_grad = lambda b: dot(z.dh[:, b * BLK : (b + 1) * BLK], z.n1T[:, b * BLK : (b + 1) * BLK], NT)
+        last = z.nb - 1
+        ahead, g = dprob(last), None
+        for b in range(last, -1, -1):
             dp = ahead
-            if b + 1 < z.nb:
-                ahead = dprob(b + 1)
+            if b:
+                ahead = dprob(b - 1)
             nk = BLK * (b + 1)
             off = BLK * (b * (b + 1) // 2)
             sl = slice(b * BLK, nk)
             gq = gs[:, sl]
             e = z.E[hi, off : off + nk, :]
             dv = dot(gq, e, NT)
+            if b < last:
+                g = head_grad(b + 1) if g is None else g + head_grad(b + 1)
             ds = (e.astype(F32) * (dp - delta[:, sl])).astype(BF16)
             z.dh[0:HD, sl] = (dot(z.kT[s, hr, 0:nk], ds) * 0.125).astype(BF16)
             dk = dot(z.qT[s, hr, sl], ds, NT)
+            if b < last:
+                dv = dv + z.dva[:, 0:nk]
+                dk = dk + z.dka[:, 0:nk]
             if b:
-                z.dva[:, 0 : nk - BLK] = z.dva[:, 0 : nk - BLK] + dv[:, 0 : nk - BLK]
-                z.dka[:, 0 : nk - BLK] = z.dka[:, 0 : nk - BLK] + dk[:, 0 : nk - BLK]
-            z.dva[:, sl] = dv[:, nk - BLK : nk]
-            z.dka[:, sl] = dk[:, nk - BLK : nk]
-        z.dh[HD : 2 * HD, :] = (z.dka[...] * LN2).astype(BF16)
-        z.dh[2 * HD : 3 * HD, :] = z.dva[...].astype(BF16)
+                z.dva[:, 0 : nk - BLK] = dv[:, 0 : nk - BLK]
+                z.dka[:, 0 : nk - BLK] = dk[:, 0 : nk - BLK]
+            z.dh[HD : 2 * HD, sl] = (dk[:, nk - BLK : nk] * LN2).astype(BF16)
+            z.dh[2 * HD : 3 * HD, sl] = dv[:, nk - BLK : nk].astype(BF16)
         for j in range(3):
             z.dT[s, pl.ds(pl.multiple_of(j * HALF + h * HD, HD), HD), :] = z.dh[j * HD : (j + 1) * HD, :]
-        g = dot(z.dh[...], z.n1T[...], NT).astype(BF16)
+        g = ((g + head_grad(0)) if g is not None else head_grad(0)).astype(BF16)
         for q in range(4):
             z.GH[s][h, q * 192 : (q + 1) * 192, :] = g[:, q * 128 : (q + 1) * 128]
         hook(h)
@@ -305,9 +310,10 @@
         self.local_count += 1
         return lambda: pltpu.make_async_copy(src(), dst(), self.local.at[i])
 
-    def drain(self):
-        for make in self.pending:
+    def drain(self, n=None):
+        for make in self.pending[:n]:
             make().wait_send()
+        self.pending = self.pending[n:] if n else []
 
 
 def add_rows(dst, srcs, at, n, cols):
@@ -462,11 +468,11 @@
         ("U0", 512, 512, [[1], [2], [4, 8]], 2),
         ("D1", 512, 512, [[1], [2], [4, 8]], 1),
         ("U1", 512, 512, [[1], [2], [4, 8]], 2),
-        ("O", 256, 512, [[1], [2], [4, 8]], 1),
-        ("H0", 768, 128, [[1], [2], [4, 8]], 1),
+        ("O", 256, 512, [[1], [2], [4, 8]], 2),
+        ("H0", 768, 128, [[1], [2], [4, 8]], 2),
         ("H1", 768, 128, [[1], [2], [4, 8]], 1),
         ("H2", 768, 128, [[1], [2], [4, 8]], 2),
-        ("H3", 768, 128, [[1], [2], [4, 8]], 1)]
+        ("H3", 768, 128, [[1], [2], [4, 8]], 2)]
 
 HOOKS = {
     "f0_0": ["WhwA"],
@@ -483,32 +489,35 @@
     "dD00": ["D0o"],
     "dU00": ["U0o"],
     "ffn11_1": ["U0o"],
-    "dD11": ["U0p", "D1p"],
+    "dD11": ["D1p", "U0p"],
     "dU11": ["U1p"],
     "ffn10_0": ["D0o", "D1p", "U1p"],
     "dD10": ["D1o"],
     "dU10": ["U0o", "U1o"],
-    "dO1": ["Op"],
-    "gm": ["U1o", "D0o", "Op"],
-    "b1_0": ["H0p"],
-    "b1_1": ["U0o", "U1p", "H0p", "H1p", "D1o"],
-    "b1_2": ["D0o", "Oo", "H2p"],
-    "b1_3": ["H1p", "H3p", "H2p", "U1o", "Oo"],
-    "b0_0": ["D1o", "H0o", "H3p"],
-    "b0_1": ["U0o", "H2p", "H1o", "H0o", "D0o", "Oo"],
-    "b0_2": ["U1o", "H2o", "H1o"],
-    "b0_3": ["D1o", "U0o", "H2o", "H3o"],
-    "gin0": ["H0o", "Oo"],
-    "gin1": ["U0o", "H3o"],
-    "gin3": ["D0o", "So", "U1o"],
-    "fo1": ["H1o"],
-    "fo2": ["D0o"],
-    "fo3": ["H2o", "So"],
-    "tail": ["D1o", "H3o", "H0o", "So", "Oo", "U1o", "H1o", "H2o", "U1o", "H3o", "D1o", "H0o", "So", "H1o", "Oo", "H2o", "Oo", "H0o", "H3o", "D1o", "H1o", "H0o", "H2o", "H1o", "So", "H3o", "H2o", "H3o"],
+    "dO0": ["Op", "Oo"],
+    "gm": ["U1o", "D0o"],
+    "b1_0": ["Op", "Oo"],
+    "b1_1": ["U0o", "U1p", "D1o", "H1p"],
+    "b1_2": ["H2p", "D0o", "H1p", "H0p", "Op"],
+    "b1_3": ["H2p", "H3p", "U1o"],
+    "b0_0": ["U0o", "H3p", "D1o", "H0p", "H0o"],
+    "b0_1": ["H2p", "D0o", "H1o", "Oo", "H0o"],
+    "b0_2": ["U0o", "H1o", "U1o", "H2o"],
+    "b0_3": ["U0o", "H3p", "D1o", "H0p", "H2o", "H3o"],
+    "gin0": ["Oo"],
+    "gin1": ["H3o"],
+    "gin2": ["D0o"],
+    "gin3": ["So", "U1o", "H0o"],
+    "fo0": ["D0o", "H1o"],
+    "fo2": ["H2o"],
+    "fo3": ["So", "H3o", "D1o"],
+    "tail": ["So", "Oo", "H0o", "U1o", "H1o", "U1o", "H2o", "H3o", "D1o", "H0o", "D1o", "H1o", "Oo", "So", "H2o", "Oo", "H0o", "H3o", "H1o", "H0o", "H2o", "H1o", "H3o", "H2o", "So", "H3o"],
 }
 BEFORE = {
     "qkv1a": ["WhwA"],
 }
+
+GROUPS = [g for g in ([4, 8], [2, 4, 8]) if any(g in st for _, _, _, st, _ in JOBS) or g in SMALL_STAGES]
 
 
 def scratch(T, ndp):
@@ -540,7 +549,7 @@
 
 
 def run(z, ndp):
-    c = Comm(ndp, [[4, 8], [2, 4, 8]], z.send, z.recv, z.local)
+    c = Comm(ndp, GROUPS, z.send, z.recv, z.local)
     lv = c.levels
     c.barrier_signal()
     slot0 = lambda r: r.at[0]
@@ -686,6 +695,7 @@
     d_headb(z, 0)
     d_headb(z, 1)
     after("hb")
+    c.drain(31)
     grad_in(z, after)
     s_ig().start()
     for r in range(z.nb):

time: 103 us -> 101 us (0.981)
  Pallas kernels: 101 us -> 99.6 us
    pallas_call x1, Pallas kernels: 94.8 us -> 93.6 us  [main_call(): pl.pallas_call(kernel, out_shape=outs, in_specs=[hbm] * 6 + [vm] * 7, out...]
where the time goes in v6:
time: 101 us; the launch traced here: 100 us
  Pallas kernels  99.6 us (99%)
    pallas_call x1, Pallas kernels, main_call(): pl.pallas_call(kernel, out_shape=outs, in_specs=[hbm] * 6 + [vm] * 7, out...  93.6 us
    pallas_call x1, Pallas kernels, widen(): pl.pallas_call(kernel, out_shape=out_shape, in_specs=[hbm] * 4 + [vm] + [...  6.03 us

profile of v6, /device:TPU:0, one launch (start us, length us, event | category | flops | bytes accessed | tf_op | source)
XLA Modules:
  0.0 100.5 jit_solution(5893857502221126560)
XLA Ops:
  0.6 93.6 %layer.1 = (bf16[1024,512]{1,0:T(8,128)(2,1)}, bf16[1024,512]{1,0:T(8,128)(2,1)}, bf16[4,768,128]{2,1,0:T(8,128)(2,1)}, bf16[256,512]{1,0:T(8,128)(2,1)}, bf16[5...) custom-call(bf16[1024,512]{1,0:T(8,128)(2,1)} %refs_0_.1, bf16[1024,512]{1,0:T(8,128)(2,1)} %refs_1_.1, ...), custom_call_target="tpu_custom_call" | custom-call | tf_op jit(solution)/shard_map/layer/pallas_call | solution.py:733
  94.3 6.0 %widen.1 = (f32[3,512,256]{2,1,0:T(8,128)}, f32[256,512]{1,0:T(8,128)}, f32[512,1024]{1,0:T(8,128)}, f32[1024,512]{1,0:T(8,128)}, bf16[1024,512]{1,0:T(8,128)(2,...) custom-call(bf16[4,768,128]{2,1,0:T(8,128)(2,1)} %get-tuple-element., ...), custom_call_target="tpu_custom_call" | custom-call | tf_op jit(solution)/shard_map/widen/pallas_call | solution.py:801

commit v7 on v6

--- a/solution.py
+++ b/solution.py
@@ -468,10 +468,10 @@
         ("U0", 512, 512, [[1], [2], [4, 8]], 2),
         ("D1", 512, 512, [[1], [2], [4, 8]], 1),
         ("U1", 512, 512, [[1], [2], [4, 8]], 2),
-        ("O", 256, 512, [[1], [2], [4, 8]], 2),
-        ("H0", 768, 128, [[1], [2], [4, 8]], 2),
-        ("H1", 768, 128, [[1], [2], [4, 8]], 1),
-        ("H2", 768, 128, [[1], [2], [4, 8]], 2),
+        ("O", 256, 512, [[1], [2], [4, 8]], 1),
+        ("H0", 768, 128, [[1], [2], [4, 8]], 1),
+        ("H1", 768, 128, [[1], [2], [4, 8]], 2),
+        ("H2", 768, 128, [[1], [2], [4, 8]], 1),
         ("H3", 768, 128, [[1], [2], [4, 8]], 2)]
 
 HOOKS = {
@@ -489,29 +489,28 @@
     "dD00": ["D0o"],
     "dU00": ["U0o"],
     "ffn11_1": ["U0o"],
-    "dD11": ["D1p", "U0p"],
+    "dD11": ["U0p", "D1p"],
     "dU11": ["U1p"],
     "ffn10_0": ["D0o", "D1p", "U1p"],
     "dD10": ["D1o"],
     "dU10": ["U0o", "U1o"],
-    "dO0": ["Op", "Oo"],
-    "gm": ["U1o", "D0o"],
-    "b1_0": ["Op", "Oo"],
-    "b1_1": ["U0o", "U1p", "D1o", "H1p"],
-    "b1_2": ["H2p", "D0o", "H1p", "H0p", "Op"],
-    "b1_3": ["H2p", "H3p", "U1o"],
-    "b0_0": ["U0o", "H3p", "D1o", "H0p", "H0o"],
-    "b0_1": ["H2p", "D0o", "H1o", "Oo", "H0o"],
-    "b0_2": ["U0o", "H1o", "U1o", "H2o"],
-    "b0_3": ["U0o", "H3p", "D1o", "H0p", "H2o", "H3o"],
-    "gin0": ["Oo"],
-    "gin1": ["H3o"],
+    "dO1": ["Op"],
+    "gm": ["D0o", "U1o", "Op"],
+    "b1_0": ["H0p"],
+    "b1_1": ["U0o", "U1p", "D1o", "H1p", "H0p"],
+    "b1_2": ["Oo", "D0o", "H1p"],
+    "b1_3": ["Oo", "H2p", "U1o", "H3p", "D1o"],
+    "b0_0": ["H2p", "H1p", "H3p", "H0o"],
+    "b0_1": ["H0o", "Oo", "H1o", "D0o"],
+    "b0_2": ["H1o", "H2o", "U0o", "H3p", "U1o"],
+    "b0_3": ["H3o", "H2o", "D1o"],
+    "gin0": ["Oo", "D0o", "H3o"],
+    "gin1": ["H1o", "H0o"],
     "gin2": ["D0o"],
-    "gin3": ["So", "U1o", "H0o"],
-    "fo0": ["D0o", "H1o"],
-    "fo2": ["H2o"],
-    "fo3": ["So", "H3o", "D1o"],
-    "tail": ["So", "Oo", "H0o", "U1o", "H1o", "U1o", "H2o", "H3o", "D1o", "H0o", "D1o", "H1o", "Oo", "So", "H2o", "Oo", "H0o", "H3o", "H1o", "H0o", "H2o", "H1o", "H3o", "H2o", "So", "H3o"],
+    "gin3": ["U1o", "So"],
+    "fo1": ["U0o"],
+    "fo3": ["H2o"],
+    "tail": ["So", "D1o", "U0o", "H3o", "So", "Oo", "H1o", "U1o", "H0o", "H2o", "U1o", "H3o", "H1o", "So", "D1o", "H0o", "Oo", "D1o", "H2o", "Oo", "H1o", "H3o", "H0o", "H1o", "H2o", "H0o", "So", "H3o", "H2o", "H3o"],
 }
 BEFORE = {
     "qkv1a": ["WhwA"],

time: 101 us -> 103 us (1.020)
  Pallas kernels: 99.6 us -> 101 us
    pallas_call x1, Pallas kernels: 93.6 us -> 94.8 us  [main_call(): pl.pallas_call(kernel, out_shape=outs, in_specs=[hbm] * 6 + [vm] * 7, out...]
where the time goes in v7:
time: 103 us; the launch traced here: 102 us
  Pallas kernels  101 us (98%)
    pallas_call x1, Pallas kernels, main_call(): pl.pallas_call(kernel, out_shape=outs, in_specs=[hbm] * 6 + [vm] * 7, out...  94.8 us
    pallas_call x1, Pallas kernels, widen(): pl.pallas_call(kernel, out_shape=out_shape, in_specs=[hbm] * 4 + [vm] + [...  6.03 us

profile of v7, /device:TPU:0, one launch (start us, length us, event | category | flops | bytes accessed | tf_op | source)
XLA Modules:
  0.0 101.7 jit_solution(10757496235548210730)
XLA Ops:
  0.6 94.8 %layer.1 = (bf16[1024,512]{1,0:T(8,128)(2,1)}, bf16[1024,512]{1,0:T(8,128)(2,1)}, bf16[4,768,128]{2,1,0:T(8,128)(2,1)}, bf16[256,512]{1,0:T(8,128)(2,1)}, bf16[5...) custom-call(bf16[1024,512]{1,0:T(8,128)(2,1)} %refs_0_.1, bf16[1024,512]{1,0:T(8,128)(2,1)} %refs_1_.1, ...), custom_call_target="tpu_custom_call" | custom-call | tf_op jit(solution)/shard_map/layer/pallas_call | solution.py:732
  95.5 6.0 %widen.1 = (f32[3,512,256]{2,1,0:T(8,128)}, f32[256,512]{1,0:T(8,128)}, f32[512,1024]{1,0:T(8,128)}, f32[1024,512]{1,0:T(8,128)}, bf16[1024,512]{1,0:T(8,128)(2,...) custom-call(bf16[4,768,128]{2,1,0:T(8,128)(2,1)} %get-tuple-element., ...), custom_call_target="tpu_custom_call" | custom-call | tf_op jit(solution)/shard_map/widen/pallas_call | solution.py:800
